TPU v7x, 32 devices: a whole 2x2x4 slice. The times are simulated.
32 devices in a mesh: grp: 4 (over y, core), seq: 8 (over z, x).
Axes of the slice: x: 2, y: 2, z: 4, core: 2. Of those that a mesh axis runs over, the one named last changes fastest.
Arguments:
- layer_input: bfloat16 [8192, 2048], P(('grp', 'seq')), may hold values from -6 to 6
- entry_gain: float32 [2048], replicated, may hold values from 0.1 to 1.9
- entry_shift: float32 [2048], replicated, may hold values from -1.75 to 1.75
- joint_weight: bfloat16 [2048, 6144], P(('grp', 'seq')), may hold values from -0.125 to 0.125
- query_offset: float32 [2048], replicated, may hold values from -3 to 3
- value_offset: float32 [2048], replicated, may hold values from -0.3125 to 0.3125
- mixing_weight: bfloat16 [2048, 2048], P(('grp', 'seq')), may hold values from -1 to 1
- attention_offset: float32 [2048], replicated, may hold values from -3 to 3
- middle_gain: float32 [2048], replicated, may hold values from 0.1 to 1.9
- middle_shift: float32 [2048], replicated, may hold values from -1.75 to 1.75
- expand_weight: bfloat16 [2048, 8192], P(('grp', 'seq')), may hold values from -0.125 to 0.125
- expand_offset: float32 [8192], replicated, may hold values from -3 to 3
- shrink_weight: bfloat16 [2048, 8192], P(('grp', 'seq')), may hold values from -0.0625 to 0.0625
- shrink_offset: float32 [2048], replicated, may hold values from -3 to 3
- placement: int32 [4, 2048], P('grp'), may hold values from 0 to 2047, each once within a row
- slot_lengths: int32 [4, 4], P('grp'), may hold values from 1 to 256, 832 in all within a row
- cotangent: bfloat16 [8192, 2048], P(('grp', 'seq')), may hold values from -6 to 6
Outputs:
- layer_output: bfloat16 [8192, 2048], P(('grp', 'seq'))
- input_gradient: bfloat16 [8192, 2048], P(('grp', 'seq'))
- entry_gain_gradient: float32 [2048], replicated
- entry_shift_gradient: float32 [2048], replicated
- joint_gradient: float32 [2048, 6144], P(('grp', 'seq'))
- query_gradient: float32 [2048], replicated
- value_gradient: float32 [2048], replicated
- mixing_gradient: float32 [2048, 2048], P(('grp', 'seq'))
- attention_offset_gradient: float32 [2048], replicated
- middle_gain_gradient: float32 [2048], replicated
- middle_shift_gradient: float32 [2048], replicated
- expand_gradient: float32 [2048, 8192], P(('grp', 'seq'))
- expand_offset_gradient: float32 [8192], replicated
- shrink_gradient: float32 [2048, 8192], P(('grp', 'seq'))
- shrink_offset_gradient: float32 [2048], replicated
Inputs may be any that keep to these rules, and one draw needn't show every extreme that they name: `placement`: each row holds every position of its group once. `slot_lengths`: the real tokens of each slot of 256 positions; the rest of a slot is padding; some slot of every group is full.
All inputs are finite; a program needn't handle non-finite values.
Results may differ from a plain program's by a relative error of at most 0.013.
Values may be sent and summed in bfloat16 or wider, within the bound.
A program may use at most 704 MiB of HBM per device.

v0:
```python
import jax
import jax.numpy as jnp
from jax import lax
from jax.sharding import PartitionSpec as P

HEADS = 16
CONT = 256
QBLOCK = 512


norm_epsilon = 1e-05
masked_score = -1e30


def layer_norm(values, scale_vector, shift_vector):
    average = jnp.mean(values, axis=-1, keepdims=True)
    centered = values - average
    variance = jnp.mean(centered * centered, axis=-1, keepdims=True)
    return centered * lax.rsqrt(variance + norm_epsilon) * scale_vector + shift_vector


def exact_gelu(values):
    return jax.nn.gelu(values, approximate=False)


def key_facts(positions, lengths, prompt):
    segment = (positions - prompt) // CONT
    within = positions - prompt - segment * CONT
    slot_ids = jnp.arange(lengths.shape[0], dtype=jnp.int32)
    slot_limit = jnp.sum(
        jnp.where(segment[:, None] == slot_ids[None, :], lengths[None, :], 0), axis=1
    )
    return (segment, (positions < prompt) | (within < slot_limit))


def block_mask(query_place, key_place, key_segment, key_live, prompt):
    query_col = query_place[:, None]
    key_row = key_place[None, :]
    query_segment = (query_col - prompt) // CONT
    prompt_keys = (key_row < prompt) & ((query_col >= prompt) | (key_row <= query_col))
    same_slot = (
        (query_col >= prompt)
        & (key_row >= prompt)
        & (query_segment == key_segment[None, :])
        & (key_row <= query_col)
        & key_live[None, :]
    )
    return prompt_keys | same_slot


def rows_product(left_matrix, weight):
    return jnp.dot(
        left_matrix,
        lax.all_gather(weight, ("grp", "seq"), axis=0, tiled=True),
        preferred_element_type=jnp.float32,
    )


def rows_transposed(left_matrix, weight):
    return lax.dot_general(
        left_matrix,
        lax.all_gather(weight, ("grp", "seq"), axis=0, tiled=True),
        (((1,), (1,)), ((), ())),
        preferred_element_type=jnp.float32,
    )


def row_outer(left_matrix, right_matrix):
    return lax.dot_general(
        left_matrix, right_matrix, (((0,), (0,)), ((), ())), preferred_element_type=jnp.float32
    )


def attention_forward(packed, places, key_segment, key_live, prompt, score_scale):
    grouped = packed[:, 0]
    queries = grouped[:, :, 0]
    key_vectors = grouped[:, :, 1]
    values = grouped[:, :, 2]
    rows_total = grouped.shape[0]
    head_count = grouped.shape[1]

    def one_block(block_index):
        first_row = block_index * QBLOCK
        block_queries = lax.dynamic_slice_in_dim(queries, first_row, QBLOCK, 0)
        block_places = lax.dynamic_slice_in_dim(places, first_row, QBLOCK, 0)
        allowed = block_mask(block_places, places, key_segment, key_live, prompt)
        scores = (
            jnp.einsum(
                "qhe,khe->hqk", block_queries, key_vectors, preferred_element_type=jnp.float32
            )
            * score_scale
        )
        scores = jnp.where(allowed[None], scores, masked_score)
        row_top = jnp.max(scores, axis=2, keepdims=True)
        row_total = jnp.sum(jnp.exp(scores - row_top), axis=2, keepdims=True)
        log_total = row_top + jnp.log(row_total)
        soft_weights = jnp.exp(scores - log_total).astype(jnp.bfloat16)
        mixture = jnp.einsum(
            "hqk,khe->qhe", soft_weights, values, preferred_element_type=jnp.float32
        )
        return (mixture.astype(jnp.bfloat16), jnp.transpose(log_total[:, :, 0]))

    mixture, log_totals = lax.map(one_block, jnp.arange(rows_total // QBLOCK, dtype=jnp.int32))
    return (
        mixture.reshape(rows_total, 1, head_count, -1),
        log_totals.reshape(rows_total, 1, head_count),
        packed,
    )


def attention_backward(
    kept_heads, log_totals, head_slopes, places, key_segment, key_live, prompt, score_scale
):
    grouped = kept_heads[:, 0]
    queries = grouped[:, :, 0]
    key_vectors = grouped[:, :, 1]
    values = grouped[:, :, 2]
    slopes = head_slopes[:, 0]
    totals = log_totals[:, 0]
    rows_total = grouped.shape[0]

    def one_block(running, block_index):
        key_sum, value_sum = running
        first_row = block_index * QBLOCK
        block_queries = lax.dynamic_slice_in_dim(queries, first_row, QBLOCK, 0)
        block_slopes = lax.dynamic_slice_in_dim(slopes, first_row, QBLOCK, 0)
        block_totals = lax.dynamic_slice_in_dim(totals, first_row, QBLOCK, 0)
        block_places = lax.dynamic_slice_in_dim(places, first_row, QBLOCK, 0)
        allowed = block_mask(block_places, places, key_segment, key_live, prompt)
        scores = (
            jnp.einsum(
                "qhe,khe->hqk", block_queries, key_vectors, preferred_element_type=jnp.float32
            )
            * score_scale
        )
        scores = jnp.where(allowed[None], scores, masked_score)
        probable = jnp.exp(scores - jnp.transpose(block_totals)[:, :, None])
        weight_slope = jnp.einsum(
            "qhe,khe->hqk", block_slopes, values, preferred_element_type=jnp.float32
        )
        centre = jnp.sum(probable * weight_slope, axis=2, keepdims=True)
        score_slope = (probable * (weight_slope - centre)).astype(jnp.bfloat16)
        query_slope = (
            jnp.einsum("hqk,khe->qhe", score_slope, key_vectors, preferred_element_type=jnp.float32)
            * score_scale
        )
        key_sum = (
            key_sum
            + jnp.einsum(
                "hqk,qhe->khe", score_slope, block_queries, preferred_element_type=jnp.float32
            )
            * score_scale
        )
        value_sum = value_sum + jnp.einsum(
            "hqk,qhe->khe",
            probable.astype(jnp.bfloat16),
            block_slopes,
            preferred_element_type=jnp.float32,
        )
        return ((key_sum, value_sum), query_slope)

    empty_sums = jnp.zeros(values.shape, jnp.float32)
    (key_sum, value_sum), query_slopes = lax.scan(
        one_block, (empty_sums, empty_sums), jnp.arange(rows_total // QBLOCK, dtype=jnp.int32)
    )
    query_slopes = query_slopes.reshape(values.shape)
    return jnp.stack([query_slopes, key_sum, value_sum], axis=2).astype(jnp.bfloat16)[:, None]


def shards(
    layer_input,
    entry_gain,
    entry_shift,
    joint_weight,
    query_offset,
    value_offset,
    mixing_weight,
    attention_offset,
    middle_gain,
    middle_shift,
    expand_weight,
    expand_offset,
    shrink_weight,
    shrink_offset,
    placement,
    slot_lengths,
    cotangent,
):
    token_rows = layer_input.shape[0]
    width = layer_input.shape[1]
    hidden_width = expand_weight.shape[1]
    seq_count = lax.axis_size("seq")
    head_size = width // HEADS
    local_heads = HEADS // seq_count
    score_scale = head_size ** (-0.5)
    places = placement[0]
    prompt = places.shape[0] // 2
    key_segment, key_live = key_facts(places, slot_lengths[0], prompt)
    input_float = layer_input.astype(jnp.float32)
    entry_float, entry_back = jax.vjp(layer_norm, input_float, entry_gain, entry_shift)
    entry_normed = entry_float.astype(jnp.bfloat16)
    joint_float = rows_product(entry_normed, joint_weight).reshape(token_rows, HEADS, 3, head_size)
    offsets = jnp.stack(
        [
            query_offset.reshape(HEADS, head_size),
            jnp.zeros((HEADS, head_size), jnp.float32),
            value_offset.reshape(HEADS, head_size),
        ],
        axis=1,
    )
    joint_values = (
        (joint_float + offsets)
        .astype(jnp.bfloat16)
        .reshape(token_rows, seq_count, local_heads, 3, head_size)
    )
    head_mixture, log_totals, kept_heads = attention_forward(
        lax.all_to_all(joint_values, "seq", split_axis=1, concat_axis=0, tiled=True),
        places,
        key_segment,
        key_live,
        prompt,
        score_scale,
    )
    attended = lax.all_to_all(head_mixture, "seq", split_axis=0, concat_axis=1, tiled=True).reshape(
        token_rows, width
    )
    branch = rows_product(attended, mixing_weight) + attention_offset
    residual = input_float + branch
    middle_float, middle_back = jax.vjp(layer_norm, residual, middle_gain, middle_shift)
    middle_normed = middle_float.astype(jnp.bfloat16)
    expanded = rows_product(middle_normed, expand_weight) + expand_offset
    activated_float, gelu_back = jax.vjp(exact_gelu, expanded)
    activated = activated_float.astype(jnp.bfloat16)
    output_float = residual + rows_transposed(activated, shrink_weight) + shrink_offset
    layer_output = output_float.astype(jnp.bfloat16)
    activated_slope = rows_product(cotangent, shrink_weight)
    expanded_slope = gelu_back(activated_slope)[0].astype(jnp.bfloat16)
    normed_slope = rows_transposed(expanded_slope, expand_weight)
    residual_part, middle_gain_slope, middle_shift_slope = middle_back(normed_slope)
    residual_slope = cotangent.astype(jnp.float32) + residual_part
    branch_slope = residual_slope.astype(jnp.bfloat16)
    attended_slope = rows_transposed(branch_slope, mixing_weight).astype(jnp.bfloat16)
    attended_slope = attended_slope.reshape(token_rows, seq_count, local_heads, head_size)
    head_slopes = lax.all_to_all(attended_slope, "seq", split_axis=1, concat_axis=0, tiled=True)
    joint_heads = attention_backward(
        kept_heads, log_totals, head_slopes, places, key_segment, key_live, prompt, score_scale
    )
    joint_slope = lax.all_to_all(
        joint_heads, "seq", split_axis=0, concat_axis=1, tiled=True
    ).reshape(token_rows, 3 * width)
    entry_slope = rows_transposed(joint_slope, joint_weight)
    input_part, entry_gain_slope, entry_shift_slope = entry_back(entry_slope)
    input_gradient = (residual_slope + input_part).astype(jnp.bfloat16)
    slope_float = joint_slope.astype(jnp.float32).reshape(token_rows, HEADS, 3, head_size)
    small_sums = lax.psum(
        (
            entry_gain_slope,
            entry_shift_slope,
            jnp.sum(slope_float[:, :, 0], axis=0).reshape(width),
            jnp.sum(slope_float[:, :, 2], axis=0).reshape(width),
            jnp.sum(branch_slope.astype(jnp.float32), axis=0),
            middle_gain_slope,
            middle_shift_slope,
            jnp.sum(expanded_slope.astype(jnp.float32), axis=0),
            jnp.sum(cotangent.astype(jnp.float32), axis=0),
        ),
        ("grp", "seq"),
    )
    joined = lax.psum_scatter(
        jnp.concatenate(
            [
                row_outer(entry_normed, joint_slope),
                row_outer(attended, branch_slope),
                row_outer(middle_normed, expanded_slope),
                row_outer(cotangent, activated),
            ],
            axis=1,
        ),
        ("grp", "seq"),
        scatter_dimension=0,
        tiled=True,
    )
    attention_grads = joined[:, : 4 * width]
    hidden_grads = joined[:, 4 * width :]
    joint_gradient = attention_grads[:, : 3 * width]
    mixing_gradient = attention_grads[:, 3 * width :]
    expand_gradient = hidden_grads[:, :hidden_width]
    shrink_gradient = hidden_grads[:, hidden_width:]
    return (
        layer_output,
        input_gradient,
        small_sums[0],
        small_sums[1],
        joint_gradient,
        small_sums[2],
        small_sums[3],
        mixing_gradient,
        small_sums[4],
        small_sums[5],
        small_sums[6],
        expand_gradient,
        small_sums[7],
        shrink_gradient,
        small_sums[8],
    )


def solution(mesh):
    return jax.shard_map(
        shards,
        mesh=mesh,
        in_specs=(
            P(("grp", "seq"), None),
            P(),
            P(),
            P(("grp", "seq"), None),
            P(),
            P(),
            P(("grp", "seq"), None),
            P(),
            P(),
            P(),
            P(("grp", "seq"), None),
            P(),
            P(("grp", "seq"), None),
            P(),
            P("grp", None),
            P("grp", None),
            P(("grp", "seq"), None),
        ),
        out_specs=(
            P(("grp", "seq"), None),
            P(("grp", "seq"), None),
            P(),
            P(),
            P(("grp", "seq"), None),
            P(),
            P(),
            P(("grp", "seq"), None),
            P(),
            P(),
            P(),
            P(("grp", "seq"), None),
            P(),
            P(("grp", "seq"), None),
            P(),
        ),
        check_vma=False,
    )
```

profile of v0, /device:TPU:19, one launch (start us, length us, event | category | flops | bytes accessed | tf_op | source)
XLA Modules:
  0.0 2911.6 jit_solution(11853759373609467969)
XLA Ops:
  12.6 153.6 %all-gather.5.cloned.1.call-done = bf16[2048,6144]{1,0:T(8,128)(2,1)} async-done(((bf16[64,6144]{1,0:T(8,128)(2,1)}), bf16[2048,6144]{1,0:T(8,128)(2,1)}) %all-gather.5.cloned.1.call-update) | async-done | bytes 25165840 | tf_op jit(solution)/shard_map/all_gather | solution.py:54
  166.3 16.6 fusion.71
  187.4 5.1 all-to-all-start
  192.6 101.2 %all-to-all-done = bf16[256,8,2,3,128]{0,4,3,2,1:T(8,128)(2,1)S(1)} async-done(((bf16[256,8,2,3,128]{0,4,3,2,1:T(8,128)(2,1)}), bf16[256,8,2,3,128]{0,4,3,2,1:T(8,128)(2,1)S(1)}, u32[]{:S(2)}, u32[]{:S(2)}) %all-to-all-start) | async-done | bytes 3145760 | tf_op jit(solution)/shard_map/all_to_all | solution.py:217
  298.7 46.2 %while.31 = (s32[]{:T(128)}, bf16[4,512,2,128]{3,1,0,2:T(8,128)(2,1)}, f32[4,512,2]{1,2,0:T(2,128)S(1)}, s32[1,2048]{1,0:T(1,128)S(1)}, s32[4]{0:T(128)S(1)}, /*...) while((s32[]{:T(128)}, ...), condition=%wide.region_6.7_spmd, body=%wide.region_3.6_spmd.sunk | while | flops 1106390528 | bytes 32062688 | solution.py:103
  349.0 7.5 all-to-all-start.1
  356.5 47.3 %all-to-all-done.1 = bf16[2048,1,2,128]{3,2,1,0:T(2,128)(2,1)} async-done(((bf16[2048,1,2,128]{3,2,1,0:T(2,128)(2,1)}), bf16[2048,1,2,128]{3,2,1,0:T(2,128)(2,1)}, u32[]{:S(2)}, u32[]{:S(2)}) %all-to-all-start.1) | async-done | bytes 1048608 | tf_op jit(solution)/shard_map/all_to_all | solution.py:224
  408.5 6.4 fusion.80
  416.6 95.2 %all-gather.9.cloned.1.call-done = bf16[2048,8192]{1,0:T(8,128)(2,1)} async-done(((bf16[64,8192]{1,0:T(8,128)(2,1)}), bf16[2048,8192]{1,0:T(8,128)(2,1)}) %all-gather.9.cloned.1.call-update) | async-done | bytes 33554448 | tf_op jit(solution)/shard_map/all_gather | solution.py:54
  511.8 18.4 convolution_add_fusion
  530.2 177.5 %all-gather.11.cloned.1.call-done = bf16[2048,8192]{1,0:T(8,128)(2,1)} async-done(((bf16[64,8192]{1,0:T(8,128)(2,1)}), bf16[2048,8192]{1,0:T(8,128)(2,1)}) %all-gather.11.cloned.1.call-update) | async-done | bytes 33554448 | tf_op jit(solution)/shard_map/all_gather | solution.py:62
  707.6 34.3 %convert_reduce_fusion = (f32[8192]{0:T(1024)}, bf16[256,8192]{1,0:T(8,128)(2,1)}, f32[256,8192]{1,0:T(8,128)}) fusion(f32[256,8192]{1,0:T(8,128)} %convolution_add_fusion, bf16[256,2048]{1,0:T(8,128)(2,1)} %param.37, bf16[2048,8192]{1,0:T(8,128)(2,1)} %all-gather.11.cloned.1.call-done), kind=kOutput, calls=%fused_computation.77 | convolution fusion | flops 8745115648 | bytes 55607296 | tf_op jit(solution)/shard_map/dot_general | solution.py:52
  741.9 18.9 multiply_reduce_fusion.1
  766.2 8.1 fusion.81
  783.2 5.5 all-to-all-start.2
  788.7 9.1 multiply_convert_fusion.1
  797.9 13.4 all-to-all-done.2
  811.3 86.8 %while.32 = (s32[]{:T(128)}, f32[2048,2,128]{0,2,1:T(8,128)S(1)}, f32[2048,2,128]{0,2,1:T(8,128)}, bf16[4,512,2,128]{3,1,0,2:T(8,128)(2,1)}, s32[4]{0:T(128)S(1)...) while((s32[]{:T(128)}, f32[2048,2,128]{0,2,1:T(8,128)S(1)}, ...), condition=%wide.region_13.14_spmd.clone, body=%wide.region_11.13_spmd.clone.sunk | while | flops 2728013312 | bytes 93400416 | solution.py:163
  839.2 5.0 fusion.145
  861.3 5.0 fusion.145
  883.3 5.0 fusion.145
  902.3 28.7 copy.112
  930.9 7.6 all-to-all-start.3
  938.7 25.4 convolution_bitcast_fusion
  964.1 25.4 fusion.74
  989.6 16.2 all-to-all-done.3
  1014.5 21.5 fusion.69
  1036.0 130.5 %pad_maximum_fusion = f32[2048,24576]{1,0:T(8,128)} fusion(f32[2048,8192]{1,0:T(8,128)} %convolution_bitcast_fusion, f32[2048,8192]{1,0:T(8,128)} %fusion.74, f32[2048,2048]{1,0:T(8,128)} %fusion.81, f32[2048,6144]{1,0:T(8,128)} %fusion.69), kind=kLoop, calls=%fused_computation.72 | loop fusion | flops 150994944 | bytes 402653184 | tf_op jit(solution)/shard_map/concatenate | solution.py:270
  1168.1 20.0 fusion.56
  1192.8 20.5 fusion.75
  1221.8 1537.0 %reduce-scatter.2.cloned.1.call-done = f32[64,24576]{1,0:T(8,128)} async-done(((f32[2048,24576]{1,0:T(8,128)}), f32[64,24576]{1,0:T(8,128)}) %reduce-scatter.2.cloned.1.call-update) | async-done | bytes 6291472 | tf_op jit(solution)/shard_map/reduce_scatter | solution.py:269
  2768.0 124.6 %all-reduce.3.cloned.1.call-done = (f32[2048]{0:T(1024)}, f32[2048]{0:T(1024)}, f32[2048]{0:T(1024)}, f32[2048]{0:T(1024)}, f32[2048]{0:T(1024)}, /*index=5*/f32...) async-done(((f32[2048]{0:T(1024)}, f32[2048]{0:T(1024)}, f32[2048]{0:T(1024)}, f32[2048]{0:T(1024)}, f32[2048]{0:T(1024)}, /*index=5*/f32[2048]{0:T(1024)}, ...) | async-done | bytes 98320 | tf_op jit(solution)/shard_map/psum | solution.py:255
  (270 shorter events, 200.3 us)
Async XLA Ops:
  7.2 159.0 %copy-start.20 = (f32[2048]{0:T(1024)S(1)}, f32[2048]{0:T(1024)}, u32[]{:S(2)}) copy-start(f32[2048]{0:T(1024)} %param.22) | copy-start | bytes 24580
  7.2 159.0 %copy-start.25 = (f32[2048]{0:T(1024)S(1)}, f32[2048]{0:T(1024)}, u32[]{:S(2)}) copy-start(f32[2048]{0:T(1024)} %param.23) | copy-start | bytes 24580
  7.2 159.0 %all-gather.5.cloned.1.call-start = ((), (), s32[]{:S(2)}) async-start(), calls=%async_computation.5 | async-start | bytes 25952256 | tf_op jit(solution)/shard_map/all_gather | solution.py:54
  8.0 400.5 %all-gather.7.cloned.1.call-start = ((), (), s32[]{:S(2)}) async-start(), calls=%async_computation.6 | async-start | bytes 8650752 | tf_op jit(solution)/shard_map/all_gather | solution.py:54
  8.7 503.1 %all-gather.9.cloned.1.call-start = ((), (), s32[]{:S(2)}) async-start(), calls=%async_computation.7 | async-start | bytes 34603008 | tf_op jit(solution)/shard_map/all_gather | solution.py:54
  9.5 698.2 %all-gather.11.cloned.1.call-start = ((), (), s32[]{:S(2)}) async-start(), calls=%async_computation.8 | async-start | bytes 34603008 | tf_op jit(solution)/shard_map/all_gather | solution.py:62
  11.6 171.3 %copy-start.29 = (f32[256]{0:T(256)}, f32[256]{0:T(256)S(1)}, u32[]{:S(2)}) copy-start(f32[256]{0:T(256)S(1)} %broadcast_multiply_fusion.1) | copy-start | bytes 3076
  12.0 170.8 %copy-start.34 = (f32[256]{0:T(256)}, f32[256]{0:T(256)S(1)}, u32[]{:S(2)}) copy-start(f32[256]{0:T(256)S(1)} %fusion.67) | copy-start | bytes 3076
  187.4 106.5 %all-to-all-start = ((bf16[256,8,2,3,128]{0,4,3,2,1:T(8,128)(2,1)}), bf16[256,8,2,3,128]{0,4,3,2,1:T(8,128)(2,1)S(1)}, u32[]{:S(2)}, u32[]{:S(2)}) async-start(bf16[256,8,2,3,128]{0,4,3,2,1:T(8,128)(2,1)} %add_convert_fusion.1), calls=%async_computation | async-start | bytes 6291456 | tf_op jit(solution)/shard_map/all_to_all | solution.py:217
  345.0 11.5 copy-start.3
  345.0 11.5 copy-start.10
  345.0 63.5 %copy-start.41 = (f32[2048]{0:T(1024)S(1)}, f32[2048]{0:T(1024)}, u32[]{:S(2)}) copy-start(f32[2048]{0:T(1024)} %param.28) | copy-start | bytes 24580
  349.0 54.8 %all-to-all-start.1 = ((bf16[2048,1,2,128]{3,2,1,0:T(2,128)(2,1)}), bf16[2048,1,2,128]{3,2,1,0:T(2,128)(2,1)}, u32[]{:S(2)}, u32[]{:S(2)}) async-start(bf16[2048,1,2,128]{3,2,1,0:T(2,128)(2,1)} %copy.104), calls=%async_computation.1 | async-start | bytes 2097152 | tf_op jit(solution)/shard_map/all_to_all | solution.py:224
  408.4 103.4 %copy-start.18 = (f32[2048]{0:T(1024)S(1)}, f32[2048]{0:T(1024)}, u32[]{:S(2)}) copy-start(f32[2048]{0:T(1024)} %param.29) | copy-start | bytes 24580
  408.4 103.4 %copy-start.23 = (f32[2048]{0:T(1024)S(1)}, f32[2048]{0:T(1024)}, u32[]{:S(2)}) copy-start(f32[2048]{0:T(1024)} %param.30) | copy-start | bytes 24580
  408.4 103.4 %copy-start.45 = (f32[8192]{0:T(1024)S(1)}, f32[8192]{0:T(1024)}, u32[]{:S(2)}) copy-start(f32[8192]{0:T(1024)} %param.32) | copy-start | bytes 98308
  414.9 346.0 %copy-start.27 = (f32[256]{0:T(256)}, f32[256]{0:T(256)S(1)}, u32[]{:S(2)}) copy-start(f32[256]{0:T(256)S(1)} %broadcast_multiply_fusion) | copy-start | bytes 3076
  416.6 344.3 %copy-start.32 = (f32[256]{0:T(256)}, f32[256]{0:T(256)S(1)}, u32[]{:S(2)}) copy-start(f32[256]{0:T(256)S(1)} %fusion.68) | copy-start | bytes 3076
  760.9 13.4 slice-start
  783.2 28.1 all-to-all-start.2
  930.9 74.8 %all-to-all-start.3 = ((bf16[2048,1,2,3,128]{4,2,3,1,0:T(2,128)(2,1)}), bf16[2048,1,2,3,128]{4,2,3,1,0:T(2,128)(2,1)}, u32[]{:S(2)}, u32[]{:S(2)}) async-start(bf16[2048,1,2,3,128]{4,2,3,1,0:T(2,128)(2,1)} %copy.112), calls=%async_computation.3 | async-start | bytes 6291456 | tf_op jit(solution)/shard_map/all_to_all | solution.py:248
  938.6 25.5 copy-start.6
  938.6 25.5 copy-start.19
  938.6 25.5 copy-start.24
  938.6 25.5 copy-start.28
  938.6 25.5 copy-start.33
  938.6 1820.2 %reduce-scatter.2.cloned.1.call-start = ((), (), s32[]{:S(2)}) async-start(), calls=%async_computation.9 | async-start | bytes 207618048 | tf_op jit(solution)/shard_map/reduce_scatter | solution.py:269
  1166.5 1726.0 %all-reduce.3.cloned.1.call-start = ((), (), s32[]{:S(2)}) async-start(), calls=%async_computation.10 | async-start | bytes 196608 | tf_op jit(solution)/shard_map/psum | solution.py:255
  1192.8 20.5 copy-start.40
  1192.8 20.5 copy-start.36
  1192.8 24.2 copy-start.14
  1192.8 24.2 copy-start.38
  (36 other events, 138.8 us)
Sparse Core Ops, SparseCore 0:
  11.0 155.1 all-gather.4
  169.2 120.9 all-gather.6
  293.2 218.5 all-gather.8
  514.6 192.9 all-gather.10
  1166.6 1592.1 reduce-scatter.1
  2766.2 126.2 all-reduce.2
where the time goes:
time: 2920 us; the launch traced here: 2910 us
  waiting for transfers between devices  2270 us (78%)
  matrix products  296 us (10%)
  other arithmetic  202 us (7%)
  local copies, waits for them, and re-layouts  98 us (3%)
    reduce_scatter x1, waiting for transfers between devices, shards(): lax.psum_scatter(jnp.concatenate([row_outer(entry_normed, joint_slope), r...  1540 us
    all_gather x3, waiting for transfers between devices, rows_product(): lax.all_gather(weight, ('grp', 'seq'), axis=0, tiled=True)  249 us
    all_gather x1, waiting for transfers between devices, rows_transposed(): lax.all_gather(weight, ('grp', 'seq'), axis=0, tiled=True)  177 us
    concatenate x1, other arithmetic, shards(): jnp.concatenate([row_outer(entry_normed, joint_slope), row_outer(attended...  130 us
    psum x1, waiting for transfers between devices, shards(): lax.psum((entry_gain_slope, entry_shift_slope, jnp.sum(slope_float[:, :,...  125 us
    all_to_all x1, waiting for transfers between devices, shards(): lax.all_to_all(joint_values, 'seq', split_axis=1, concat_axis=0, tiled=True)  101 us
    dot_general x4, matrix products, row_outer(): lax.dot_general(left_matrix, right_matrix, (((0,), (0,)), ((), ())), pref...  80.5 us
    dot_general x4, matrix products, rows_product(): jnp.dot(left_matrix, lax.all_gather(weight, ('grp', 'seq'), axis=0, tiled...  75.6 us
  transfers between devices with their start and end apart: 10, of which 9 were waited for; matrix products, arithmetic and copies ran while one was open for 8% of the time, Pallas kernels for 0%

commit v1 on v0

v1 whole, which is shorter than its diff:
```python
import jax
import jax.numpy as jnp
from jax import lax
from jax.sharding import Mesh, PartitionSpec as P

HEADS = 16
CONT = 256
QBLOCK = 512
PLANE = ("grp", "sub")
EVERY = ("grp", "rep", "sub")

norm_epsilon = 1e-05
masked_score = -1e30


def norm_terms(values):
    average = jnp.mean(values, axis=-1, keepdims=True)
    centered = values - average
    variance = jnp.mean(centered * centered, axis=-1, keepdims=True)
    inverse = lax.rsqrt(variance + norm_epsilon)
    return centered * inverse, inverse


def norm_back(slope, gain, normal, inverse):
    scaled = slope * gain
    return inverse * (
        scaled
        - jnp.mean(scaled, axis=-1, keepdims=True)
        - normal * jnp.mean(scaled * normal, axis=-1, keepdims=True)
    )


def exact_gelu(values):
    return jax.nn.gelu(values, approximate=False)


def key_bounds(positions, lengths, prompt):
    segment = (positions - prompt) // CONT
    within = positions - prompt - segment * CONT
    slot_ids = jnp.arange(lengths.shape[0], dtype=jnp.int32)
    slot_limit = jnp.sum(
        jnp.where(segment[:, None] == slot_ids[None, :], lengths[None, :], 0), axis=1
    )
    last = prompt + (segment + 1) * CONT - 1
    last = jnp.where(within < slot_limit, last, -1)
    return jnp.where(positions < prompt, positions.shape[0], last)


def block_mask(query_place, key_place, key_last):
    query_col = query_place[:, None]
    return (key_place[None, :] <= query_col) & (query_col <= key_last[None, :])


def product(left_matrix, right_matrix):
    return jnp.dot(left_matrix, right_matrix, preferred_element_type=jnp.float32)


def product_transposed(left_matrix, right_matrix):
    return lax.dot_general(
        left_matrix,
        right_matrix,
        (((1,), (1,)), ((), ())),
        preferred_element_type=jnp.float32,
    )


def row_outer(left_matrix, right_matrix):
    return lax.dot_general(
        left_matrix, right_matrix, (((0,), (0,)), ((), ())), preferred_element_type=jnp.float32
    )


def attention_forward(grouped, places, key_last, score_scale):
    queries = grouped[:, :, 0]
    key_vectors = grouped[:, :, 1]
    values = grouped[:, :, 2]
    rows_total = grouped.shape[0]

    def one_block(block_index):
        first_row = block_index * QBLOCK
        block_queries = lax.dynamic_slice_in_dim(queries, first_row, QBLOCK, 0)
        block_places = lax.dynamic_slice_in_dim(places, first_row, QBLOCK, 0)
        allowed = block_mask(block_places, places, key_last)
        scores = (
            jnp.einsum(
                "qhe,khe->hqk", block_queries, key_vectors, preferred_element_type=jnp.float32
            )
            * score_scale
        )
        scores = jnp.where(allowed[None], scores, masked_score)
        row_top = jnp.max(scores, axis=2, keepdims=True)
        row_total = jnp.sum(jnp.exp(scores - row_top), axis=2, keepdims=True)
        log_total = row_top + jnp.log(row_total)
        soft_weights = jnp.exp(scores - log_total).astype(jnp.bfloat16)
        mixture = jnp.einsum(
            "hqk,khe->qhe", soft_weights, values, preferred_element_type=jnp.float32
        )
        return (mixture.astype(jnp.bfloat16), jnp.transpose(log_total[:, :, 0]))

    mixture, log_totals = lax.map(one_block, jnp.arange(rows_total // QBLOCK, dtype=jnp.int32))
    return mixture.reshape(rows_total, -1), log_totals.reshape(rows_total, -1)


def attention_backward(grouped, log_totals, slopes, places, key_last, score_scale):
    queries = grouped[:, :, 0]
    key_vectors = grouped[:, :, 1]
    values = grouped[:, :, 2]
    rows_total = grouped.shape[0]

    def one_block(running, block_index):
        key_sum, value_sum = running
        first_row = block_index * QBLOCK
        block_queries = lax.dynamic_slice_in_dim(queries, first_row, QBLOCK, 0)
        block_slopes = lax.dynamic_slice_in_dim(slopes, first_row, QBLOCK, 0)
        block_totals = lax.dynamic_slice_in_dim(log_totals, first_row, QBLOCK, 0)
        block_places = lax.dynamic_slice_in_dim(places, first_row, QBLOCK, 0)
        allowed = block_mask(block_places, places, key_last)
        scores = (
            jnp.einsum(
                "qhe,khe->hqk", block_queries, key_vectors, preferred_element_type=jnp.float32
            )
            * score_scale
        )
        scores = jnp.where(allowed[None], scores, masked_score)
        probable = jnp.exp(scores - jnp.transpose(block_totals)[:, :, None])
        weight_slope = jnp.einsum(
            "qhe,khe->hqk", block_slopes, values, preferred_element_type=jnp.float32
        )
        centre = jnp.sum(probable * weight_slope, axis=2, keepdims=True)
        score_slope = (probable * (weight_slope - centre)).astype(jnp.bfloat16)
        query_slope = (
            jnp.einsum("hqk,khe->qhe", score_slope, key_vectors, preferred_element_type=jnp.float32)
            * score_scale
        )
        key_sum = (
            key_sum
            + jnp.einsum(
                "hqk,qhe->khe", score_slope, block_queries, preferred_element_type=jnp.float32
            )
            * score_scale
        )
        value_sum = value_sum + jnp.einsum(
            "hqk,qhe->khe",
            probable.astype(jnp.bfloat16),
            block_slopes,
            preferred_element_type=jnp.float32,
        )
        return ((key_sum, value_sum), query_slope)

    empty_sums = jnp.zeros(values.shape, jnp.float32)
    (key_sum, value_sum), query_slopes = lax.scan(
        one_block, (empty_sums, empty_sums), jnp.arange(rows_total // QBLOCK, dtype=jnp.int32)
    )
    query_slopes = query_slopes.reshape(values.shape)
    return jnp.stack([query_slopes, key_sum, value_sum], axis=2).astype(jnp.bfloat16)


def plane_columns(weight, plane_count):
    rows, columns = weight.shape
    own = lax.all_to_all(
        weight.reshape(rows, plane_count, columns // plane_count),
        PLANE,
        split_axis=1,
        concat_axis=0,
        tiled=True,
    ).reshape(plane_count * rows, columns // plane_count)
    every = lax.all_gather(own, "rep", axis=0, tiled=True)
    groups, reps, subs = (lax.axis_size(name) for name in EVERY)
    every = every.reshape(reps, groups, subs, rows, -1).transpose(1, 0, 2, 3, 4)
    return every.reshape(reps * groups * subs * rows, -1)


def owner_rows(gradient, plane_count):
    groups, reps, subs = (lax.axis_size(name) for name in EVERY)
    columns = gradient.shape[1]
    rows = gradient.shape[0] // (groups * reps * subs)
    ordered = gradient.astype(jnp.bfloat16).reshape(groups, reps, subs, rows, columns)
    ordered = ordered.transpose(1, 0, 2, 3, 4).reshape(-1, columns)
    summed = lax.psum_scatter(ordered, "rep", scatter_dimension=0, tiled=True)
    own = lax.all_to_all(
        summed.reshape(plane_count, rows, columns), PLANE, split_axis=0, concat_axis=0, tiled=True
    )
    return own.transpose(1, 0, 2).reshape(rows, plane_count * columns).astype(jnp.float32)


def shards(
    layer_input,
    entry_gain,
    entry_shift,
    joint_weight,
    query_offset,
    value_offset,
    mixing_weight,
    attention_offset,
    middle_gain,
    middle_shift,
    expand_weight,
    expand_offset,
    shrink_weight,
    shrink_offset,
    placement,
    slot_lengths,
    cotangent,
):
    token_rows, width = layer_input.shape
    hidden_width = expand_weight.shape[1]
    groups, reps, subs = (lax.axis_size(name) for name in EVERY)
    plane_count = groups * subs
    plane_index = lax.axis_index(PLANE)
    rep_index = lax.axis_index("rep")
    head_size = width // HEADS
    local_heads = HEADS // plane_count
    head_columns = local_heads * head_size
    score_scale = head_size ** (-0.5)

    placements = lax.all_gather(placement, "grp", axis=0, tiled=True)
    lengths_all = lax.all_gather(slot_lengths, "grp", axis=0, tiled=True)
    places = lax.dynamic_index_in_dim(placements, rep_index, 0, keepdims=False)
    lengths = lax.dynamic_index_in_dim(lengths_all, rep_index, 0, keepdims=False)
    prompt = places.shape[0] // 2
    key_last = key_bounds(places, lengths, prompt)

    joint_slice = plane_columns(joint_weight, plane_count)
    expand_slice = plane_columns(expand_weight, plane_count)
    shrink_slice = plane_columns(shrink_weight, plane_count)
    mixing_whole = lax.all_gather(mixing_weight, EVERY, axis=0, tiled=True)

    input_float = layer_input.astype(jnp.float32)
    entry_normal, entry_inverse = norm_terms(input_float)
    entry_normed = (entry_normal * entry_gain + entry_shift).astype(jnp.bfloat16)
    entry_all = lax.all_gather(entry_normed, PLANE, axis=0, tiled=True)
    plane_rows = entry_all.shape[0]

    offsets = jnp.stack(
        [
            query_offset.reshape(HEADS, head_size),
            jnp.zeros((HEADS, head_size), jnp.float32),
            value_offset.reshape(HEADS, head_size),
        ],
        axis=1,
    ).reshape(-1)
    offsets = lax.dynamic_slice_in_dim(offsets, plane_index * 3 * head_columns, 3 * head_columns)
    joint_values = (product(entry_all, joint_slice) + offsets).astype(jnp.bfloat16)
    heads_kept = lax.all_to_all(
        joint_values.reshape(groups, plane_rows // groups, 3 * head_columns),
        "rep",
        split_axis=0,
        concat_axis=0,
        tiled=True,
    ).reshape(plane_rows, local_heads, 3, head_size)
    mixture, log_totals = attention_forward(heads_kept, places, key_last, score_scale)

    def to_tokens(array):
        columns = array.shape[1]
        at_plane = lax.all_to_all(
            array.reshape(reps, plane_rows // reps, columns),
            "rep",
            split_axis=0,
            concat_axis=0,
            tiled=True,
        )
        return at_plane.reshape(plane_count, token_rows, columns)

    attended = lax.all_to_all(to_tokens(mixture), PLANE, split_axis=0, concat_axis=0, tiled=True)
    attended = attended.transpose(1, 0, 2).reshape(token_rows, width)
    residual = input_float + (product(attended, mixing_whole) + attention_offset)
    middle_normal, middle_inverse = norm_terms(residual)
    middle_normed = (middle_normal * middle_gain + middle_shift).astype(jnp.bfloat16)
    middle_all = lax.all_gather(middle_normed, PLANE, axis=0, tiled=True)
    cotangent_all = lax.all_gather(cotangent, PLANE, axis=0, tiled=True)

    hidden_local = hidden_width // plane_count
    offset_local = lax.dynamic_slice_in_dim(expand_offset, plane_index * hidden_local, hidden_local)
    expanded = product(middle_all, expand_slice) + offset_local
    activated_float, gelu_back = jax.vjp(exact_gelu, expanded)
    activated = activated_float.astype(jnp.bfloat16)
    activated_slope = product(cotangent_all, shrink_slice)
    expanded_slope = gelu_back(activated_slope)[0].astype(jnp.bfloat16)
    slope_part = product_transposed(expanded_slope, expand_slice).astype(jnp.bfloat16)
    normed_slope = lax.psum_scatter(slope_part, PLANE, scatter_dimension=0, tiled=True).astype(
        jnp.float32
    )
    output_part = product_transposed(activated, shrink_slice).astype(jnp.bfloat16)
    shrunk = lax.psum_scatter(output_part, PLANE, scatter_dimension=0, tiled=True)
    layer_output = (residual + shrunk.astype(jnp.float32) + shrink_offset).astype(jnp.bfloat16)

    cotangent_float = cotangent.astype(jnp.float32)
    residual_slope = cotangent_float + norm_back(
        normed_slope, middle_gain, middle_normal, middle_inverse
    )
    branch_slope = residual_slope.astype(jnp.bfloat16)
    attended_slope = product_transposed(branch_slope, mixing_whole).astype(jnp.bfloat16)
    slope_plane = lax.all_to_all(
        attended_slope.reshape(token_rows, plane_count, head_columns).transpose(1, 0, 2),
        PLANE,
        split_axis=0,
        concat_axis=0,
        tiled=True,
    )
    head_slopes = lax.all_to_all(
        slope_plane.reshape(groups, plane_rows // groups, head_columns),
        "rep",
        split_axis=0,
        concat_axis=0,
        tiled=True,
    ).reshape(plane_rows, local_heads, head_size)
    joint_heads = attention_backward(
        heads_kept, log_totals, head_slopes, places, key_last, score_scale
    )
    joint_slope = to_tokens(joint_heads.reshape(plane_rows, 3 * head_columns)).reshape(
        plane_rows, 3 * head_columns
    )
    entry_part = product_transposed(joint_slope, joint_slice).astype(jnp.bfloat16)
    entry_slope = lax.psum_scatter(entry_part, PLANE, scatter_dimension=0, tiled=True).astype(
        jnp.float32
    )
    input_gradient = (
        residual_slope + norm_back(entry_slope, entry_gain, entry_normal, entry_inverse)
    ).astype(jnp.bfloat16)

    slope_sums = jnp.sum(joint_slope.astype(jnp.float32), axis=0).reshape(local_heads, 3, head_size)

    def placed(piece, whole_size):
        return lax.dynamic_update_slice_in_dim(
            jnp.zeros((whole_size,), jnp.float32), piece, plane_index * piece.shape[0], 0
        )

    small_sums = lax.psum(
        (
            jnp.sum(entry_slope * entry_normal, axis=0),
            jnp.sum(entry_slope, axis=0),
            placed(slope_sums[:, 0].reshape(-1), width),
            placed(slope_sums[:, 2].reshape(-1), width),
            jnp.sum(branch_slope.astype(jnp.float32), axis=0),
            jnp.sum(normed_slope * middle_normal, axis=0),
            jnp.sum(normed_slope, axis=0),
            placed(jnp.sum(expanded_slope.astype(jnp.float32), axis=0), hidden_width),
            jnp.sum(cotangent_float, axis=0),
        ),
        EVERY,
    )
    shrink_gradient = owner_rows(row_outer(cotangent_all, activated), plane_count)
    expand_gradient = owner_rows(row_outer(middle_all, expanded_slope), plane_count)
    mixing_gradient = lax.psum_scatter(
        row_outer(attended, branch_slope).astype(jnp.bfloat16),
        EVERY,
        scatter_dimension=0,
        tiled=True,
    ).astype(jnp.float32)
    joint_gradient = owner_rows(row_outer(entry_all, joint_slope), plane_count)
    return (
        layer_output,
        input_gradient,
        small_sums[0],
        small_sums[1],
        joint_gradient,
        small_sums[2],
        small_sums[3],
        mixing_gradient,
        small_sums[4],
        small_sums[5],
        small_sums[6],
        expand_gradient,
        small_sums[7],
        shrink_gradient,
        small_sums[8],
    )


def solution(mesh):
    groups, sequence = mesh.shape["grp"], mesh.shape["seq"]
    subs = sequence // groups
    planes = Mesh(mesh.devices.reshape(groups, sequence // subs, subs), EVERY)
    rows, whole, group_rows = P(EVERY, None), P(), P("grp", None)
    return jax.shard_map(
        shards,
        mesh=planes,
        in_specs=(
            (rows, whole, whole, rows, whole, whole, rows, whole, whole, whole, rows, whole, rows)
            + (whole, group_rows, group_rows, rows)
        ),
        out_specs=(
            (rows, rows, whole, whole, rows, whole, whole, rows, whole, whole, whole, rows, whole)
            + (rows, whole)
        ),
        check_vma=False,
    )
```

time: 2920 us -> 1540 us (0.53)
  waiting for transfers between devices: 2270 us -> 865 us
  blocking collectives: 0 us -> 156 us
  other arithmetic: 202 us -> 72.9 us
  matrix products: 296 us -> 255 us
    reduce_scatter x1 -> x7, waiting for transfers between devices: 1540 us -> 343 us  [the longest x1 162 us: shards(): lax.psum_scatter(row_outer(attended, branch_slope).astype(jnp.bfloat16),...]
    all_gather x4 -> x7, waiting for transfers between devices: 426 us -> 215 us  [the longest x3 67.3 us: plane_columns(): every = lax.all_gather(own, 'rep', axis=0, tiled=True)]
    all_to_all x0 -> x4, blocking collectives: none -> 145 us  [the longest x2 111 us: to_tokens(): lax.all_to_all(array.reshape(reps, plane_rows // reps, columns), 'rep', s...]
    concatenate x1 -> x0, other arithmetic: 130 us -> none  [shards(): jnp.concatenate([row_outer(entry_normed, joint_slope), row_outer(attended...]
    dot_general x4, matrix products: 80.5 us -> 43.1 us  [row_outer(): lax.dot_general(left_matrix, right_matrix, (((0,), (0,)), ((), ())), pref...]
    dot_general x8, matrix products: 138 us -> 109 us  [the longest x4 65.3 us: product(): jnp.dot(left_matrix, right_matrix, preferred_element_type=jnp.float32)]
    all_to_all x4 -> x8, waiting for transfers between devices: 178 us -> 177 us  [the longest x1 87.1 us: shards(): lax.all_to_all(joint_values.reshape(groups, plane_rows // groups, 3 * hea...]
  transfers between devices with their start and end apart: 10 -> 23, of which waited for: 9 -> 18; matrix products, arithmetic and copies ran while one was open for 8% -> 25% of each run, Pallas kernels for 0% -> 0%
where the time goes in v1:
time: 1540 us
  waiting for transfers between devices  865 us (56%)
  matrix products  255 us (17%)
  blocking collectives  156 us (10%)
  local copies, waits for them, and re-layouts  124 us (8%)
  other arithmetic  72.9 us (5%)
  starting transfers between devices  41.9 us (3%)
    reduce_scatter x1, waiting for transfers between devices, shards(): lax.psum_scatter(row_outer(attended, branch_slope).astype(jnp.bfloat16),...  162 us
    psum x1, waiting for transfers between devices, shards(): lax.psum((jnp.sum(entry_slope * entry_normal, axis=0), jnp.sum(entry_slop...  128 us
    all_to_all x2, blocking collectives, to_tokens(): lax.all_to_all(array.reshape(reps, plane_rows // reps, columns), 'rep', s...  111 us
    all_to_all x1, waiting for transfers between devices, shards(): lax.all_to_all(joint_values.reshape(groups, plane_rows // groups, 3 * hea...  87.1 us
    reduce_scatter x1, waiting for transfers between devices, shards(): lax.psum_scatter(entry_part, PLANE, scatter_dimension=0, tiled=True)  72.9 us
    reduce_scatter x1, waiting for transfers between devices, shards(): lax.psum_scatter(output_part, PLANE, scatter_dimension=0, tiled=True)  72.3 us
    all_gather x3, waiting for transfers between devices, plane_columns(): every = lax.all_gather(own, 'rep', axis=0, tiled=True)  67.3 us
    dot_general x4, matrix products, product(): jnp.dot(left_matrix, right_matrix, preferred_element_type=jnp.float32)  65.3 us
  transfers between devices with their start and end apart: 23, of which 18 were waited for; matrix products, arithmetic and copies ran while one was open for 25% of the time, Pallas kernels for 0%

profile of v1, /device:TPU:19, one launch (start us, length us, event | category | flops | bytes accessed | tf_op | source)
XLA Modules:
  0.0 1535.1 jit_solution(3426588837099018649)
XLA Ops:
  8.5 15.2 all_to_all.90
  34.7 12.2 all-to-all-done.4
  52.4 34.0 %all-gather.12.cloned.1.call-done = bf16[2048,768]{1,0:T(8,128)(2,1)} async-done(((bf16[512,768]{1,0:T(8,128)(2,1)}), bf16[2048,768]{1,0:T(8,128)(2,1)}) %all-gather.12.cloned.1.call-update) | async-done | bytes 3145744 | tf_op jit(solution)/shard_map/all_gather | solution.py:167
  90.2 53.4 %all-gather.10.cloned.1.call-done = bf16[2048,2048]{1,0:T(8,128)(2,1)} async-done(((bf16[256,2048]{1,0:T(8,128)(2,1)}), bf16[2048,2048]{1,0:T(8,128)(2,1)}) %all-gather.10.cloned.1.call-update) | async-done | bytes 8388624 | tf_op jit(solution)/shard_map/all_gather | solution.py:231
  143.7 11.2 add_convert_fusion.1
  175.4 87.1 %all-to-all-done.1 = bf16[4,512,768]{1,2,0:T(8,128)(2,1)} async-done(((bf16[4,512,768]{1,2,0:T(8,128)(2,1)}), bf16[4,512,768]{1,2,0:T(8,128)(2,1)}, u32[]{:S(2)}, u32[]{:S(2)}) %all-to-all-start.1) | async-done | bytes 3145760 | tf_op jit(solution)/shard_map/all_to_all | solution.py:244
  281.4 53.2 %while.27 = (s32[]{:T(128)}, bf16[4,512,2,128]{1,3,2,0:T(8,128)(2,1)}, f32[4,512,2]{1,2,0:T(2,128)}, s32[2048]{0:T(1024)S(1)}, s32[4]{0:T(128)S(1)}, /*index=5*/...) while((s32[]{:T(128)}, ...), condition=%wide.region_6.7_spmd, body=%wide.region_3.6_spmd.sunk | while | flops 1100086272 | bytes 33086656 | solution.py:100
  334.7 37.8 %all_to_all.91 = bf16[4,512,256]{1,2,0:T(8,128)(2,1)} all-to-all(bf16[4,512,256]{1,2,0:T(8,128)(2,1)} %bitcast.238), channel_id=1, replica_groups=mesh['grp'=4,'rep'=4,'sub'=2] {'rep'}, dimensions={0} | all-to-all | bytes 2097152 | tf_op jit(solution)/shard_map/all_to_all | solution.py:255
  374.8 18.5 %all_to_all.92 = bf16[8,256,256]{2,1,0:T(8,128)(2,1)} all-to-all(bf16[8,256,256]{2,1,0:T(8,128)(2,1)} %bitcast.217), channel_id=1, replica_groups=mesh['grp'=4,'rep'=4,'sub'=2] {'grp','sub'}, dimensions={0} | all-to-all | bytes 2097152 | tf_op jit(solution)/shard_map/all_to_all | solution.py:264
  411.8 33.4 %all-gather.20.cloned.1.call-done = bf16[2048,1024]{1,0:T(8,128)(2,1)} async-done(((bf16[512,1024]{1,0:T(8,128)(2,1)}), bf16[2048,1024]{1,0:T(8,128)(2,1)}) %all-gather.20.cloned.1.call-update) | async-done | bytes 4194320 | tf_op jit(solution)/shard_map/all_gather | solution.py:167
  450.1 52.3 %all-gather.16.cloned.1.call-done = bf16[2048,2048]{1,0:T(8,128)(2,1)} async-done(((bf16[256,2048]{1,0:T(8,128)(2,1)}), bf16[2048,2048]{1,0:T(8,128)(2,1)}) %all-gather.16.cloned.1.call-update) | async-done | bytes 8388624 | tf_op jit(solution)/shard_map/all_gather | solution.py:269
  502.3 14.4 fusion.70
  516.8 41.9 %all-gather.22.cloned.1.call-done = bf16[2048,2048]{1,0:T(8,128)(2,1)} async-done(((bf16[256,2048]{1,0:T(8,128)(2,1)}), bf16[2048,2048]{1,0:T(8,128)(2,1)}) %all-gather.22.cloned.1.call-update) | async-done | bytes 8388624 | tf_op jit(solution)/shard_map/all_gather | solution.py:270
  558.6 33.5 %convert_reduce_fusion = (f32[1024]{0:T(1024)}, bf16[2048,1024]{1,0:T(8,128)(2,1)S(1)}, f32[2048,1024]{1,0:T(8,128)}) fusion(f32[2048,1024]{1,0:T(8,128)} %fusion.70, f32[1024]{0:T(1024)S(1)} %dynamic_slice.42, bf16[2048,2048]{1,0:T(8,128)(2,1)} %all-gather.22.cloned.1.call-done, bf16[2048,1024]{1,0:T(8,128)(2,1)} %bitcast.207), kind=kOutput, calls=%fused_computation.46 | convolution fusion | flops 8747219968 | bytes 33562624 | tf_op jit(solution)/shard_map/dot_general | solution.py:55
  594.1 11.3 convolution_convert_fusion.2
  605.5 10.7 multiply_convert_fusion.1
  616.2 14.2 convolution_convert_fusion.3
  630.4 13.1 convolution_convert_fusion.4
  646.1 30.2 %reduce-scatter.10.cloned.1.call-done = bf16[256,2048]{1,0:T(8,128)(2,1)} async-done(((bf16[2048,2048]{1,0:T(8,128)(2,1)}), bf16[256,2048]{1,0:T(8,128)(2,1)}) %reduce-scatter.10.cloned.1.call-update) | async-done | bytes 1048592 | tf_op jit(solution)/shard_map/reduce_scatter | solution.py:280
  679.2 72.3 %reduce-scatter.8.cloned.1.call-done = bf16[256,2048]{1,0:T(8,128)(2,1)} async-done(((bf16[2048,2048]{1,0:T(8,128)(2,1)}), bf16[256,2048]{1,0:T(8,128)(2,1)}) %reduce-scatter.8.cloned.1.call-update) | async-done | bytes 1048592 | tf_op jit(solution)/shard_map/reduce_scatter | solution.py:284
  768.9 13.5 all-to-all-done.6
  787.0 14.1 convert_bitcast_fusion
  812.5 24.9 %all-to-all-done.7 = bf16[4,512,256]{2,1,0:T(8,128)(2,1)S(1)} async-done(((bf16[4,512,256]{2,1,0:T(8,128)(2,1)}), bf16[4,512,256]{2,1,0:T(8,128)(2,1)S(1)}, u32[]{:S(2)}, u32[]{:S(2)}) %all-to-all-start.7) | async-done | bytes 1048608 | tf_op jit(solution)/shard_map/all_to_all | solution.py:300
  839.0 112.1 %while.28 = (s32[]{:T(128)}, f32[2048,2,128]{0,2,1:T(8,128)}, f32[2048,2,128]{0,2,1:T(8,128)}, bf16[4,512,2,128]{3,1,0,2:T(8,128)(2,1)}, s32[4]{0:T(128)S(1)}, /...) while((s32[]{:T(128)}, f32[2048,2,128]{0,2,1:T(8,128)}, ...), condition=%wide.region_15.16_spmd.clone, body=%wide.region_13.15_spmd.clone.sunk | while | flops 2721709056 | bytes 147901232 | solution.py:151
  965.7 73.6 %all_to_all.93 = bf16[4,512,768]{1,2,0:T(8,128)(2,1)S(1)} all-to-all(bf16[4,512,768]{1,2,0:T(8,128)(2,1)S(1)} %copy.180), channel_id=1, replica_groups=mesh['grp'=4,'rep'=4,'sub'=2] {'rep'}, dimensions={0} | all-to-all | bytes 6291456 | tf_op jit(solution)/shard_map/all_to_all | solution.py:255
  1061.5 11.4 convolution_convert_fusion.1
  1079.6 13.5 all-to-all-done.10
  1102.2 10.3 all-to-all-done.11
  1127.7 15.4 %all-to-all-done.9 = bf16[8,64,768]{2,1,0:T(8,128)(2,1)} async-done(((bf16[8,64,768]{2,1,0:T(8,128)(2,1)}), bf16[8,64,768]{2,1,0:T(8,128)(2,1)}, u32[]{:S(2)}, u32[]{:S(2)}) %all-to-all-start.9) | async-done | bytes 786464 | tf_op jit(solution)/shard_map/all_to_all | solution.py:180
  1145.7 162.1 %reduce-scatter.16.cloned.1.call-done = bf16[64,2048]{1,0:T(8,128)(2,1)} async-done(((bf16[2048,2048]{1,0:T(8,128)(2,1)}), bf16[64,2048]{1,0:T(8,128)(2,1)}) %reduce-scatter.16.cloned.1.call-update) | async-done | bytes 262160 | tf_op jit(solution)/shard_map/reduce_scatter | solution.py:344
  1309.6 72.9 %reduce-scatter.12.cloned.1.call-done = bf16[256,2048]{1,0:T(8,128)(2,1)} async-done(((bf16[2048,2048]{1,0:T(8,128)(2,1)}), bf16[256,2048]{1,0:T(8,128)(2,1)}) %reduce-scatter.12.cloned.1.call-update) | async-done | bytes 1048592 | tf_op jit(solution)/shard_map/reduce_scatter | solution.py:314
  1388.4 128.2 %all-reduce.3.cloned.1.call-done = (f32[2048]{0:T(1024)}, f32[2048]{0:T(1024)}, f32[2048]{0:T(1024)}, f32[2048]{0:T(1024)}, f32[2048]{0:T(1024)}, /*index=5*/f32...) async-done(((f32[2048]{0:T(1024)}, f32[2048]{0:T(1024)}, f32[2048]{0:T(1024)}, f32[2048]{0:T(1024)}, f32[2048]{0:T(1024)}, /*index=5*/f32[2048]{0:T(1024)}, ...) | async-done | bytes 98320 | tf_op jit(solution)/shard_map/psum | solution.py:328
  (332 shorter events, 378.2 us)
Async XLA Ops:
  7.2 79.1 %all-gather.12.cloned.1.call-start = ((), (), s32[]{:S(2)}) async-start(), calls=%async_computation.20 | async-start | bytes 3932160 | tf_op jit(solution)/shard_map/all_gather | solution.py:167
  23.8 119.9 %all-gather.10.cloned.1.call-start = ((), (), s32[]{:S(2)}) async-start(), calls=%async_computation.19 | async-start | bytes 9437184 | tf_op jit(solution)/shard_map/all_gather | solution.py:231
  26.6 369.0 %all-gather.14.cloned.1.call-start = ((), (), s32[]{:S(2)}) async-start(), calls=%async_computation.21 | async-start | bytes 8650752 | tf_op jit(solution)/shard_map/all_gather | solution.py:226
  28.4 18.5 %all-to-all-start.4 = ((bf16[64,8,1024]{2,0,1:T(8,128)(2,1)}), bf16[64,8,1024]{2,0,1:T(8,128)(2,1)S(1)}, u32[]{:S(2)}, u32[]{:S(2)}) async-start(bf16[64,8,1024]{2,0,1:T(8,128)(2,1)} %bitcast.167), calls=%async_computation.4 | async-start | bytes 2097152 | tf_op jit(solution)/shard_map/all_to_all | solution.py:160
  46.9 112.6 %all-to-all-start.5 = ((bf16[64,8,1024]{2,0,1:T(8,128)(2,1)}), bf16[64,8,1024]{2,0,1:T(8,128)(2,1)S(1)}, u32[]{:S(2)}, u32[]{:S(2)}) async-start(bf16[64,8,1024]{2,0,1:T(8,128)(2,1)} %bitcast.214), calls=%async_computation.5 | async-start | bytes 2097152 | tf_op jit(solution)/shard_map/all_to_all | solution.py:160
  51.8 355.1 %all-gather.18.cloned.1.call-start = ((), (), s32[]{:S(2)}) async-start(), calls=%async_computation.23 | async-start | bytes 5242880 | tf_op jit(solution)/shard_map/all_gather | solution.py:167
  159.6 102.9 %all-to-all-start.1 = ((bf16[4,512,768]{1,2,0:T(8,128)(2,1)}), bf16[4,512,768]{1,2,0:T(8,128)(2,1)}, u32[]{:S(2)}, u32[]{:S(2)}) async-start(bf16[4,512,768]{1,2,0:T(8,128)(2,1)} %copy.159), calls=%async_computation.1 | async-start | bytes 6291456 | tf_op jit(solution)/shard_map/all_to_all | solution.py:244
  164.6 280.6 %all-gather.20.cloned.1.call-start = ((), (), s32[]{:S(2)}) async-start(), calls=%async_computation.24 | async-start | bytes 5242880 | tf_op jit(solution)/shard_map/all_gather | solution.py:167
  175.2 327.1 %all-gather.16.cloned.1.call-start = ((), (), s32[]{:S(2)}) async-start(), calls=%async_computation.22 | async-start | bytes 9437184 | tf_op jit(solution)/shard_map/all_gather | solution.py:269
  334.6 61.0 %copy-start.43 = (f32[2048]{0:T(1024)S(1)}, f32[2048]{0:T(1024)}, u32[]{:S(2)}) copy-start(f32[2048]{0:T(1024)} %param.28) | copy-start | bytes 24580
  405.2 153.4 %all-gather.22.cloned.1.call-start = ((), (), s32[]{:S(2)}) async-start(), calls=%async_computation.26 | async-start | bytes 9437184 | tf_op jit(solution)/shard_map/all_gather | solution.py:270
  406.0 270.4 %reduce-scatter.10.cloned.1.call-start = ((), (), s32[]{:S(2)}) async-start(), calls=%async_computation.27 | async-start | bytes 9437184 | tf_op jit(solution)/shard_map/reduce_scatter | solution.py:280
  605.4 146.1 %reduce-scatter.8.cloned.1.call-start = ((), (), s32[]{:S(2)}) async-start(), calls=%async_computation.25 | async-start | bytes 9437184 | tf_op jit(solution)/shard_map/reduce_scatter | solution.py:284
  630.4 442.6 %reduce-scatter.18.cloned.1.call-start = ((), (), s32[]{:S(2)}) async-start(), calls=%async_computation.31 | async-start | bytes 5242880 | tf_op jit(solution)/shard_map/reduce_scatter | solution.py:179
  646.0 105.4 %copy-start.20 = (bf16[256,2048]{1,0:T(8,128)(2,1)S(1)}, bf16[256,2048]{1,0:T(8,128)(2,1)}, u32[]{:S(2)}) copy-start(bf16[256,2048]{1,0:T(8,128)(2,1)} %param.37) | copy-start | bytes 3145732
  646.1 105.4 %copy-start.48 = (f32[2048]{0:T(1024)S(1)}, f32[2048]{0:T(1024)}, u32[]{:S(2)}) copy-start(f32[2048]{0:T(1024)} %param.34) | copy-start | bytes 24580
  763.6 18.8 %all-to-all-start.6 = ((bf16[8,256,256]{2,1,0:T(8,128)(2,1)}), bf16[8,256,256]{2,1,0:T(8,128)(2,1)}, u32[]{:S(2)}, u32[]{:S(2)}) async-start(bf16[8,256,256]{2,1,0:T(8,128)(2,1)} %bitcast.165), calls=%async_computation.8 | async-start | bytes 2097152 | tf_op jit(solution)/shard_map/all_to_all | solution.py:293
  782.5 55.0 %all-to-all-start.7 = ((bf16[4,512,256]{2,1,0:T(8,128)(2,1)}), bf16[4,512,256]{2,1,0:T(8,128)(2,1)S(1)}, u32[]{:S(2)}, u32[]{:S(2)}) async-start(bf16[4,512,256]{2,1,0:T(8,128)(2,1)} %bitcast.41), calls=%async_computation.9 | async-start | bytes 2097152 | tf_op jit(solution)/shard_map/all_to_all | solution.py:300
  787.0 292.6 %reduce-scatter.20.cloned.1.call-start = ((), (), s32[]{:S(2)}) async-start(), calls=%async_computation.32 | async-start | bytes 5242880 | tf_op jit(solution)/shard_map/reduce_scatter | solution.py:179
  812.5 305.3 %reduce-scatter.14.cloned.1.call-start = ((), (), s32[]{:S(2)}) async-start(), calls=%async_computation.29 | async-start | bytes 3932160 | tf_op jit(solution)/shard_map/reduce_scatter | solution.py:179
  1054.8 253.0 %reduce-scatter.16.cloned.1.call-start = ((), (), s32[]{:S(2)}) async-start(), calls=%async_computation.30 | async-start | bytes 8650752 | tf_op jit(solution)/shard_map/reduce_scatter | solution.py:344
  1061.4 321.0 %reduce-scatter.12.cloned.1.call-start = ((), (), s32[]{:S(2)}) async-start(), calls=%async_computation.28 | async-start | bytes 9437184 | tf_op jit(solution)/shard_map/reduce_scatter | solution.py:314
  1072.9 20.2 %all-to-all-start.10 = ((bf16[8,64,1024]{2,1,0:T(8,128)(2,1)}), bf16[8,64,1024]{2,1,0:T(8,128)(2,1)S(1)}, u32[]{:S(2)}, u32[]{:S(2)}) async-start(bf16[8,64,1024]{2,1,0:T(8,128)(2,1)} %bitcast.236), calls=%async_computation.16 | async-start | bytes 2097152 | tf_op jit(solution)/shard_map/all_to_all | solution.py:180
  1094.1 18.4 %all-to-all-start.11 = ((bf16[8,64,1024]{2,1,0:T(8,128)(2,1)}), bf16[8,64,1024]{2,1,0:T(8,128)(2,1)S(1)}, u32[]{:S(2)}, u32[]{:S(2)}) async-start(bf16[8,64,1024]{2,1,0:T(8,128)(2,1)} %bitcast.237), calls=%async_computation.18 | async-start | bytes 2097152 | tf_op jit(solution)/shard_map/all_to_all | solution.py:180
  1117.8 25.3 %all-to-all-start.9 = ((bf16[8,64,768]{2,1,0:T(8,128)(2,1)}), bf16[8,64,768]{2,1,0:T(8,128)(2,1)}, u32[]{:S(2)}, u32[]{:S(2)}) async-start(bf16[8,64,768]{2,1,0:T(8,128)(2,1)} %bitcast.242), calls=%async_computation.13 | async-start | bytes 1572864 | tf_op jit(solution)/shard_map/all_to_all | solution.py:180
  1122.7 393.9 %all-reduce.3.cloned.1.call-start = ((), (), s32[]{:S(2)}) async-start(), calls=%async_computation.33 | async-start | bytes 196608 | tf_op jit(solution)/shard_map/psum | solution.py:328
  1124.4 258.0 %copy-start.10 = (bf16[256,2048]{1,0:T(8,128)(2,1)S(1)}, bf16[256,2048]{1,0:T(8,128)(2,1)}, u32[]{:S(2)}) copy-start(bf16[256,2048]{1,0:T(8,128)(2,1)} %param.21) | copy-start | bytes 3145732
  1124.4 258.0 %copy-start.29 = (f32[2048]{0:T(1024)S(1)}, f32[2048]{0:T(1024)}, u32[]{:S(2)}) copy-start(f32[2048]{0:T(1024)} %param.22) | copy-start | bytes 24580
  1124.4 258.0 %copy-start.35 = (f32[256]{0:T(256)S(1)}, f32[256]{0:T(256)}, u32[]{:S(2)}) copy-start(f32[256]{0:T(256)} %copy-done.34) | copy-start | bytes 3076
  1124.4 258.0 %copy-start.39 = (f32[256]{0:T(256)S(1)}, f32[256]{0:T(256)}, u32[]{:S(2)}) copy-start(f32[256]{0:T(256)} %copy-done.38) | copy-start | bytes 3076
  1127.4 257.9 %copy-start.33 = (f32[2048]{0:T(1024)}, f32[2048]{0:T(1024)S(1)}, u32[]{:S(2)}) copy-start(f32[2048]{0:T(1024)S(1)} %dynamic_update_slice.21) | copy-start | bytes 24580
  1127.7 257.6 %copy-start.32 = (f32[2048]{0:T(1024)}, f32[2048]{0:T(1024)S(1)}, u32[]{:S(2)}) copy-start(f32[2048]{0:T(1024)S(1)} %dynamic_update_slice.22) | copy-start | bytes 24580
  (49 other events, 808.8 us)
Sparse Core Ops, SparseCore 0:
  23.9 62.4 all-gather.11
  88.8 54.7 all-gather.9
  146.6 120.7 all-gather.13
  269.4 86.7 all-gather.17
  357.6 87.5 all-gather.19
  447.5 54.7 all-gather.15
  504.2 54.3 all-gather.21
  605.5 70.7 reduce-scatter.9
  680.2 71.2 reduce-scatter.7
  753.6 98.4 reduce-scatter.17
  854.5 77.2 reduce-scatter.19
  1054.9 62.8 reduce-scatter.13
  1120.1 187.6 reduce-scatter.15
  1311.1 71.2 reduce-scatter.11
  1391.0 125.5 all-reduce.2

commit v2 on v1

v2 whole, which is shorter than its diff:
```python
import functools
import jax
import jax.numpy as jnp
from jax import lax
from jax.experimental import pallas as pl
from jax.experimental.pallas import tpu as pltpu
from jax.sharding import Mesh, PartitionSpec as P
HEADS = 16
CONT = 256
PLANE = ('grp', 'sub')
EVERY = ('grp', 'rep', 'sub')
MESH = pl.DeviceIdType.MESH
ANY = pl.BlockSpec(memory_space=pl.ANY)
VMEM = pl.BlockSpec(memory_space=pltpu.VMEM)
DMA = pltpu.SemaphoreType.DMA
MIB = 1 << 20
norm_epsilon = 1e-05
masked_score = -1e+30
log2_e = 1.4426950408889634

def norm_terms(values):
    average = jnp.mean(values, axis=-1, keepdims=True)
    centered = values - average
    variance = jnp.mean(centered * centered, axis=-1, keepdims=True)
    inverse = lax.rsqrt(variance + norm_epsilon)
    return (centered * inverse, inverse)

def norm_back(slope, gain, normal, inverse):
    scaled = slope * gain
    return inverse * (scaled - jnp.mean(scaled, axis=-1, keepdims=True) - normal * jnp.mean(scaled * normal, axis=-1, keepdims=True))

def exact_gelu(values):
    return jax.nn.gelu(values, approximate=False)

def key_bounds(positions, lengths, prompt):
    segment = (positions - prompt) // CONT
    within = positions - prompt - segment * CONT
    slot_ids = jnp.arange(lengths.shape[0], dtype=jnp.int32)
    slot_limit = jnp.sum(jnp.where(segment[:, None] == slot_ids[None, :], lengths[None, :], 0), axis=1)
    last = prompt + (segment + 1) * CONT - 1
    last = jnp.where(within < slot_limit, last, -1)
    return jnp.where(positions < prompt, positions.shape[0], last)

def product(left_matrix, right_matrix):
    return jnp.dot(left_matrix, right_matrix, preferred_element_type=jnp.float32)

def product_transposed(left_matrix, right_matrix):
    return lax.dot_general(left_matrix, right_matrix, (((1,), (1,)), ((), ())), preferred_element_type=jnp.float32)

def row_outer(left_matrix, right_matrix):
    return lax.dot_general(left_matrix, right_matrix, (((0,), (0,)), ((), ())), preferred_element_type=jnp.float32)

def attention_forward(packed, places, key_last, heads):
    rows, columns = packed.shape
    size = columns // (3 * heads)
    block = 256
    factor = size ** (-0.5) * log2_e

    def kernel(q_ref, k_ref, v_ref, place_ref, first_ref, last_ref, out_ref, total_ref):
        scores = product_transposed(q_ref[...], k_ref[...])
        place = place_ref[...]
        allowed = (first_ref[...] <= place) & (place <= last_ref[...])
        scores = jnp.where(allowed, scores * factor, masked_score)
        top = jnp.max(scores, axis=1, keepdims=True)
        soft = jnp.exp2(scores - top)
        total = jnp.sum(soft, axis=1, keepdims=True)
        mixture = product(soft.astype(jnp.bfloat16), v_ref[...])
        out_ref[...] = (mixture / total).astype(jnp.bfloat16)
        log_total = jnp.broadcast_to(top + jnp.log2(total), (block, 128))
        total_ref[0] = log_total.T[:8]
    return pl.pallas_call(kernel, grid=(heads, rows // block), in_specs=[pl.BlockSpec((block, size), lambda h, i: (i, 3 * h)), pl.BlockSpec((rows, size), lambda h, i: (0, 3 * h + 1)), pl.BlockSpec((rows, size), lambda h, i: (0, 3 * h + 2)), pl.BlockSpec((block, 1), lambda h, i: (i, 0)), pl.BlockSpec((1, rows), lambda h, i: (0, 0)), pl.BlockSpec((1, rows), lambda h, i: (0, 0))], out_specs=[pl.BlockSpec((block, size), lambda h, i: (i, h)), pl.BlockSpec((1, 8, block), lambda h, i: (h, 0, i))], out_shape=[jax.ShapeDtypeStruct((rows, heads * size), jnp.bfloat16), jax.ShapeDtypeStruct((heads, 8, rows), jnp.float32)], compiler_params=pltpu.CompilerParams(vmem_limit_bytes=56 * MIB), cost_estimate=pl.CostEstimate(flops=4 * heads * rows * rows * size, bytes_accessed=4 * rows * heads * size * 2, transcendentals=heads * rows * rows), name='attention_forward')(packed, packed, packed, places[:, None], places[None, :], key_last[None, :])

def attention_backward(packed, totals, slopes, places, key_last, heads):
    rows, columns = packed.shape
    size = columns // (3 * heads)
    block = 256
    scale = size ** (-0.5)
    factor = scale * log2_e

    def kernel(q_ref, k_ref, v_ref, slope_ref, total_ref, place_ref, first_ref, last_ref, out_ref, turned_ref, key_sum, value_sum):
        step = pl.program_id(1)

        @pl.when(step == 0)
        def _():
            turned_ref[...] = k_ref[...].T
            key_sum[...] = jnp.zeros_like(key_sum)
            value_sum[...] = jnp.zeros_like(value_sum)
        queries = q_ref[...]
        slope = slope_ref[...]
        scores = product_transposed(k_ref[...], queries)
        place = place_ref[...]
        allowed = (first_ref[...] <= place) & (place <= last_ref[...])
        soft = jnp.where(allowed, jnp.exp2(scores * factor - total_ref[0, :1]), 0.0)
        weight_slope = product_transposed(v_ref[...], slope)
        centre = jnp.sum(soft * weight_slope, axis=0, keepdims=True)
        score_slope = (soft * (weight_slope - centre)).astype(jnp.bfloat16)
        value_sum[...] += product(soft.astype(jnp.bfloat16), slope)
        key_sum[...] += product(score_slope, queries)
        query_slope = product(turned_ref[...], score_slope)
        here = pl.ds(pl.multiple_of(step * block, block), block)
        out_ref[here, :size] = (query_slope.T * scale).astype(jnp.bfloat16)

        @pl.when(step == pl.num_programs(1) - 1)
        def _():
            out_ref[:, size:2 * size] = (key_sum[...] * scale).astype(jnp.bfloat16)
            out_ref[:, 2 * size:] = value_sum[...].astype(jnp.bfloat16)
    return pl.pallas_call(kernel, grid=(heads, rows // block), in_specs=[pl.BlockSpec((block, size), lambda h, i: (i, 3 * h)), pl.BlockSpec((rows, size), lambda h, i: (0, 3 * h + 1)), pl.BlockSpec((rows, size), lambda h, i: (0, 3 * h + 2)), pl.BlockSpec((block, size), lambda h, i: (i, h)), pl.BlockSpec((1, 8, block), lambda h, i: (h, 0, i)), pl.BlockSpec((1, block), lambda h, i: (0, i)), pl.BlockSpec((rows, 1), lambda h, i: (0, 0)), pl.BlockSpec((rows, 1), lambda h, i: (0, 0))], out_specs=pl.BlockSpec((rows, 3 * size), lambda h, i: (0, h)), out_shape=jax.ShapeDtypeStruct((rows, columns), jnp.bfloat16), scratch_shapes=[pltpu.VMEM((size, rows), jnp.bfloat16), pltpu.VMEM((rows, size), jnp.float32), pltpu.VMEM((rows, size), jnp.float32)], compiler_params=pltpu.CompilerParams(vmem_limit_bytes=56 * MIB), cost_estimate=pl.CostEstimate(flops=10 * heads * rows * rows * size, bytes_accessed=8 * rows * heads * size * 2, transcendentals=heads * rows * rows), name='attention_backward')(packed, packed, packed, slopes, totals, places[None, :], places[:, None], key_last[:, None])

def small_plane():
    return (lax.axis_size('grp'), lax.axis_size('sub')) == (4, 2)

def plane_ids():
    g, r, u = (lax.axis_index(n) for n in ('grp', 'rep', 'sub'))
    y, c = (g // 2, g % 2)
    across, up, partner = ((g, r, 1 - u), ((1 - y) * 2 + c, r, u), (y * 2 + 1 - c, r, u))

    def piece(k):
        return ((1 - y if k & 4 else y) * 2 + (1 - c if k & 2 else c)) * 2 + (1 - u if k & 1 else u)
    return (across, up, partner, piece)

def greet(devices):
    barrier = pltpu.get_barrier_semaphore()
    for device in devices:
        pl.semaphore_signal(barrier, inc=1, device_id=device, device_id_type=MESH)
    pl.semaphore_wait(barrier, len(devices))

def remote(source, target, send, recv, number, device):
    return pltpu.make_async_remote_copy(src_ref=source, dst_ref=target, send_sem=send.at[number], recv_sem=recv.at[number], device_id=device, device_id_type=MESH)

def gather_pieces(slots, send, recv, ids, on_piece):
    across, up, partner, _ = ids
    half = slots.shape[1] // 2
    low, high = (pl.ds(0, half), pl.ds(half, half))

    def copy(number, source, target, device):
        return remote(slots.at[source], slots.at[target], send, recv, number, device)
    x0 = copy(0, (0, low), (1, low), across)
    y1 = copy(1, (0, high), (4, high), up)
    x1 = copy(2, (0, high), (1, high), across)
    y0 = copy(3, (0, low), (4, low), up)
    own = copy(4, 0, 2, partner)
    started = [x0, y1, own, x1, y0]
    for one in started:
        one.start()
    on_piece(0)
    own.wait_recv()
    on_piece(2)

    def forward(number, source, target, device):
        one = copy(number, source, target, device)
        one.start()
        started.append(one)
        return one
    x0.wait_recv()
    d0 = forward(5, (1, low), (5, low), up)
    y1.wait_recv()
    d1 = forward(6, (4, high), (5, high), across)
    x1.wait_recv()
    px = forward(7, 1, 3, partner)
    on_piece(1)
    y0.wait_recv()
    py = forward(8, 4, 6, partner)
    on_piece(4)
    px.wait_recv()
    on_piece(3)
    py.wait_recv()
    on_piece(6)
    d0.wait_recv()
    p0 = forward(9, (5, low), (7, low), partner)
    d1.wait_recv()
    p1 = forward(10, (5, high), (7, high), partner)
    on_piece(5)
    p0.wait_recv()
    p1.wait_recv()
    on_piece(7)
    for one in started:
        one.wait_send()

def gather_kernel(parts, x_ref, out_ref, slots, load, send, recv, store):
    ids = plane_ids()
    first = pltpu.make_async_copy(x_ref, slots.at[0], load)
    first.start()
    greet(ids[:3])
    first.wait()
    stores = []
    small = slots.shape[1] // parts

    def on_piece(k):
        piece = ids[3](k)
        for part in range(parts):
            one = pltpu.make_async_copy(slots.at[k, pl.ds(part * small, small)], out_ref.at[piece // 2, part, lax.rem(piece, 2)], store.at[k, part])
            one.start()
            stores.append(one)
    gather_pieces(slots, send, recv, ids, on_piece)
    for one in stores:
        one.wait()

def plane_gather(x, collective_id, parts=1):
    rows, width = x.shape
    groups, _, subs = (lax.axis_size(n) for n in EVERY)
    if not small_plane():
        every = lax.all_gather(x, PLANE, axis=0).reshape(groups, subs, parts, rows // parts, width)
        return every.transpose(0, 2, 1, 3, 4).reshape(-1, width)
    return pl.pallas_call(functools.partial(gather_kernel, parts), out_shape=jax.ShapeDtypeStruct((groups, parts, subs, rows // parts, width), x.dtype), in_specs=[ANY], out_specs=ANY, scratch_shapes=[pltpu.VMEM((8, rows, width), x.dtype), DMA, DMA((11,)), DMA((11,)), DMA((8, parts))], compiler_params=pltpu.CompilerParams(collective_id=collective_id, has_side_effects=True, vmem_limit_bytes=40 * MIB), name='plane_gather')(x).reshape(-1, width)

def reduce_scratch(rows, width):
    f, h = (jnp.float32, jnp.bfloat16)
    return [pltpu.VMEM((4, rows, width), f), pltpu.VMEM((4, rows, width), h), pltpu.VMEM((4, rows, width), h), pltpu.VMEM((3, rows, width), h), pltpu.VMEM((3, rows, width), h), DMA((10,)), DMA((10,))]
SUM = {0: 0, 1: 1, 4: 2, 5: 3}

def reduce_pieces(refs, ids, make_piece, out):
    sums, give, take, leave, come, send, recv = refs
    across, up, partner, _ = ids
    half = sums.shape[1] // 2
    low, high = (pl.ds(0, half), pl.ds(half, half))
    started = []

    def start(number, source, target, device):
        one = remote(source, target, send, recv, number, device)
        one.start()
        started.append(one)
        return one

    def pair(k, number):
        give[SUM[k]] = make_piece(k + 2).astype(jnp.bfloat16)
        one = start(number, give.at[SUM[k]], take.at[SUM[k]], partner)
        sums[SUM[k]] = make_piece(k)
        return one

    def settle(k, one):
        one.wait_recv()
        sums[SUM[k]] += take[SUM[k]].astype(jnp.float32)
    settle(5, pair(5, 0))
    leave[2] = sums[3].astype(jnp.bfloat16)
    dx = start(4, leave.at[2, low], come.at[2, low], across)
    dy = start(5, leave.at[2, high], come.at[2, high], up)
    settle(1, pair(1, 1))
    leave[0, low] = sums[1, low].astype(jnp.bfloat16)
    xl = start(6, leave.at[0, low], come.at[0, low], across)
    settle(4, pair(4, 2))
    leave[1, high] = sums[2, high].astype(jnp.bfloat16)
    yh = start(7, leave.at[1, high], come.at[1, high], up)
    last = pair(0, 3)
    dy.wait_recv()
    leave[0, high] = (sums[1, high] + come[2, high].astype(jnp.float32)).astype(jnp.bfloat16)
    xh = start(8, leave.at[0, high], come.at[0, high], across)
    dx.wait_recv()
    leave[1, low] = (sums[2, low] + come[2, low].astype(jnp.float32)).astype(jnp.bfloat16)
    yl = start(9, leave.at[1, low], come.at[1, low], up)
    settle(0, last)
    for one in (xl, yh, xh, yl):
        one.wait_recv()
    out[...] = sums[0] + come[0].astype(jnp.float32) + come[1].astype(jnp.float32)
    for one in started:
        one.wait_send()

def product_reduce_kernel(slope_ref, weight_ref, out_ref, slopes, load, *refs):
    ids = plane_ids()
    order = (7, 5, 3, 1, 6, 4, 2, 0)
    loads = {k: pltpu.make_async_copy(slope_ref.at[ids[3](k)], slopes.at[k], load.at[k]) for k in order}
    for k in order:
        loads[k].start()
    greet(ids[:3])

    def make_piece(k):
        loads[k].wait()
        return lax.dot_general(slopes[k], weight_ref[...], (((1,), (1,)), ((), ())), preferred_element_type=jnp.float32)
    reduce_pieces(refs, ids, make_piece, out_ref)

def product_reduce(slopes, weight, collective_id):
    if not small_plane():
        part = product_transposed(slopes.reshape(-1, slopes.shape[2]), weight)
        return lax.psum_scatter(part.astype(jnp.bfloat16), PLANE, scatter_dimension=0, tiled=True).astype(jnp.float32)
    count, rows, inner = slopes.shape
    width = weight.shape[0]
    return pl.pallas_call(product_reduce_kernel, out_shape=jax.ShapeDtypeStruct((rows, width), jnp.float32), in_specs=[ANY, VMEM], out_specs=VMEM, scratch_shapes=[pltpu.VMEM((8, rows, inner), slopes.dtype), DMA((8,)), *reduce_scratch(rows, width)], compiler_params=pltpu.CompilerParams(collective_id=collective_id, has_side_effects=True, vmem_limit_bytes=60 << 20), name='product_reduce')(slopes, weight)

def total_kernel(x_ref, out_ref, *refs):
    axes = ('grp', 'rep', 'sub')
    here = {n: lax.axis_index(n) for n in axes}
    phases = ('grp', 'sub', 'rep')

    def other(name, step):
        size = lax.axis_size(name)
        return tuple((lax.rem(here[n] + step, size) if n == name else here[n] for n in axes))
    greet([other(n, s) for n in phases for s in range(1, lax.axis_size(n))])
    out_ref[...] = x_ref[...]
    for j, name in enumerate(phases):
        slots, send, recv = refs[3 * j:3 * j + 3]
        size = lax.axis_size(name)
        me = here[name]
        slots[me] = out_ref[...]
        copies = []
        for s in range(1, size):
            one = pltpu.make_async_remote_copy(src_ref=out_ref, dst_ref=slots.at[me], send_sem=send.at[s], recv_sem=recv.at[s], device_id=other(name, s), device_id_type=MESH)
            one.start()
            copies.append(one)
        for one in copies:
            one.wait_recv()
        for one in copies:
            one.wait_send()
        value = slots[0]
        for s in range(1, size):
            value = value + slots[s]
        out_ref[...] = value

def total_everywhere(x, collective_id):
    scratch = []
    for name in ('grp', 'sub', 'rep'):
        n = lax.axis_size(name)
        scratch += [pltpu.VMEM((n,) + x.shape, x.dtype), DMA((n,)), DMA((n,))]
    return pl.pallas_call(total_kernel, out_shape=jax.ShapeDtypeStruct(x.shape, x.dtype), in_specs=[VMEM], out_specs=VMEM, scratch_shapes=scratch, compiler_params=pltpu.CompilerParams(collective_id=collective_id, has_side_effects=True), name='total_everywhere')(x)

def exchange_kernel(to_tokens, x_ref, out_ref, send, recv, local):
    groups, reps, subs = (lax.axis_size(n) for n in EVERY)
    g, r, u = (lax.axis_index(n) for n in EVERY)
    count = groups * subs
    place = g * subs + u
    if to_tokens:
        tokens, width = (out_ref.shape[0], x_ref.shape[1])
    else:
        tokens, width = (x_ref.shape[0], out_ref.shape[1])

    def rows(ref, t):
        return ref.at[pl.ds(pl.multiple_of(t * tokens, tokens), tokens), :]

    def columns(ref, t):
        return ref.at[:, pl.ds(pl.multiple_of(t * width, width), width)]
    source, target = (rows, columns) if to_tokens else (columns, rows)
    peers = [lax.rem(place + step, count) for step in range(1, count)]

    def device(t):
        return (t // subs, r, lax.rem(t, subs))
    own = pltpu.make_async_copy(source(x_ref, place), target(out_ref, place), local)
    own.start()
    greet([device(t) for t in peers])
    copies = []
    for step, t in enumerate(peers):
        one = pltpu.make_async_remote_copy(src_ref=source(x_ref, t), dst_ref=target(out_ref, place), send_sem=send.at[step], recv_sem=recv.at[step], device_id=device(t), device_id_type=MESH)
        one.start()
        copies.append(one)
    own.wait()
    for one in copies:
        one.wait_recv()
    for one in copies:
        one.wait_send()

def exchange(x, to_tokens, collective_id):
    count = lax.axis_size('grp') * lax.axis_size('sub')
    shape = (x.shape[0] // count, x.shape[1] * count) if to_tokens else (x.shape[0] * count, x.shape[1] // count)
    return pl.pallas_call(functools.partial(exchange_kernel, to_tokens), out_shape=jax.ShapeDtypeStruct(shape, x.dtype), in_specs=[ANY], out_specs=ANY, scratch_shapes=[DMA((count - 1,)), DMA((count - 1,)), DMA], compiler_params=pltpu.CompilerParams(collective_id=collective_id, has_side_effects=True), name='to_tokens' if to_tokens else 'to_heads')(x)

def outer_reduce_kernel(left_ref, right_ref, out_ref, *refs):
    ids = plane_ids()
    greet(ids[:3])
    wide = left_ref.shape[1] // 8

    def make_piece(k):
        block = left_ref[:, pl.ds(pl.multiple_of(ids[3](k) * wide, wide), wide)]
        return row_outer(block, right_ref[...])
    reduce_pieces(refs, ids, make_piece, out_ref)

def outer_reduce(left, right, collective_id):
    if not small_plane():
        return lax.psum_scatter(row_outer(left, right).astype(jnp.bfloat16), PLANE, scatter_dimension=0, tiled=True).astype(jnp.float32)
    rows, width = (left.shape[1] // 8, right.shape[1])
    return pl.pallas_call(outer_reduce_kernel, out_shape=jax.ShapeDtypeStruct((rows, width), jnp.float32), in_specs=[VMEM, VMEM], out_specs=VMEM, scratch_shapes=reduce_scratch(rows, width), compiler_params=pltpu.CompilerParams(collective_id=collective_id, has_side_effects=True, vmem_limit_bytes=60 * MIB), name='outer_reduce')(left, right)

def plane_of(group):
    groups = lax.axis_size('grp')
    return lax.rem(group, 2) * (groups // 2) + group // 2

def group_of(plane):
    groups = lax.axis_size('grp')
    return lax.rem(plane, groups // 2) * 2 + plane // (groups // 2)

def opening_kernel(x_ref, w_ref, moved_ref, columns_ref, move_send, move_recv, send, recv, local):
    groups, reps, subs = (lax.axis_size(n) for n in EVERY)
    g, r, u = (lax.axis_index(n) for n in EVERY)
    count = groups * subs
    place = g * subs + u
    rows, width = (w_ref.shape[0], columns_ref.shape[1])
    peers = [lax.rem(place + step, count) for step in range(1, count)]

    def device(t):
        return (t // subs, r, lax.rem(t, subs))
    target, source = ((r, plane_of(g), u), (group_of(r), g, u))
    stays = (r == g) & (plane_of(g) == r)

    def block(t):
        return w_ref.at[:, pl.ds(pl.multiple_of(t * width, width), width)]
    landing = columns_ref.at[pl.ds(pl.multiple_of(place * rows, rows), rows), :]
    own = pltpu.make_async_copy(block(place), landing, local.at[0])
    own.start()
    kept = pltpu.make_async_copy(x_ref, moved_ref, local.at[1])
    moved = pltpu.make_async_remote_copy(src_ref=x_ref, dst_ref=moved_ref, send_sem=move_send, recv_sem=move_recv, device_id=target, device_id_type=MESH)
    barrier = pltpu.get_barrier_semaphore()
    for t in peers:
        pl.semaphore_signal(barrier, inc=1, device_id=device(t), device_id_type=MESH)

    @pl.when(stays)
    def _():
        kept.start()

    @pl.when(jnp.logical_not(stays))
    def _():
        pl.semaphore_signal(barrier, inc=1, device_id=source, device_id_type=MESH)
    pl.semaphore_wait(barrier, count - stays.astype(jnp.int32))

    @pl.when(jnp.logical_not(stays))
    def _():
        moved.start()
    copies = []
    for step, t in enumerate(peers):
        one = pltpu.make_async_remote_copy(src_ref=block(t), dst_ref=landing, send_sem=send.at[step], recv_sem=recv.at[step], device_id=device(t), device_id_type=MESH)
        one.start()
        copies.append(one)
    own.wait()
    for one in copies:
        one.wait_recv()
    for one in copies:
        one.wait_send()

    @pl.when(stays)
    def _():
        kept.wait()

    @pl.when(jnp.logical_not(stays))
    def _():
        moved.wait_recv()
        moved.wait_send()

def opening(x, weight, collective_id):
    count = lax.axis_size('grp') * lax.axis_size('sub')
    columns = jax.ShapeDtypeStruct((weight.shape[0] * count, weight.shape[1] // count), weight.dtype)
    return pl.pallas_call(opening_kernel, out_shape=[jax.ShapeDtypeStruct(x.shape, x.dtype), columns], in_specs=[VMEM, ANY], out_specs=[VMEM, ANY], scratch_shapes=[DMA, DMA, DMA((count - 1,)), DMA((count - 1,)), DMA((2,))], compiler_params=pltpu.CompilerParams(collective_id=collective_id, has_side_effects=True), name='opening')(x, weight)

def rep_rows(own):
    groups, reps, subs = (lax.axis_size(name) for name in EVERY)
    every = lax.all_gather(own, 'rep', axis=0, tiled=True)
    every = every.reshape(reps, groups, subs, -1, own.shape[1]).transpose(1, 0, 2, 3, 4)
    return every.reshape(-1, own.shape[1])

def rep_sums(gradient):
    groups, reps, subs = (lax.axis_size(name) for name in EVERY)
    columns = gradient.shape[1]
    ordered = gradient.astype(jnp.bfloat16).reshape(groups, reps, subs, -1, columns)
    ordered = ordered.transpose(1, 0, 2, 3, 4).reshape(-1, columns)
    return lax.psum_scatter(ordered, 'rep', scatter_dimension=0, tiled=True)

def shards(layer_input, entry_gain, entry_shift, joint_weight, query_offset, value_offset, mixing_weight, attention_offset, middle_gain, middle_shift, expand_weight, expand_offset, shrink_weight, shrink_offset, placement, slot_lengths, cotangent):
    token_rows, width = layer_input.shape
    hidden_width = expand_weight.shape[1]
    groups, reps, subs = (lax.axis_size(name) for name in EVERY)
    plane_count = groups * subs
    plane_index = lax.axis_index(PLANE)
    head_size = width // HEADS
    local_heads = HEADS // plane_count
    head_columns = local_heads * head_size
    plane_rows = plane_count * token_rows
    home = [g * reps * subs + r * subs + u for g in range(groups) for r in range(reps) for u in range(subs)]
    away = [(r * reps + g % 2 * (groups // 2) + g // 2) * subs + u for g in range(groups) for r in range(reps) for u in range(subs)]

    def to_plane(array):
        return lax.ppermute(array, EVERY, list(zip(home, away)))

    def from_plane(array):
        return lax.ppermute(array, EVERY, list(zip(away, home)))
    facts = to_plane(jnp.concatenate([placement, slot_lengths], axis=1))[0]
    mixing_own = lax.all_gather(mixing_weight, 'rep', axis=0, tiled=True)
    moved_input, joint_own = opening(layer_input, joint_weight, 12)
    input_float = moved_input.astype(jnp.float32)
    joint_slice = rep_rows(joint_own)
    entry_normal, entry_inverse = norm_terms(input_float)
    entry_normed = (entry_normal * entry_gain + entry_shift).astype(jnp.bfloat16)
    entry_all = plane_gather(entry_normed, 1)
    expand_weight, shrink_weight, cotangent, facts, entry_all = lax.optimization_barrier((expand_weight, shrink_weight, cotangent, facts, entry_all))
    places, lengths = (facts[:placement.shape[1]], facts[placement.shape[1]:])
    prompt = places.shape[0] // 2
    key_last = key_bounds(places, lengths, prompt)
    expand_slice = rep_rows(exchange(expand_weight, False, 13))
    shrink_own = exchange(shrink_weight, False, 14)
    shrink_slice = rep_rows(shrink_own)
    cotangent, shrink_own = lax.optimization_barrier((cotangent, shrink_own))
    cotangent = to_plane(cotangent)
    offsets = jnp.stack([query_offset.reshape(HEADS, head_size), jnp.zeros((HEADS, head_size), jnp.float32), value_offset.reshape(HEADS, head_size)], axis=1).reshape(-1)
    offsets = lax.dynamic_slice_in_dim(offsets, plane_index * 3 * head_columns, 3 * head_columns)
    heads_kept = (product(entry_all, joint_slice) + offsets).astype(jnp.bfloat16)
    mixture, log_totals = attention_forward(heads_kept, places, key_last, local_heads)
    attended = exchange(mixture, True, 3)
    mixing_own, cotangent, attended = lax.optimization_barrier((mixing_own, cotangent, attended))
    mixing_whole = plane_gather(mixing_own, 2, reps)
    residual = input_float + (product(attended, mixing_whole) + attention_offset)
    middle_normal, middle_inverse = norm_terms(residual)
    middle_normed = (middle_normal * middle_gain + middle_shift).astype(jnp.bfloat16)
    middle_all = plane_gather(middle_normed, 5)
    cotangent, middle_all = lax.optimization_barrier((cotangent, middle_all))
    cotangent_all = plane_gather(cotangent, 4)
    hidden_local = hidden_width // plane_count
    offset_local = lax.dynamic_slice_in_dim(expand_offset, plane_index * hidden_local, hidden_local)
    expanded = product(middle_all, expand_slice) + offset_local
    activated_float, gelu_back = jax.vjp(exact_gelu, expanded)
    activated = activated_float.astype(jnp.bfloat16)
    shrink_part = row_outer(cotangent_all, activated).astype(jnp.bfloat16)
    shrink_part, cotangent_all = lax.optimization_barrier((shrink_part, cotangent_all))
    shrink_sums = rep_sums(shrink_part)
    activated_slope = product(cotangent_all, shrink_slice)
    expanded_slope = gelu_back(activated_slope)[0].astype(jnp.bfloat16)
    normed_slope = product_reduce(expanded_slope.reshape(plane_count, token_rows, hidden_local), expand_slice, 6)
    normed_slope, middle_all = lax.optimization_barrier((normed_slope, middle_all))
    expand_part = row_outer(middle_all, expanded_slope).astype(jnp.bfloat16)
    expand_part, normed_slope = lax.optimization_barrier((expand_part, normed_slope))
    expand_sums = rep_sums(expand_part)
    cotangent_float = cotangent.astype(jnp.float32)
    residual_slope = cotangent_float + norm_back(normed_slope, middle_gain, middle_normal, middle_inverse)
    branch_slope = residual_slope.astype(jnp.bfloat16)
    attended_slope = product_transposed(branch_slope, mixing_whole).astype(jnp.bfloat16)
    head_slopes = exchange(attended_slope, False, 7)
    joint_slope = attention_backward(heads_kept, log_totals, head_slopes, places, key_last, local_heads)
    shrink_sums, joint_slope = lax.optimization_barrier((shrink_sums, joint_slope))
    joint_part = row_outer(entry_all, joint_slope).astype(jnp.bfloat16)
    joint_part, joint_slope = lax.optimization_barrier((joint_part, joint_slope))
    joint_sums = rep_sums(joint_part)
    entry_slope = product_reduce(joint_slope.reshape(plane_count, token_rows, 3 * head_columns), joint_slice, 9)
    expand_sums, entry_slope = lax.optimization_barrier((expand_sums, entry_slope))
    input_gradient = from_plane((residual_slope + norm_back(entry_slope, entry_gain, entry_normal, entry_inverse)).astype(jnp.bfloat16))
    activated, attended, entry_slope = lax.optimization_barrier((activated, attended, entry_slope))
    shrunk = product_reduce(activated.reshape(plane_count, token_rows, hidden_local), shrink_slice, 8)
    joint_sums, shrunk = lax.optimization_barrier((joint_sums, shrunk))
    layer_output = from_plane((residual + shrunk + shrink_offset).astype(jnp.bfloat16))
    attended_by_sub = attended.reshape(token_rows, groups, reps, subs, -1).transpose(0, 1, 3, 2, 4)
    mixing_sums = outer_reduce(attended_by_sub.reshape(token_rows, width), branch_slope, 11)
    mixing_gradient = lax.psum_scatter(mixing_sums.astype(jnp.bfloat16), 'rep', scatter_dimension=0, tiled=True).astype(jnp.float32)
    slope_sums = jnp.sum(joint_slope.astype(jnp.float32), axis=0).reshape(local_heads, 3, head_size)

    def placed(piece, whole_size):
        return lax.dynamic_update_slice_in_dim(jnp.zeros((whole_size,), jnp.float32), piece, plane_index * piece.shape[0], 0)
    small = [jnp.sum(entry_slope * entry_normal, axis=0), jnp.sum(entry_slope, axis=0), placed(slope_sums[:, 0].reshape(-1), width), placed(slope_sums[:, 2].reshape(-1), width), jnp.sum(branch_slope.astype(jnp.float32), axis=0), jnp.sum(normed_slope * middle_normal, axis=0), jnp.sum(normed_slope, axis=0), placed(jnp.sum(expanded_slope.astype(jnp.float32), axis=0), hidden_width), jnp.sum(cotangent_float, axis=0)]
    small_all = total_everywhere(jnp.concatenate(small).reshape(-1, 128), 10).reshape(-1)
    small_sums, first = ([], 0)
    for piece in small:
        small_sums.append(small_all[first:first + piece.shape[0]])
        first += piece.shape[0]
    shrink_gradient = exchange(shrink_sums, True, 15).astype(jnp.float32)
    expand_gradient = exchange(expand_sums, True, 16).astype(jnp.float32)
    joint_gradient = exchange(joint_sums, True, 17).astype(jnp.float32)
    return (layer_output, input_gradient, small_sums[0], small_sums[1], joint_gradient, small_sums[2], small_sums[3], mixing_gradient, small_sums[4], small_sums[5], small_sums[6], expand_gradient, small_sums[7], shrink_gradient, small_sums[8])

def solution(mesh):
    groups, sequence = (mesh.shape['grp'], mesh.shape['seq'])
    subs = sequence // groups
    planes = Mesh(mesh.devices.reshape(groups, sequence // subs, subs), EVERY)
    rows, whole, group_rows = (P(EVERY, None), P(), P('grp', None))
    return jax.shard_map(shards, mesh=planes, in_specs=(rows, whole, whole, rows, whole, whole, rows, whole, whole, whole, rows, whole, rows) + (whole, group_rows, group_rows, rows), out_specs=(rows, rows, whole, whole, rows, whole, whole, rows, whole, whole, whole, rows, whole) + (rows, whole), check_vma=False)
```

time: 1540 us -> 847 us (0.55)
  waiting for transfers between devices: 865 us -> 0.94 us
  Pallas kernels: 0 us -> 620 us
  blocking collectives: 156 us -> 0 us
  matrix products: 255 us -> 107 us
  local copies, waits for them, and re-layouts: 124 us -> 45.2 us
  other arithmetic: 72.9 us -> 35.1 us
  starting transfers between devices: 41.9 us -> 15.3 us
    pallas_call x0 -> x19, Pallas kernels: none -> 620 us  [the longest x4 162 us: plane_gather(): pl.pallas_call(functools.partial(gather_kernel, parts), out_shape=jax.Sha...]
    reduce_scatter x7 -> x4, waiting for transfers between devices: 343 us -> 0.06 us  [the longest x3 0.04 us: rep_sums(): return lax.psum_scatter(ordered, 'rep', scatter_dimension=0, tiled=True)]
    all_gather x7 -> x4, waiting for transfers between devices: 215 us -> 0.06 us  [the longest x3 0.04 us: rep_rows(): every = lax.all_gather(own, 'rep', axis=0, tiled=True)]
    all_to_all x8 -> x0, waiting for transfers between devices: 177 us -> none  [the longest x1 87.1 us: shards(): lax.all_to_all(joint_values.reshape(groups, plane_rows // groups, 3 * hea...]
    all_to_all x4 -> x0, blocking collectives: 145 us -> none  [the longest x2 111 us: to_tokens(): lax.all_to_all(array.reshape(reps, plane_rows // reps, columns), 'rep', s...]
    psum x1 -> x0, waiting for transfers between devices: 128 us -> none  [shards(): lax.psum((jnp.sum(entry_slope * entry_normal, axis=0), jnp.sum(entry_slop...]
    dot_general x28 -> x0, matrix products: 104 us -> none  [the longest x4 20.7 us: one_block(): jnp.einsum('hqk,qhe->khe', score_slope, block_queries, preferred_element_...]
    all_to_all x8 -> x0, starting transfers between devices: 41.1 us -> none  [the longest x3 16.4 us: owner_rows(): lax.all_to_all(summed.reshape(plane_count, rows, columns), PLANE, split_a...]
  transfers between devices with their start and end apart: 23 -> 12, of which waited for: 18 -> 0; matrix products, arithmetic and copies ran while one was open for 25% -> 20% of each run, Pallas kernels for 0% -> 70%
where the time goes in v2:
time: 847 us; the launch traced here: 839 us
  Pallas kernels  620 us (73%)
  matrix products  107 us (13%)
  local copies, waits for them, and re-layouts  45.2 us (5%)
  other arithmetic  35.1 us (4%)
  starting transfers between devices  15.3 us (2%)
  between operations  15.2 us (2%)
    pallas_call x4, Pallas kernels, plane_gather(): pl.pallas_call(functools.partial(gather_kernel, parts), out_shape=jax.Sha...  162 us
    pallas_call x3, Pallas kernels, product_reduce(): pl.pallas_call(product_reduce_kernel, out_shape=jax.ShapeDtypeStruct((row...  133 us
    pallas_call x7, Pallas kernels, exchange(): pl.pallas_call(functools.partial(exchange_kernel, to_tokens), out_shape=j...  107 us
    pallas_call x1, Pallas kernels, total_everywhere(): pl.pallas_call(total_kernel, out_shape=jax.ShapeDtypeStruct(x.shape, x.dt...  68.2 us
    dot_general x4, matrix products, product(): jnp.dot(left_matrix, right_matrix, preferred_element_type=jnp.float32)  67 us
    pallas_call x1, Pallas kernels, outer_reduce(): pl.pallas_call(outer_reduce_kernel, out_shape=jax.ShapeDtypeStruct((rows,...  49.7 us
    pallas_call x1, Pallas kernels, attention_backward(): pl.pallas_call(kernel, grid=(heads, rows // block), in_specs=[pl.BlockSpe...  40.9 us
    pallas_call x1, Pallas kernels, opening(): pl.pallas_call(opening_kernel, out_shape=[jax.ShapeDtypeStruct(x.shape, x...  35.8 us
  transfers between devices with their start and end apart: 12, of which 0 were waited for; matrix products, arithmetic and copies ran while one was open for 20% of the time, Pallas kernels for 70%

profile of v2, /device:TPU:19, one launch (start us, length us, event | category | flops | bytes accessed | tf_op | source)
XLA Modules:
  0.0 839.0 jit_solution(13294196184664787426)
XLA Ops:
  7.2 35.8 %opening.1 = (bf16[256,2048]{1,0:T(8,128)(2,1)}, bf16[512,768]{1,0:T(8,128)(2,1)}) custom-call(bf16[256,2048]{1,0:T(8,128)(2,1)} %x_ref.1, bf16[64,6144]{1,0:T(8,128)(2,1)} %w_ref.1), custom_call_target="tpu_custom_call" | custom-call | tf_op jit(solution)/shard_map/opening/pallas_call | solution.py:436
  44.5 3.3 collective-permute-start
  53.3 43.3 %plane_gather.4 = bf16[4,1,2,256,2048]{4,3,2,1,0:T(8,128)(2,1)S(1)} custom-call(bf16[256,2048]{1,0:T(8,128)(2,1)S(1)} %fusion.13.x_ref), custom_call_target="tpu_custom_call" | custom-call | tf_op jit(solution)/shard_map/plane_gather/pallas_call | solution.py:204
  99.9 15.2 %to_heads.4 = bf16[512,1024]{1,0:T(8,128)(2,1)} custom-call(bf16[64,8192]{1,0:T(8,128)(2,1)} %x_ref.3), custom_call_target="tpu_custom_call" | custom-call | tf_op jit(solution)/shard_map/to_heads/pallas_call | solution.py:351
  116.1 15.4 %to_heads.3 = bf16[512,1024]{1,0:T(8,128)(2,1)} custom-call(bf16[64,8192]{1,0:T(8,128)(2,1)} %x_ref.2), custom_call_target="tpu_custom_call" | custom-call | tf_op jit(solution)/shard_map/to_heads/pallas_call | solution.py:351
  138.2 11.3 %add_convert_fusion.1.q_ref.k_ref.v_ref = bf16[2048,768]{1,0:T(8,128)(2,1)} fusion(f32[768]{0:T(1024)S(1)} %dynamic_slice.6, bf16[2048,2048]{1,0:T(8,128)(2,1)} %bitcast.79, bf16[2048,768]{1,0:T(8,128)(2,1)S(1)} %bitcast.96), kind=kOutput, calls=%fused_computation.19 | convolution fusion | flops 6445596672 | bytes 14683136 | tf_op jit(solution)/shard_map/dot_general | solution.py:45
  149.6 23.6 %attention_forward.1 = (bf16[2048,256]{1,0:T(8,128)(2,1)}, f32[2,8,2048]{2,1,0:T(8,128)}) custom-call(bf16[2048,768]{1,0:T(8,128)(2,1)} %add_convert_fusion.1.q_ref.k_ref.v_ref, bf16[2048,768]{1,0:T(8,128)(2,1)} %add_convert_fusion.1.q_ref.k_ref.v_ref, bf16[2048,768]{1,0:T(8,128)(2,1)} %add_convert_fusion.1.q_ref.k_ref.v_ref, ...), custom_call_target="tpu_custom_call" | custom-call | flops 4294967296 | bytes 4194304 | tf_op jit(solution)/shard_map/attention_forward/pallas_call | solution.py:71
  173.1 15.5 %to_tokens.4 = bf16[256,2048]{1,0:T(8,128)(2,1)} custom-call(bf16[2048,256]{1,0:T(8,128)(2,1)} %get-tuple-element.54.x_ref), custom_call_target="tpu_custom_call" | custom-call | tf_op jit(solution)/shard_map/to_tokens/pallas_call | solution.py:351
  189.9 39.7 %plane_gather.5 = bf16[4,4,2,64,2048]{4,3,2,1,0:T(8,128)(2,1)S(1)} custom-call(bf16[256,2048]{1,0:T(8,128)(2,1)S(1)} %copy-done.5), custom_call_target="tpu_custom_call" | custom-call | tf_op jit(solution)/shard_map/plane_gather/pallas_call | solution.py:204
  229.6 4.6 fusion.26
  235.1 39.5 %plane_gather.6 = bf16[4,1,2,256,2048]{4,3,2,1,0:T(8,128)(2,1)S(1)} custom-call(bf16[256,2048]{1,0:T(8,128)(2,1)S(1)} %add_convert_fusion.3.x_ref), custom_call_target="tpu_custom_call" | custom-call | tf_op jit(solution)/shard_map/plane_gather/pallas_call | solution.py:204
  277.8 39.4 %plane_gather.7 = bf16[4,1,2,256,2048]{4,3,2,1,0:T(8,128)(2,1)S(1)} custom-call(bf16[256,2048]{1,0:T(8,128)(2,1)S(1)} %collective-permute-done.1.x_ref), custom_call_target="tpu_custom_call" | custom-call | tf_op jit(solution)/shard_map/plane_gather/pallas_call | solution.py:204
  323.2 3.3 copy-done.3
  326.6 28.8 %multiply_convert_fusion = (bf16[2048,1024]{1,0:T(8,128)(2,1)S(1)}, f32[2048,1024]{1,0:T(8,128)}, f32[2048,1024]{1,0:T(8,128)}) fusion(f32[1024]{0:T(1024)S(1)} %dynamic_slice.7, bf16[2048,2048]{1,0:T(8,128)(2,1)S(1)} %bitcast.84, bf16[2048,1024]{1,0:T(8,128)(2,1)S(1)} %bitcast.93), kind=kOutput, calls=%fused_computation.4 | convolution fusion | flops 8728346624 | bytes 33558528 | tf_op jit(solution)/shard_map/dot_general | solution.py:45
  355.4 10.1 %convolution_convert_fusion.1 = bf16[2048,1024]{1,0:T(8,128)(2,1)S(1)} fusion(bf16[2048,2048]{1,0:T(8,128)(2,1)S(1)} %bitcast.88, bf16[2048,1024]{1,0:T(8,128)(2,1)S(1)} %get-tuple-element.72), kind=kOutput, calls=%fused_computation.21 | convolution fusion | flops 8592031744 | bytes 16777216 | tf_op jit(solution)/shard_map/dot_general | solution.py:51
  370.8 22.3 %convert_reduce_fusion = (f32[1024]{0:T(1024)S(1)}, bf16[2048,1024]{1,0:T(8,128)(2,1)}) fusion(f32[2048,1024]{1,0:T(8,128)} %get-tuple-element.93, f32[2048,1024]{1,0:T(8,128)} %get-tuple-element.110, f32[1024]{0:T(1024)S(1)} %dynamic_slice.7, bf16[2048,2048]{1,0:T(8,128)(2,1)} %bitcast.85, bf16[2048,1024]{1,0:T(8,128)(2,1)S(1)} %bitcast.89), kind=kOutput, calls=%fused_computation.2 | convolution fusion | flops 8625585152 | bytes 33562624 | tf_op jit(solution)/shard_map/dot_general | solution.py:45
  393.1 44.1 %product_reduce.3 = f32[256,2048]{1,0:T(8,128)} custom-call(bf16[8,256,1024]{2,1,0:T(8,128)(2,1)} %bitcast.102, bf16[2048,1024]{1,0:T(8,128)(2,1)} %bitcast.94), custom_call_target="tpu_custom_call" | custom-call | tf_op jit(solution)/shard_map/product_reduce/pallas_call | solution.py:276
  437.2 13.0 %convolution_convert_fusion = bf16[2048,1024]{1,0:T(8,128)(2,1)S(1)} fusion(bf16[2048,2048]{1,0:T(8,128)(2,1)} %bitcast.83, bf16[2048,1024]{1,0:T(8,128)(2,1)} %get-tuple-element.88), kind=kOutput, calls=%fused_computation.20 | convolution fusion | flops 8592031744 | bytes 16777216 | tf_op jit(solution)/shard_map/dot_general | solution.py:51
  456.5 4.2 convert_reduce_fusion.4
  461.6 6.7 convolution_convert_fusion.3.x_ref
  468.4 15.7 %to_heads.5.slope_ref = bf16[2048,256]{1,0:T(8,128)(2,1)} custom-call(bf16[256,2048]{1,0:T(8,128)(2,1)} %convolution_convert_fusion.3.x_ref), custom_call_target="tpu_custom_call" | custom-call | tf_op jit(solution)/shard_map/to_heads/pallas_call | solution.py:351
  484.1 40.9 %attention_backward.1 = bf16[2048,768]{1,0:T(8,128)(2,1)} custom-call(bf16[2048,768]{1,0:T(8,128)(2,1)} %add_convert_fusion.1.q_ref.k_ref.v_ref, bf16[2048,768]{1,0:T(8,128)(2,1)} %add_convert_fusion.1.q_ref.k_ref.v_ref, bf16[2048,768]{1,0:T(8,128)(2,1)} %add_convert_fusion.1.q_ref.k_ref.v_ref, bf16[2048,256]{1,0:T(8,128)(2,1)} %to_heads.5.slope_ref, ...), custom_call_target="tpu_custom_call" | custom-call | flops 10737418240 | bytes 8388608 | tf_op jit(solution)/shard_map/attention_backward/pallas_call | solution.py:107
  525.0 10.3 %convolution_convert_fusion.2 = bf16[2048,768]{1,0:T(8,128)(2,1)S(1)} fusion(bf16[2048,2048]{1,0:T(8,128)(2,1)} %bitcast.80, bf16[2048,768]{1,0:T(8,128)(2,1)} %attention_backward.1), kind=kOutput, calls=%fused_computation.22 | convolution fusion | flops 6444023808 | bytes 14680064 | tf_op jit(solution)/shard_map/dot_general | solution.py:51
  537.9 44.0 %product_reduce.4 = f32[256,2048]{1,0:T(8,128)} custom-call(bf16[8,256,768]{2,1,0:T(8,128)(2,1)} %bitcast.98, bf16[2048,768]{1,0:T(8,128)(2,1)} %bitcast.97), custom_call_target="tpu_custom_call" | custom-call | tf_op jit(solution)/shard_map/product_reduce/pallas_call | solution.py:276
  581.9 44.8 %product_reduce.5 = f32[256,2048]{1,0:T(8,128)} custom-call(bf16[8,256,1024]{2,1,0:T(8,128)(2,1)} %bitcast.99, bf16[2048,1024]{1,0:T(8,128)(2,1)} %bitcast.90), custom_call_target="tpu_custom_call" | custom-call | tf_op jit(solution)/shard_map/product_reduce/pallas_call | solution.py:276
  629.2 4.2 fusion.23
  642.3 49.7 %outer_reduce.1 = f32[256,2048]{1,0:T(8,128)} custom-call(bf16[256,2048]{1,0:T(8,128)(2,1)} %copy.62.left_ref, bf16[256,2048]{1,0:T(8,128)(2,1)} %copy-done.13), custom_call_target="tpu_custom_call" | custom-call | tf_op jit(solution)/shard_map/outer_reduce/pallas_call | solution.py:367
  697.3 6.1 collective-permute-start.2
  704.1 68.2 %total_everywhere.1 = f32[192,128]{1,0:T(8,128)} custom-call(f32[192,128]{1,0:T(8,128)} %bitcast.109), custom_call_target="tpu_custom_call" | custom-call | tf_op jit(solution)/shard_map/total_everywhere/pallas_call | solution.py:312
  772.4 18.1 %to_tokens.6 = bf16[64,8192]{1,0:T(8,128)(2,1)} custom-call(bf16[512,1024]{1,0:T(8,128)(2,1)} %reduce-scatter.9.cloned.1.call-done.x_ref), custom_call_target="tpu_custom_call" | custom-call | tf_op jit(solution)/shard_map/to_tokens/pallas_call | solution.py:351
  793.1 15.1 %to_tokens.7 = bf16[64,8192]{1,0:T(8,128)(2,1)} custom-call(bf16[512,1024]{1,0:T(8,128)(2,1)} %reduce-scatter.5.cloned.1.call-done.x_ref), custom_call_target="tpu_custom_call" | custom-call | tf_op jit(solution)/shard_map/to_tokens/pallas_call | solution.py:351
  814.0 12.3 %to_tokens.5 = bf16[64,6144]{1,0:T(8,128)(2,1)} custom-call(bf16[512,768]{1,0:T(8,128)(2,1)} %reduce-scatter.7.cloned.1.call-done.x_ref), custom_call_target="tpu_custom_call" | custom-call | tf_op jit(solution)/shard_map/to_tokens/pallas_call | solution.py:351
  (158 shorter events, 75.4 us)
Async XLA Ops:
  7.2 128.8 %all-gather.7.cloned.1.call-start = ((), (), s32[]{:S(2)}) async-start(), calls=%async_computation.5 | async-start | bytes 3932160 | tf_op jit(solution)/shard_map/all_gather | solution.py:440
  43.0 145.6 %all-gather.5.cloned.1.call-start = ((), (), s32[]{:S(2)}) async-start(), calls=%async_computation.4 | async-start | bytes 1310720 | tf_op jit(solution)/shard_map/all_gather | solution.py:470
  43.8 276.6 %all-gather.9.cloned.1.call-start = ((), (), s32[]{:S(2)}) async-start(), calls=%async_computation.6 | async-start | bytes 5242880 | tf_op jit(solution)/shard_map/all_gather | solution.py:440
  44.5 55.4 %collective-permute-start = (s32[1,2052]{1,0:T(1,128)S(1)}, s32[1,2052]{1,0:T(1,128)S(1)}, u32[]{:S(2)}, u32[]{:S(2)}) collective-permute-start(s32[1,2052]{1,0:T(1,128)S(1)} %pad_add_fusion), channel_id=1, source_target_pairs={{0,0},{1,1},{2,8},{3,9},{4,16},{5,17},{6,24},{7,25},{8,4},{9,5},{1... | collective-permute-start | bytes 24632 | tf_op jit(solution)/shard_map/ppermute | solution.py:465
  53.3 62.0 %copy-start.26 = (f32[2048]{0:T(1024)S(1)}, f32[2048]{0:T(1024)}, u32[]{:S(2)}) copy-start(f32[2048]{0:T(1024)} %param.22) | copy-start | bytes 24580
  53.3 62.0 %copy-start.27 = (f32[2048]{0:T(1024)S(1)}, f32[2048]{0:T(1024)}, u32[]{:S(2)}) copy-start(f32[2048]{0:T(1024)} %param.21) | copy-start | bytes 24580
  53.3 78.2 %copy-start.28 = (bf16[256,2048]{1,0:T(8,128)(2,1)S(1)}, bf16[256,2048]{1,0:T(8,128)(2,1)}, u32[]{:S(2)}) copy-start(bf16[256,2048]{1,0:T(8,128)(2,1)} %param.33) | copy-start | bytes 3145732
  115.1 252.9 %all-gather.11.cloned.1.call-start = ((), (), s32[]{:S(2)}) async-start(), calls=%async_computation.8 | async-start | bytes 5242880 | tf_op jit(solution)/shard_map/all_gather | solution.py:440
  131.5 57.1 %collective-permute-start.1 = (bf16[256,2048]{1,0:T(8,128)(2,1)S(1)}, bf16[256,2048]{1,0:T(8,128)(2,1)S(1)}, u32[]{:S(2)}, u32[]{:S(2)}) collective-permute-start(bf16[256,2048]{1,0:T(8,128)(2,1)S(1)} %copy-done.28), channel_id=1, source_target_pairs={{0,0},{1,1},{2,8},{3,9},{4,16},{5,17},{6,24},{7,25},{8,4},{9,5},{1... | collective-permute-start | bytes 3145736 | tf_op jit(solution)/shard_map/ppermute | solution.py:465
  134.3 15.3 %copy-start.18 = (s32[2048]{0:T(1024)}, s32[2048]{0:T(1024)S(1)}, u32[]{:S(2)}) copy-start(s32[2048]{0:T(1024)S(1)} %get-tuple-element.105) | copy-start | bytes 24580
  135.6 389.3 %reduce-scatter.5.cloned.1.call-start = ((), (), s32[]{:S(2)}) async-start(), calls=%async_computation.7 | async-start | bytes 5242880 | tf_op jit(solution)/shard_map/reduce_scatter | solution.py:449
  138.2 11.4 %copy-start.9 = (bf16[4,4,2,64,768]{4,3,2,0,1:T(8,128)(2,1)}, bf16[4,4,2,64,768]{4,3,2,0,1:T(8,128)(2,1)S(1)}, u32[]{:S(2)}) copy-start(bf16[4,4,2,64,768]{4,3,2,0,1:T(8,128)(2,1)S(1)} %copy.51) | copy-start | bytes 9437188
  173.1 56.4 %copy-start.29 = (f32[2048]{0:T(1024)S(1)}, f32[2048]{0:T(1024)}, u32[]{:S(2)}) copy-start(f32[2048]{0:T(1024)} %param.24) | copy-start | bytes 24580
  189.9 39.7 %copy-start.12 = (bf16[256,2048]{1,0:T(8,128)(2,1)S(1)}, bf16[256,2048]{1,0:T(8,128)(2,1)}, u32[]{:S(2)}) copy-start(bf16[256,2048]{1,0:T(8,128)(2,1)} %to_tokens.4) | copy-start | bytes 3145732
  320.4 6.2 copy-start.3
  320.4 35.0 %slice-start = ((s8[8388608]{0:T(1024)(128)(4,1)}), s8[4194304]{0:T(1024)(128)(4,1)S(1)}, s32[]{:S(2)}) async-start(s8[8388608]{0:T(1024)(128)(4,1)} %bitcast.86), calls=%async_computation.12 | async-start | bytes 8388608
  323.2 32.2 %copy-start.8 = (bf16[4,4,2,64,1024]{4,3,2,0,1:T(8,128)(2,1)}, bf16[4,4,2,64,1024]{4,3,2,0,1:T(8,128)(2,1)S(1)}, u32[]{:S(2)}) copy-start(bf16[4,4,2,64,1024]{4,3,2,0,1:T(8,128)(2,1)S(1)} %copy.53) | copy-start | bytes 12582916
  326.6 28.8 %slice-start.1 = ((s8[8388608]{0:T(1024)(128)(4,1)}), s8[4194304]{0:T(1024)(128)(4,1)S(1)}, s32[]{:S(2)}) async-start(s8[8388608]{0:T(1024)(128)(4,1)} %bitcast.86), calls=%async_computation.13 | async-start | bytes 8388608
  355.4 10.2 %copy-start.11 = (bf16[2048,1024]{1,0:T(8,128)(2,1)}, bf16[2048,1024]{1,0:T(8,128)(2,1)S(1)}, u32[]{:S(2)}) copy-start(bf16[2048,1024]{1,0:T(8,128)(2,1)S(1)} %get-tuple-element.72) | copy-start | bytes 12582916
  368.0 214.0 %reduce-scatter.9.cloned.1.call-start = ((), (), s32[]{:S(2)}) async-start(), calls=%async_computation.10 | async-start | bytes 5242880 | tf_op jit(solution)/shard_map/reduce_scatter | solution.py:449
  370.8 22.3 %copy-start.7 = (bf16[4,4,2,64,1024]{4,3,2,0,1:T(8,128)(2,1)}, bf16[4,4,2,64,1024]{4,3,2,0,1:T(8,128)(2,1)S(1)}, u32[]{:S(2)}) copy-start(bf16[4,4,2,64,1024]{4,3,2,0,1:T(8,128)(2,1)S(1)} %copy.55) | copy-start | bytes 12582916
  452.6 242.8 %reduce-scatter.7.cloned.1.call-start = ((), (), s32[]{:S(2)}) async-start(), calls=%async_computation.9 | async-start | bytes 3932160 | tf_op jit(solution)/shard_map/reduce_scatter | solution.py:449
  537.3 274.8 %reduce-scatter.11.cloned.1.call-start = ((), (), s32[]{:S(2)}) async-start(), calls=%async_computation.11 | async-start | bytes 1310720 | tf_op jit(solution)/shard_map/reduce_scatter | solution.py:533
  581.9 44.9 %copy-start.6 = (bf16[256,2048]{1,0:T(8,128)(2,1)S(1)}, bf16[256,2048]{1,0:T(8,128)(2,1)}, u32[]{:S(2)}) copy-start(bf16[256,2048]{1,0:T(8,128)(2,1)} %get-tuple-element.47) | copy-start | bytes 3145732
  581.9 44.9 %copy-start.17 = (f32[2048]{0:T(1024)S(1)}, f32[2048]{0:T(1024)}, u32[]{:S(2)}) copy-start(f32[2048]{0:T(1024)} %param.18) | copy-start | bytes 24580
  581.9 44.9 %copy-start.21 = (f32[256]{0:T(256)S(1)}, f32[256]{0:T(256)}, u32[]{:S(2)}) copy-start(f32[256]{0:T(256)} %copy-done.20) | copy-start | bytes 3076
  581.9 44.9 %copy-start.23 = (f32[256]{0:T(256)S(1)}, f32[256]{0:T(256)}, u32[]{:S(2)}) copy-start(f32[256]{0:T(256)} %copy-done.22) | copy-start | bytes 3076
  626.8 10.0 %copy-start.10 = (bf16[2048,768]{1,0:T(8,128)(2,1)S(1)}, bf16[2048,768]{1,0:T(8,128)(2,1)}, u32[]{:S(2)}) copy-start(bf16[2048,768]{1,0:T(8,128)(2,1)} %attention_backward.1) | copy-start | bytes 9437188
  633.4 178.8 %collective-permute-start.3 = (bf16[256,2048]{1,0:T(8,128)(2,1)}, bf16[256,2048]{1,0:T(8,128)(2,1)}, u32[]{:S(2)}, u32[]{:S(2)}) collective-permute-start(bf16[256,2048]{1,0:T(8,128)(2,1)} %get-tuple-element.94), channel_id=1, source_target_pairs={{0,0},{1,1},{8,2},{9,3},{16,4},{17,5},{24,6},{25,7},{4,8},{5,9},{1... | collective-permute-start | bytes 3145736 | tf_op jit(solution)/shard_map/ppermute | solution.py:468
  639.0 56.4 %copy-start.25 = (f32[2048]{0:T(1024)S(1)}, f32[2048]{0:T(1024)}, u32[]{:S(2)}) copy-start(f32[2048]{0:T(1024)} %param.30) | copy-start | bytes 24580
  697.3 131.3 %collective-permute-start.2 = (bf16[256,2048]{1,0:T(8,128)(2,1)S(1)}, bf16[256,2048]{1,0:T(8,128)(2,1)S(1)}, u32[]{:S(2)}, u32[]{:S(2)}) collective-permute-start(bf16[256,2048]{1,0:T(8,128)(2,1)S(1)} %add_convert_fusion.2), channel_id=1, source_target_pairs={{0,0},{1,1},{8,2},{9,3},{16,4},{17,5},{24,6},{25,7},{4,8},{5,9},{1... | collective-permute-start | bytes 3145736 | tf_op jit(solution)/shard_map/ppermute | solution.py:468
  772.4 38.5 %copy-start.14 = (f32[192,128]{1,0:T(8,128)S(1)}, f32[192,128]{1,0:T(8,128)}, u32[]{:S(2)}) copy-start(f32[192,128]{1,0:T(8,128)} %total_everywhere.1) | copy-start | bytes 294916
  (12 other events, 31.8 us)
Sparse Core Ops, SparseCore 0:
  43.1 66.5 all-gather.6
  111.3 29.4 all-gather.4
  142.3 100.6 all-gather.8
  244.5 79.2 all-gather.10
  368.1 77.6 reduce-scatter.4
  452.7 78.7 reduce-scatter.8
  537.5 61.2 reduce-scatter.6
  694.9 64.8 reduce-scatter.10

commit v3 on v2

--- a/solution.py
+++ b/solution.py
@@ -115,7 +115,8 @@
     across, up, partner = ((g, r, 1 - u), ((1 - y) * 2 + c, r, u), (y * 2 + 1 - c, r, u))
 
     def piece(k):
-        return ((1 - y if k & 4 else y) * 2 + (1 - c if k & 2 else c)) * 2 + (1 - u if k & 1 else u)
+        above, beside, side = (k // 4, k // 2 % 2, k % 2)
+        return ((y + above) % 2 * 2 + (c + beside) % 2) * 2 + (u + side) % 2
     return (across, up, partner, piece)
 
 def greet(devices):
@@ -204,76 +205,103 @@
     return pl.pallas_call(functools.partial(gather_kernel, parts), out_shape=jax.ShapeDtypeStruct((groups, parts, subs, rows // parts, width), x.dtype), in_specs=[ANY], out_specs=ANY, scratch_shapes=[pltpu.VMEM((8, rows, width), x.dtype), DMA, DMA((11,)), DMA((11,)), DMA((8, parts))], compiler_params=pltpu.CompilerParams(collective_id=collective_id, has_side_effects=True, vmem_limit_bytes=40 * MIB), name='plane_gather')(x).reshape(-1, width)
 
 def reduce_scratch(rows, width):
-    f, h = (jnp.float32, jnp.bfloat16)
-    return [pltpu.VMEM((4, rows, width), f), pltpu.VMEM((4, rows, width), h), pltpu.VMEM((4, rows, width), h), pltpu.VMEM((3, rows, width), h), pltpu.VMEM((3, rows, width), h), DMA((10,)), DMA((10,))]
-SUM = {0: 0, 1: 1, 4: 2, 5: 3}
-
-def reduce_pieces(refs, ids, make_piece, out):
+    wide, narrow = (jnp.float32, jnp.bfloat16)
+    return [pltpu.VMEM((4, rows, width), wide), pltpu.VMEM((4, rows, width), narrow), pltpu.VMEM((4, rows, width), narrow), pltpu.VMEM((3, rows, width), narrow), pltpu.VMEM((3, rows, width), narrow), DMA((10,)), DMA((10,))]
+
+def reduce_order(step):
+    return 7 - 2 * step + 7 * (step // 4)
+
+def reduce_step(step, piece, refs, ids, out):
     sums, give, take, leave, come, send, recv = refs
     across, up, partner, _ = ids
     half = sums.shape[1] // 2
     low, high = (pl.ds(0, half), pl.ds(half, half))
-    started = []
-
-    def start(number, source, target, device):
-        one = remote(source, target, send, recv, number, device)
-        one.start()
-        started.append(one)
-        return one
-
-    def pair(k, number):
-        give[SUM[k]] = make_piece(k + 2).astype(jnp.bfloat16)
-        one = start(number, give.at[SUM[k]], take.at[SUM[k]], partner)
-        sums[SUM[k]] = make_piece(k)
-        return one
-
-    def settle(k, one):
-        one.wait_recv()
-        sums[SUM[k]] += take[SUM[k]].astype(jnp.float32)
-    settle(5, pair(5, 0))
-    leave[2] = sums[3].astype(jnp.bfloat16)
-    dx = start(4, leave.at[2, low], come.at[2, low], across)
-    dy = start(5, leave.at[2, high], come.at[2, high], up)
-    settle(1, pair(1, 1))
-    leave[0, low] = sums[1, low].astype(jnp.bfloat16)
-    xl = start(6, leave.at[0, low], come.at[0, low], across)
-    settle(4, pair(4, 2))
-    leave[1, high] = sums[2, high].astype(jnp.bfloat16)
-    yh = start(7, leave.at[1, high], come.at[1, high], up)
-    last = pair(0, 3)
-    dy.wait_recv()
-    leave[0, high] = (sums[1, high] + come[2, high].astype(jnp.float32)).astype(jnp.bfloat16)
-    xh = start(8, leave.at[0, high], come.at[0, high], across)
-    dx.wait_recv()
-    leave[1, low] = (sums[2, low] + come[2, low].astype(jnp.float32)).astype(jnp.bfloat16)
-    yl = start(9, leave.at[1, low], come.at[1, low], up)
-    settle(0, last)
-    for one in (xl, yh, xh, yl):
-        one.wait_recv()
-    out[...] = sums[0] + come[0].astype(jnp.float32) + come[1].astype(jnp.float32)
-    for one in started:
-        one.wait_send()
+    pair = step // 2
+
+    def to_partner(number):
+        return remote(give.at[number], take.at[number], send, recv, number, partner)
+
+    def part(number, which, rows, device):
+        return remote(leave.at[which, rows], come.at[which, rows], send, recv, number, device)
+
+    def down(value):
+        return value.astype(jnp.bfloat16)
+
+    def up_cast(value):
+        return value.astype(jnp.float32)
+
+    @pl.when(lax.rem(step, 2) == 0)
+    def _():
+        give[pair] = down(piece)
+        to_partner(pair).start()
+
+    @pl.when(lax.rem(step, 2) == 1)
+    def _():
+        sums[pair] = piece
+        to_partner(pair).wait_recv()
+        sums[pair] += up_cast(take[pair])
+    diagonal_across, diagonal_up = (part(4, 2, low, across), part(5, 2, high, up))
+    across_low, up_high = (part(6, 0, low, across), part(7, 1, high, up))
+    across_high, up_low = (part(8, 0, high, across), part(9, 1, low, up))
+
+    @pl.when(step == 1)
+    def _():
+        leave[2] = down(sums[0])
+        diagonal_across.start()
+        diagonal_up.start()
+
+    @pl.when(step == 3)
+    def _():
+        leave[0, low] = down(sums[1, low])
+        across_low.start()
+
+    @pl.when(step == 5)
+    def _():
+        leave[1, high] = down(sums[2, high])
+        up_high.start()
+
+    @pl.when(step == 7)
+    def _():
+        diagonal_up.wait_recv()
+        leave[0, high] = down(sums[1, high] + up_cast(come[2, high]))
+        across_high.start()
+        diagonal_across.wait_recv()
+        leave[1, low] = down(sums[2, low] + up_cast(come[2, low]))
+        up_low.start()
+        for one in (across_low, up_high, across_high, up_low):
+            one.wait_recv()
+        out[...] = sums[3] + up_cast(come[0]) + up_cast(come[1])
+        for number in range(4):
+            to_partner(number).wait_send()
+        for one in (diagonal_across, diagonal_up, across_low, up_high, across_high, up_low):
+            one.wait_send()
 
 def product_reduce_kernel(slope_ref, weight_ref, out_ref, slopes, load, *refs):
     ids = plane_ids()
-    order = (7, 5, 3, 1, 6, 4, 2, 0)
-    loads = {k: pltpu.make_async_copy(slope_ref.at[ids[3](k)], slopes.at[k], load.at[k]) for k in order}
-    for k in order:
-        loads[k].start()
-    greet(ids[:3])
-
-    def make_piece(k):
-        loads[k].wait()
-        return lax.dot_general(slopes[k], weight_ref[...], (((1,), (1,)), ((), ())), preferred_element_type=jnp.float32)
-    reduce_pieces(refs, ids, make_piece, out_ref)
+    step = pl.program_id(0)
+
+    def fetch(number):
+        return pltpu.make_async_copy(slope_ref.at[ids[3](number)], slopes.at[number], load.at[number])
+
+    @pl.when(step == 0)
+    def _():
+        for early in range(8):
+            fetch(reduce_order(early)).start()
+        greet(ids[:3])
+    k = reduce_order(step)
+    fetch(k).wait()
+    reduce_step(step, product_transposed(slopes[k], weight_ref[...]), refs, ids, out_ref)
+
+def remote_params(collective_id, limit):
+    return pltpu.CompilerParams(collective_id=collective_id, has_side_effects=True, vmem_limit_bytes=limit * MIB)
 
 def product_reduce(slopes, weight, collective_id):
-    if not small_plane():
-        part = product_transposed(slopes.reshape(-1, slopes.shape[2]), weight)
-        return lax.psum_scatter(part.astype(jnp.bfloat16), PLANE, scatter_dimension=0, tiled=True).astype(jnp.float32)
     count, rows, inner = slopes.shape
     width = weight.shape[0]
-    return pl.pallas_call(product_reduce_kernel, out_shape=jax.ShapeDtypeStruct((rows, width), jnp.float32), in_specs=[ANY, VMEM], out_specs=VMEM, scratch_shapes=[pltpu.VMEM((8, rows, inner), slopes.dtype), DMA((8,)), *reduce_scratch(rows, width)], compiler_params=pltpu.CompilerParams(collective_id=collective_id, has_side_effects=True, vmem_limit_bytes=60 << 20), name='product_reduce')(slopes, weight)
+    if not small_plane():
+        part = product_transposed(slopes.reshape(-1, inner), weight)
+        return lax.psum_scatter(part.astype(jnp.bfloat16), PLANE, scatter_dimension=0, tiled=True).astype(jnp.float32)
+    return pl.pallas_call(product_reduce_kernel, grid=(8,), out_shape=jax.ShapeDtypeStruct((rows, width), jnp.float32), in_specs=[ANY, VMEM], out_specs=VMEM, scratch_shapes=[pltpu.VMEM((8, rows, inner), slopes.dtype), DMA((8,)), *reduce_scratch(rows, width)], compiler_params=remote_params(collective_id, 60), name='product_reduce')(slopes, weight)
 
 def total_kernel(x_ref, out_ref, *refs):
     axes = ('grp', 'rep', 'sub')
@@ -350,22 +378,6 @@
     shape = (x.shape[0] // count, x.shape[1] * count) if to_tokens else (x.shape[0] * count, x.shape[1] // count)
     return pl.pallas_call(functools.partial(exchange_kernel, to_tokens), out_shape=jax.ShapeDtypeStruct(shape, x.dtype), in_specs=[ANY], out_specs=ANY, scratch_shapes=[DMA((count - 1,)), DMA((count - 1,)), DMA], compiler_params=pltpu.CompilerParams(collective_id=collective_id, has_side_effects=True), name='to_tokens' if to_tokens else 'to_heads')(x)
 
-def outer_reduce_kernel(left_ref, right_ref, out_ref, *refs):
-    ids = plane_ids()
-    greet(ids[:3])
-    wide = left_ref.shape[1] // 8
-
-    def make_piece(k):
-        block = left_ref[:, pl.ds(pl.multiple_of(ids[3](k) * wide, wide), wide)]
-        return row_outer(block, right_ref[...])
-    reduce_pieces(refs, ids, make_piece, out_ref)
-
-def outer_reduce(left, right, collective_id):
-    if not small_plane():
-        return lax.psum_scatter(row_outer(left, right).astype(jnp.bfloat16), PLANE, scatter_dimension=0, tiled=True).astype(jnp.float32)
-    rows, width = (left.shape[1] // 8, right.shape[1])
-    return pl.pallas_call(outer_reduce_kernel, out_shape=jax.ShapeDtypeStruct((rows, width), jnp.float32), in_specs=[VMEM, VMEM], out_specs=VMEM, scratch_shapes=reduce_scratch(rows, width), compiler_params=pltpu.CompilerParams(collective_id=collective_id, has_side_effects=True, vmem_limit_bytes=60 * MIB), name='outer_reduce')(left, right)
-
 def plane_of(group):
     groups = lax.axis_size('grp')
     return lax.rem(group, 2) * (groups // 2) + group // 2
@@ -374,12 +386,14 @@
     groups = lax.axis_size('grp')
     return lax.rem(plane, groups // 2) * 2 + plane // (groups // 2)
 
-def opening_kernel(x_ref, w_ref, moved_ref, columns_ref, move_send, move_recv, send, recv, local):
-    groups, reps, subs = (lax.axis_size(n) for n in EVERY)
+def opening_kernel(x_ref, *refs):
+    count = lax.axis_size('grp') * lax.axis_size('sub')
+    weights = (len(refs) - 6) // 2
+    sources, (moved_ref, *landings) = (refs[:weights], refs[weights:2 * weights + 1])
+    move_send, move_recv, send, recv, local = refs[2 * weights + 1:]
+    subs = lax.axis_size('sub')
     g, r, u = (lax.axis_index(n) for n in EVERY)
-    count = groups * subs
     place = g * subs + u
-    rows, width = (w_ref.shape[0], columns_ref.shape[1])
     peers = [lax.rem(place + step, count) for step in range(1, count)]
 
     def device(t):
@@ -387,12 +401,17 @@
     target, source = ((r, plane_of(g), u), (group_of(r), g, u))
     stays = (r == g) & (plane_of(g) == r)
 
-    def block(t):
-        return w_ref.at[:, pl.ds(pl.multiple_of(t * width, width), width)]
-    landing = columns_ref.at[pl.ds(pl.multiple_of(place * rows, rows), rows), :]
-    own = pltpu.make_async_copy(block(place), landing, local.at[0])
-    own.start()
-    kept = pltpu.make_async_copy(x_ref, moved_ref, local.at[1])
+    def block(number, t):
+        width = landings[number].shape[1]
+        return sources[number].at[:, pl.ds(pl.multiple_of(t * width, width), width)]
+
+    def landing(number):
+        rows = sources[number].shape[0]
+        return landings[number].at[pl.ds(pl.multiple_of(place * rows, rows), rows), :]
+    owns = [pltpu.make_async_copy(block(number, place), landing(number), local.at[number]) for number in range(weights)]
+    for one in owns:
+        one.start()
+    kept = pltpu.make_async_copy(x_ref, moved_ref, local.at[weights])
     moved = pltpu.make_async_remote_copy(src_ref=x_ref, dst_ref=moved_ref, send_sem=move_send, recv_sem=move_recv, device_id=target, device_id_type=MESH)
     barrier = pltpu.get_barrier_semaphore()
     for t in peers:
@@ -411,11 +430,13 @@
     def _():
         moved.start()
     copies = []
-    for step, t in enumerate(peers):
-        one = pltpu.make_async_remote_copy(src_ref=block(t), dst_ref=landing, send_sem=send.at[step], recv_sem=recv.at[step], device_id=device(t), device_id_type=MESH)
-        one.start()
-        copies.append(one)
-    own.wait()
+    for number in range(weights):
+        for step, t in enumerate(peers):
+            one = pltpu.make_async_remote_copy(src_ref=block(number, t), dst_ref=landing(number), send_sem=send.at[number, step], recv_sem=recv.at[number, step], device_id=device(t), device_id_type=MESH)
+            one.start()
+            copies.append(one)
+    for one in owns:
+        one.wait()
     for one in copies:
         one.wait_recv()
     for one in copies:
@@ -430,10 +451,203 @@
         moved.wait_recv()
         moved.wait_send()
 
-def opening(x, weight, collective_id):
+def opening(x, weights, collective_id):
     count = lax.axis_size('grp') * lax.axis_size('sub')
-    columns = jax.ShapeDtypeStruct((weight.shape[0] * count, weight.shape[1] // count), weight.dtype)
-    return pl.pallas_call(opening_kernel, out_shape=[jax.ShapeDtypeStruct(x.shape, x.dtype), columns], in_specs=[VMEM, ANY], out_specs=[VMEM, ANY], scratch_shapes=[DMA, DMA, DMA((count - 1,)), DMA((count - 1,)), DMA((2,))], compiler_params=pltpu.CompilerParams(collective_id=collective_id, has_side_effects=True), name='opening')(x, weight)
+    number = len(weights)
+    columns = [jax.ShapeDtypeStruct((w.shape[0] * count, w.shape[1] // count), w.dtype) for w in weights]
+    return pl.pallas_call(opening_kernel, out_shape=[jax.ShapeDtypeStruct(x.shape, x.dtype), *columns], in_specs=[VMEM] + [ANY] * number, out_specs=[VMEM] + [ANY] * number, scratch_shapes=[DMA, DMA, DMA((number, count - 1)), DMA((number, count - 1)), DMA((number + 1,))], compiler_params=pltpu.CompilerParams(collective_id=collective_id, has_side_effects=True), name='opening')(x, *weights)
+
+def attend_kernel(heads, head_ref, place_ref, first_ref, last_ref, mixing_ref, attended_ref, total_ref, out_ref, *refs):
+    ids = plane_ids()
+    step = pl.program_id(0)
+
+    @pl.when(step == 0)
+    def _():
+        greet(ids[:3])
+    rows = out_ref.shape[0]
+    size = attended_ref.shape[1] // heads
+    factor = size ** (-0.5) * log2_e
+    first_row = pl.multiple_of(ids[3](reduce_order(step)) * rows, rows)
+    here = pl.ds(first_row, rows)
+    place = place_ref[here, :]
+    allowed = (first_ref[...] <= place) & (place <= last_ref[...])
+    for h in range(heads):
+        q, k, v = (3 * h + j for j in range(3))
+        scores = product_transposed(head_ref[here, q * size:(q + 1) * size], head_ref[:, k * size:(k + 1) * size])
+        scores = jnp.where(allowed, scores * factor, masked_score)
+        top = jnp.max(scores, axis=1, keepdims=True)
+        soft = jnp.exp2(scores - top)
+        total = jnp.sum(soft, axis=1, keepdims=True)
+        mixture = product(soft.astype(jnp.bfloat16), head_ref[:, v * size:(v + 1) * size])
+        attended_ref[here, h * size:(h + 1) * size] = (mixture / total).astype(jnp.bfloat16)
+        log_total = jnp.broadcast_to(top + jnp.log2(total), (rows, 128))
+        total_ref[h, :, here] = log_total.T[:8]
+    reduce_step(step, product(attended_ref[here, :], mixing_ref[...]), refs, ids, out_ref)
+
+def attend(packed, places, key_last, mixing, heads, token_rows, collective_id):
+    rows = packed.shape[0]
+    inner, width = mixing.shape
+    if not small_plane():
+        attended, totals = attention_forward(packed, places, key_last, heads)
+        part = product(attended, mixing).astype(jnp.bfloat16)
+        return (attended, totals, lax.psum_scatter(part, PLANE, scatter_dimension=0, tiled=True).astype(jnp.float32))
+    return pl.pallas_call(functools.partial(attend_kernel, heads), grid=(8,), out_shape=[jax.ShapeDtypeStruct((rows, inner), jnp.bfloat16), jax.ShapeDtypeStruct((heads, 8, rows), jnp.float32), jax.ShapeDtypeStruct((token_rows, width), jnp.float32)], in_specs=[VMEM] * 5, out_specs=[VMEM] * 3, scratch_shapes=reduce_scratch(token_rows, width), compiler_params=remote_params(collective_id, 60), name='attend')(packed, places[:, None], places[None, :], key_last[None, :], mixing)
+
+def gather_order(step):
+    return step + 2 * (step % 2) - 1 + (8 - step) // 8 - step // 7
+
+def gather_step(step, slots, send, recv, ids):
+    across, up, partner, _ = ids
+    half = slots.shape[1] // 2
+    low, high = (pl.ds(0, half), pl.ds(half, half))
+
+    def copy(number, source, target, device):
+        return remote(slots.at[source], slots.at[target], send, recv, number, device)
+    across_low = copy(0, (0, low), (1, low), across)
+    up_high = copy(1, (0, high), (4, high), up)
+    across_high = copy(2, (0, high), (1, high), across)
+    up_low = copy(3, (0, low), (4, low), up)
+    own = copy(4, 0, 2, partner)
+    far_low = copy(5, (1, low), (5, low), up)
+    far_high = copy(6, (4, high), (5, high), across)
+    pass_across = copy(7, 1, 3, partner)
+    pass_up = copy(8, 4, 6, partner)
+    pass_low = copy(9, (5, low), (7, low), partner)
+    pass_high = copy(10, (5, high), (7, high), partner)
+
+    @pl.when(step == 0)
+    def _():
+        for one in (across_low, up_high, own, across_high, up_low):
+            one.start()
+
+    @pl.when(step == 1)
+    def _():
+        own.wait_recv()
+
+    @pl.when(step == 2)
+    def _():
+        across_low.wait_recv()
+        far_low.start()
+        up_high.wait_recv()
+        far_high.start()
+        across_high.wait_recv()
+        pass_across.start()
+
+    @pl.when(step == 3)
+    def _():
+        up_low.wait_recv()
+        pass_up.start()
+
+    @pl.when(step == 4)
+    def _():
+        pass_across.wait_recv()
+
+    @pl.when(step == 5)
+    def _():
+        pass_up.wait_recv()
+
+    @pl.when(step == 6)
+    def _():
+        far_low.wait_recv()
+        pass_low.start()
+        far_high.wait_recv()
+        pass_high.start()
+
+    @pl.when(step == 7)
+    def _():
+        pass_low.wait_recv()
+        pass_high.wait_recv()
+        for one in (across_low, up_high, across_high, up_low, own, far_low, far_high, pass_across, pass_up, pass_low, pass_high):
+            one.wait_send()
+
+def attend_back_kernel(heads, branch_ref, head_ref, mixing_ref, total_ref, place_ref, first_ref, last_ref, every_ref, out_ref, turned, key_sum, value_sum, slots, load, send, recv, store):
+    ids = plane_ids()
+    step = pl.program_id(0)
+    rows = slots.shape[1]
+    size = head_ref.shape[1] // (3 * heads)
+    scale = size ** (-0.5)
+    factor = scale * log2_e
+
+    @pl.when(step == 0)
+    def _():
+        first = pltpu.make_async_copy(branch_ref, slots.at[0], load)
+        first.start()
+        for h in range(heads):
+            turned[h] = head_ref[:, (3 * h + 1) * size:(3 * h + 2) * size].T
+        key_sum[...] = jnp.zeros_like(key_sum)
+        value_sum[...] = jnp.zeros_like(value_sum)
+        greet(ids[:3])
+        first.wait()
+    gather_step(step, slots, send, recv, ids)
+    k = gather_order(step)
+    place_of = ids[3](k)
+
+    def keep(number):
+        return pltpu.make_async_copy(slots.at[number], every_ref.at[ids[3](number)], store.at[number])
+    keep(k).start()
+    here = pl.ds(pl.multiple_of(place_of * rows, rows), rows)
+    slopes = product_transposed(slots[k], mixing_ref[...]).astype(jnp.bfloat16)
+    place = place_ref[:, here]
+    allowed = (first_ref[...] <= place) & (place <= last_ref[...])
+    for h in range(heads):
+        queries = head_ref[here, 3 * h * size:(3 * h + 1) * size]
+        keys = head_ref[:, (3 * h + 1) * size:(3 * h + 2) * size]
+        values = head_ref[:, (3 * h + 2) * size:(3 * h + 3) * size]
+        slope = slopes[:, h * size:(h + 1) * size]
+        scores = product_transposed(keys, queries)
+        soft = jnp.where(allowed, jnp.exp2(scores * factor - total_ref[h, :1, here]), 0.0)
+        weight_slope = product_transposed(values, slope)
+        centre = jnp.sum(soft * weight_slope, axis=0, keepdims=True)
+        score_slope = (soft * (weight_slope - centre)).astype(jnp.bfloat16)
+        value_sum[h] += product(soft.astype(jnp.bfloat16), slope)
+        key_sum[h] += product(score_slope, queries)
+        query_slope = product(turned[h], score_slope)
+        out_ref[here, 3 * h * size:(3 * h + 1) * size] = (query_slope.T * scale).astype(jnp.bfloat16)
+
+    @pl.when(step == 7)
+    def _():
+        for h in range(heads):
+            out_ref[:, (3 * h + 1) * size:(3 * h + 2) * size] = (key_sum[h] * scale).astype(jnp.bfloat16)
+            out_ref[:, (3 * h + 2) * size:(3 * h + 3) * size] = value_sum[h].astype(jnp.bfloat16)
+        for number in range(8):
+            keep(number).wait()
+
+def attend_back(branch_slope, packed, mixing, totals, places, key_last, heads, collective_id):
+    rows, columns = packed.shape
+    token_rows, width = branch_slope.shape
+    size = columns // (3 * heads)
+    if not small_plane():
+        every = lax.all_gather(branch_slope, PLANE, axis=0, tiled=True)
+        slopes = product_transposed(every, mixing).astype(jnp.bfloat16)
+        return (every, attention_backward(packed, totals, slopes, places, key_last, heads))
+    every, slopes = pl.pallas_call(functools.partial(attend_back_kernel, heads), grid=(8,), out_shape=[jax.ShapeDtypeStruct((8, token_rows, width), jnp.bfloat16), jax.ShapeDtypeStruct((rows, columns), jnp.bfloat16)], in_specs=[ANY] + [VMEM] * 6, out_specs=[ANY, VMEM], scratch_shapes=[pltpu.VMEM((heads, size, rows), jnp.bfloat16), pltpu.VMEM((heads, rows, size), jnp.float32), pltpu.VMEM((heads, rows, size), jnp.float32), pltpu.VMEM((8, token_rows, width), jnp.bfloat16), DMA, DMA((11,)), DMA((11,)), DMA((8,))], compiler_params=remote_params(collective_id, 62), name='attend_back')(branch_slope, packed, mixing, totals, places[None, :], places[:, None], key_last[:, None])
+    return (every.reshape(rows, width), slopes)
+
+def sub_rows(own):
+    rows, width = own.shape
+    reps, subs = (lax.axis_size('rep'), lax.axis_size('sub'))
+    shares = own.reshape(subs, reps // subs, -1, width)
+    if subs != 2:
+        every = lax.all_to_all(shares, 'sub', split_axis=0, concat_axis=0, tiled=True)
+        return every.transpose(1, 0, 2, 3).reshape(rows, width)
+    me = lax.axis_index('sub')
+    kept = jnp.where(me == 0, shares[0], shares[1])
+    come = lax.ppermute(jnp.where(me == 0, shares[1], shares[0]), 'sub', [(0, 1), (1, 0)])
+    first, second = (jnp.where(me == 0, kept, come), jnp.where(me == 0, come, kept))
+    return jnp.stack([first, second], axis=1).reshape(rows, width)
+
+def sub_owned(part, reps):
+    rows, width = part.shape
+    subs = lax.axis_size('sub')
+    shares = part.reshape(reps // subs, subs, -1, width).transpose(1, 0, 2, 3)
+    if subs != 2:
+        every = lax.all_to_all(shares, 'sub', split_axis=0, concat_axis=0, tiled=True)
+        return every.reshape(rows, width)
+    me = lax.axis_index('sub')
+    kept = jnp.where(me == 0, shares[0], shares[1])
+    come = lax.ppermute(jnp.where(me == 0, shares[1], shares[0]), 'sub', [(0, 1), (1, 0)])
+    first, second = (jnp.where(me == 0, kept, come), jnp.where(me == 0, come, kept))
+    return jnp.concatenate([first, second], axis=0).reshape(rows, width)
 
 def rep_rows(own):
     groups, reps, subs = (lax.axis_size(name) for name in EVERY)
@@ -447,6 +661,11 @@
     ordered = gradient.astype(jnp.bfloat16).reshape(groups, reps, subs, -1, columns)
     ordered = ordered.transpose(1, 0, 2, 3, 4).reshape(-1, columns)
     return lax.psum_scatter(ordered, 'rep', scatter_dimension=0, tiled=True)
+
+def owner_rows(summed, plane_count):
+    columns = summed.shape[1]
+    own = lax.all_to_all(summed.reshape(plane_count, -1, columns), PLANE, split_axis=0, concat_axis=0, tiled=True)
+    return own.transpose(1, 0, 2).reshape(-1, plane_count * columns).astype(jnp.float32)
 
 def shards(layer_input, entry_gain, entry_shift, joint_weight, query_offset, value_offset, mixing_weight, attention_offset, middle_gain, middle_shift, expand_weight, expand_offset, shrink_weight, shrink_offset, placement, slot_lengths, cotangent):
     token_rows, width = layer_input.shape
@@ -468,29 +687,26 @@
         return lax.ppermute(array, EVERY, list(zip(away, home)))
     facts = to_plane(jnp.concatenate([placement, slot_lengths], axis=1))[0]
     mixing_own = lax.all_gather(mixing_weight, 'rep', axis=0, tiled=True)
-    moved_input, joint_own = opening(layer_input, joint_weight, 12)
+    moved_input, joint_own, expand_own, shrink_own = opening(layer_input, (joint_weight, expand_weight, shrink_weight), 12)
+    joint_own, mixing_own = lax.optimization_barrier((joint_own, mixing_own))
     input_float = moved_input.astype(jnp.float32)
     joint_slice = rep_rows(joint_own)
     entry_normal, entry_inverse = norm_terms(input_float)
     entry_normed = (entry_normal * entry_gain + entry_shift).astype(jnp.bfloat16)
     entry_all = plane_gather(entry_normed, 1)
-    expand_weight, shrink_weight, cotangent, facts, entry_all = lax.optimization_barrier((expand_weight, shrink_weight, cotangent, facts, entry_all))
+    cotangent, facts, entry_all = lax.optimization_barrier((cotangent, facts, entry_all))
     places, lengths = (facts[:placement.shape[1]], facts[placement.shape[1]:])
     prompt = places.shape[0] // 2
     key_last = key_bounds(places, lengths, prompt)
-    expand_slice = rep_rows(exchange(expand_weight, False, 13))
-    shrink_own = exchange(shrink_weight, False, 14)
+    expand_slice = rep_rows(expand_own)
     shrink_slice = rep_rows(shrink_own)
-    cotangent, shrink_own = lax.optimization_barrier((cotangent, shrink_own))
     cotangent = to_plane(cotangent)
+    mixing_slice = sub_rows(mixing_own)
     offsets = jnp.stack([query_offset.reshape(HEADS, head_size), jnp.zeros((HEADS, head_size), jnp.float32), value_offset.reshape(HEADS, head_size)], axis=1).reshape(-1)
     offsets = lax.dynamic_slice_in_dim(offsets, plane_index * 3 * head_columns, 3 * head_columns)
     heads_kept = (product(entry_all, joint_slice) + offsets).astype(jnp.bfloat16)
-    mixture, log_totals = attention_forward(heads_kept, places, key_last, local_heads)
-    attended = exchange(mixture, True, 3)
-    mixing_own, cotangent, attended = lax.optimization_barrier((mixing_own, cotangent, attended))
-    mixing_whole = plane_gather(mixing_own, 2, reps)
-    residual = input_float + (product(attended, mixing_whole) + attention_offset)
+    attended, log_totals, branch = attend(heads_kept, places, key_last, mixing_slice, local_heads, token_rows, 3)
+    residual = input_float + (branch + attention_offset)
     middle_normal, middle_inverse = norm_terms(residual)
     middle_normed = (middle_normal * middle_gain + middle_shift).astype(jnp.bfloat16)
     middle_all = plane_gather(middle_normed, 5)
@@ -514,36 +730,38 @@
     cotangent_float = cotangent.astype(jnp.float32)
     residual_slope = cotangent_float + norm_back(normed_slope, middle_gain, middle_normal, middle_inverse)
     branch_slope = residual_slope.astype(jnp.bfloat16)
-    attended_slope = product_transposed(branch_slope, mixing_whole).astype(jnp.bfloat16)
-    head_slopes = exchange(attended_slope, False, 7)
-    joint_slope = attention_backward(heads_kept, log_totals, head_slopes, places, key_last, local_heads)
-    shrink_sums, joint_slope = lax.optimization_barrier((shrink_sums, joint_slope))
+    branch_all, joint_slope = attend_back(branch_slope, heads_kept, mixing_slice, log_totals, places, key_last, local_heads, 7)
+    shrink_gradient = owner_rows(shrink_sums, plane_count)
+    shrink_gradient, joint_slope = lax.optimization_barrier((shrink_gradient, joint_slope))
     joint_part = row_outer(entry_all, joint_slope).astype(jnp.bfloat16)
-    joint_part, joint_slope = lax.optimization_barrier((joint_part, joint_slope))
+    joint_part, joint_slope, expand_sums, attended = lax.optimization_barrier((joint_part, joint_slope, expand_sums, attended))
     joint_sums = rep_sums(joint_part)
     entry_slope = product_reduce(joint_slope.reshape(plane_count, token_rows, 3 * head_columns), joint_slice, 9)
-    expand_sums, entry_slope = lax.optimization_barrier((expand_sums, entry_slope))
-    input_gradient = from_plane((residual_slope + norm_back(entry_slope, entry_gain, entry_normal, entry_inverse)).astype(jnp.bfloat16))
-    activated, attended, entry_slope = lax.optimization_barrier((activated, attended, entry_slope))
+    own_gradient = (residual_slope + norm_back(entry_slope, entry_gain, entry_normal, entry_inverse)).astype(jnp.bfloat16)
+    own_gradient, attended, expand_sums = lax.optimization_barrier((own_gradient, attended, expand_sums))
+    input_gradient = from_plane(own_gradient)
+    expand_gradient = owner_rows(expand_sums, plane_count)
+    mixing_part = sub_owned(row_outer(attended, branch_all).astype(jnp.bfloat16), reps)
+    mixing_part, activated, joint_sums = lax.optimization_barrier((mixing_part, activated, joint_sums))
+    mixing_sums = lax.psum_scatter(mixing_part, 'rep', scatter_dimension=0, tiled=True)
     shrunk = product_reduce(activated.reshape(plane_count, token_rows, hidden_local), shrink_slice, 8)
-    joint_sums, shrunk = lax.optimization_barrier((joint_sums, shrunk))
-    layer_output = from_plane((residual + shrunk + shrink_offset).astype(jnp.bfloat16))
-    attended_by_sub = attended.reshape(token_rows, groups, reps, subs, -1).transpose(0, 1, 3, 2, 4)
-    mixing_sums = outer_reduce(attended_by_sub.reshape(token_rows, width), branch_slope, 11)
-    mixing_gradient = lax.psum_scatter(mixing_sums.astype(jnp.bfloat16), 'rep', scatter_dimension=0, tiled=True).astype(jnp.float32)
+    shrunk, mixing_sums, input_gradient, expand_gradient = lax.optimization_barrier((shrunk, mixing_sums, input_gradient, expand_gradient))
+    own_output = (residual + shrunk + shrink_offset).astype(jnp.bfloat16)
+    layer_output = from_plane(own_output)
+    mixing_gradient = mixing_sums.astype(jnp.float32)
     slope_sums = jnp.sum(joint_slope.astype(jnp.float32), axis=0).reshape(local_heads, 3, head_size)
 
     def placed(piece, whole_size):
         return lax.dynamic_update_slice_in_dim(jnp.zeros((whole_size,), jnp.float32), piece, plane_index * piece.shape[0], 0)
     small = [jnp.sum(entry_slope * entry_normal, axis=0), jnp.sum(entry_slope, axis=0), placed(slope_sums[:, 0].reshape(-1), width), placed(slope_sums[:, 2].reshape(-1), width), jnp.sum(branch_slope.astype(jnp.float32), axis=0), jnp.sum(normed_slope * middle_normal, axis=0), jnp.sum(normed_slope, axis=0), placed(jnp.sum(expanded_slope.astype(jnp.float32), axis=0), hidden_width), jnp.sum(cotangent_float, axis=0)]
-    small_all = total_everywhere(jnp.concatenate(small).reshape(-1, 128), 10).reshape(-1)
+    small_own = jnp.concatenate(small).reshape(-1, 128)
+    small_own, own_output = lax.optimization_barrier((small_own, own_output))
+    small_all = total_everywhere(small_own, 10).reshape(-1)
     small_sums, first = ([], 0)
     for piece in small:
         small_sums.append(small_all[first:first + piece.shape[0]])
         first += piece.shape[0]
-    shrink_gradient = exchange(shrink_sums, True, 15).astype(jnp.float32)
-    expand_gradient = exchange(expand_sums, True, 16).astype(jnp.float32)
-    joint_gradient = exchange(joint_sums, True, 17).astype(jnp.float32)
+    joint_gradient = owner_rows(joint_sums, plane_count)
     return (layer_output, input_gradient, small_sums[0], small_sums[1], joint_gradient, small_sums[2], small_sums[3], mixing_gradient, small_sums[4], small_sums[5], small_sums[6], expand_gradient, small_sums[7], shrink_gradient, small_sums[8])
 
 def solution(mesh):

time: 847 us -> 736 us (0.87)
  Pallas kernels: 620 us -> 475 us
  waiting for transfers between devices: 0.94 us -> 32.5 us
  starting transfers between devices: 15.3 us -> 35.5 us
  matrix products: 107 us -> 95.1 us
    pallas_call x13 -> x5, Pallas kernels: 354 us -> 245 us  [the longest x3 143 us: product_reduce(): pl.pallas_call(product_reduce_kernel, grid=(8,), out_shape=jax.ShapeDtype...]
    pallas_call x4 -> x3, Pallas kernels: 162 us -> 119 us  [plane_gather(): pl.pallas_call(functools.partial(gather_kernel, parts), out_shape=jax.Sha...]
    pallas_call x1, Pallas kernels: 35.8 us -> 58.5 us  [opening(): pl.pallas_call(opening_kernel, out_shape=[jax.ShapeDtypeStruct(x.shape, x...]
    ppermute x0 -> x2, waiting for transfers between devices: none -> 20.3 us  [the longest x1 13.2 us: sub_owned(): lax.ppermute(jnp.where(me == 0, shares[1], shares[0]), 'sub', [(0, 1), (1...]
    pallas_call x1, Pallas kernels: 68.2 us -> 51.3 us  [total_everywhere(): pl.pallas_call(total_kernel, out_shape=jax.ShapeDtypeStruct(x.shape, x.dt...]
    all_to_all x0 -> x3, starting transfers between devices: none -> 16.7 us  [owner_rows(): lax.all_to_all(summed.reshape(plane_count, -1, columns), PLANE, split_axi...]
    all_to_all x0 -> x3, waiting for transfers between devices: none -> 10.7 us  [owner_rows(): lax.all_to_all(summed.reshape(plane_count, -1, columns), PLANE, split_axi...]
    dot_general x4 -> x3, matrix products: 67 us -> 56.4 us  [product(): jnp.dot(left_matrix, right_matrix, preferred_element_type=jnp.float32)]
  transfers between devices with their start and end apart: 12 -> 17, of which waited for: 0 -> 4; matrix products, arithmetic and copies ran while one was open for 20% -> 21% of each run, Pallas kernels for 70% -> 65%
where the time goes in v3:
time: 736 us; the launch traced here: 728 us
  Pallas kernels  475 us (65%)
  matrix products  95.1 us (13%)
  local copies, waits for them, and re-layouts  42 us (6%)
  starting transfers between devices  35.5 us (5%)
  other arithmetic  32.6 us (4%)
  waiting for transfers between devices  32.5 us (4%)
  between operations  15.2 us (2%)
    pallas_call x3, Pallas kernels, product_reduce(): pl.pallas_call(product_reduce_kernel, grid=(8,), out_shape=jax.ShapeDtype...  143 us
    pallas_call x3, Pallas kernels, plane_gather(): pl.pallas_call(functools.partial(gather_kernel, parts), out_shape=jax.Sha...  119 us
    pallas_call x1, Pallas kernels, opening(): pl.pallas_call(opening_kernel, out_shape=[jax.ShapeDtypeStruct(x.shape, x...  58.5 us
    dot_general x3, matrix products, product(): jnp.dot(left_matrix, right_matrix, preferred_element_type=jnp.float32)  56.4 us
    pallas_call x1, Pallas kernels, attend_back(): pl.pallas_call(functools.partial(attend_back_kernel, heads), grid=(8,), o...  55.5 us
    pallas_call x1, Pallas kernels, total_everywhere(): pl.pallas_call(total_kernel, out_shape=jax.ShapeDtypeStruct(x.shape, x.dt...  51.3 us
    pallas_call x1, Pallas kernels, attend(): pl.pallas_call(functools.partial(attend_kernel, heads), grid=(8,), out_sh...  47 us
    dot_general x4, matrix products, row_outer(): lax.dot_general(left_matrix, right_matrix, (((0,), (0,)), ((), ())), pref...  38.7 us
  transfers between devices with their start and end apart: 17, of which 4 were waited for; matrix products, arithmetic and copies ran while one was open for 21% of the time, Pallas kernels for 65%

profile of v3, /device:TPU:19, one launch (start us, length us, event | category | flops | bytes accessed | tf_op | source)
XLA Modules:
  0.0 727.5 jit_solution(13559404616643264282)
XLA Ops:
  8.0 58.5 %opening.1 = (bf16[256,2048]{1,0:T(8,128)(2,1)}, bf16[512,768]{1,0:T(8,128)(2,1)}, bf16[512,1024]{1,0:T(8,128)(2,1)}, bf16[512,1024]{1,0:T(8,128)(2,1)}) custom-call(bf16[256,2048]{1,0:T(8,128)(2,1)} %x_ref.1, bf16[64,6144]{1,0:T(8,128)(2,1)} %refs_0_.1, bf16[64,8192]{1,0:T(8,128)(2,1)} %refs_1_.1, bf16[64,8192]{1,0:T(8,128)(2,1)} %refs_2_.1), custom_call_target="tpu_custom_call" | custom-call | tf_op jit(solution)/shard_map/opening/pallas_call | solution.py:458
  76.4 40.0 %plane_gather.3 = bf16[4,1,2,256,2048]{4,3,2,1,0:T(8,128)(2,1)S(1)} custom-call(bf16[256,2048]{1,0:T(8,128)(2,1)S(1)} %fusion.13.x_ref), custom_call_target="tpu_custom_call" | custom-call | tf_op jit(solution)/shard_map/plane_gather/pallas_call | solution.py:205
  116.4 3.2 copy-done
  123.3 3.3 collective-permute-start.2
  126.7 7.1 collective-permute-done.1
  137.2 11.7 %add_convert_fusion.1.head_ref = bf16[2048,768]{1,0:T(8,128)(2,1)} fusion(f32[768]{0:T(1024)S(1)} %dynamic_slice.6, bf16[2048,2048]{1,0:T(8,128)(2,1)} %bitcast.107, bf16[2048,768]{1,0:T(8,128)(2,1)S(1)} %bitcast.123), kind=kOutput, calls=%fused_computation.19 | convolution fusion | flops 6445596672 | bytes 14683136 | tf_op jit(solution)/shard_map/dot_general | solution.py:45
  148.9 47.0 %attend.1 = (bf16[2048,256]{1,0:T(8,128)(2,1)}, f32[2,8,2048]{2,1,0:T(8,128)}, f32[256,2048]{1,0:T(8,128)}) custom-call(bf16[2048,768]{1,0:T(8,128)(2,1)} %add_convert_fusion.1.head_ref, s32[2048,1]{1,0:T(8,128)} %copy.64.place_ref.first_ref, s32[1,2048]{1,0:T(1,128)} %bitcast.149, s32[1,2048]{1,0:T(1,128)} %bitcast.152, bf16[256,2048]{1,0:T(8,128)(2,1)} %bitcast.128), custom_call_target="tpu_custom_call" | custom-call | tf_op jit(solution)/shard_map/attend/pallas_call | solution.py:494
  199.0 39.9 %plane_gather.4 = bf16[4,1,2,256,2048]{4,3,2,1,0:T(8,128)(2,1)S(1)} custom-call(bf16[256,2048]{1,0:T(8,128)(2,1)S(1)} %add_convert_fusion.3.x_ref), custom_call_target="tpu_custom_call" | custom-call | tf_op jit(solution)/shard_map/plane_gather/pallas_call | solution.py:205
  239.0 3.6 copy-done.1
  245.7 39.5 %plane_gather.5 = bf16[4,1,2,256,2048]{4,3,2,1,0:T(8,128)(2,1)S(1)} custom-call(bf16[256,2048]{1,0:T(8,128)(2,1)S(1)} %collective-permute-done.2.x_ref), custom_call_target="tpu_custom_call" | custom-call | tf_op jit(solution)/shard_map/plane_gather/pallas_call | solution.py:205
  285.2 28.8 %multiply_convert_fusion = (bf16[2048,1024]{1,0:T(8,128)(2,1)S(1)}, f32[2048,1024]{1,0:T(8,128)}, f32[2048,1024]{1,0:T(8,128)}) fusion(f32[1024]{0:T(1024)S(1)} %dynamic_slice.7, bf16[2048,2048]{1,0:T(8,128)(2,1)S(1)} %bitcast.112, bf16[2048,1024]{1,0:T(8,128)(2,1)S(1)} %bitcast.120), kind=kOutput, calls=%fused_computation.4 | convolution fusion | flops 8728346624 | bytes 33558528 | tf_op jit(solution)/shard_map/dot_general | solution.py:45
  314.0 9.8 %convolution_convert_fusion.1 = bf16[2048,1024]{1,0:T(8,128)(2,1)S(1)} fusion(bf16[2048,2048]{1,0:T(8,128)(2,1)S(1)} %bitcast.113, bf16[2048,1024]{1,0:T(8,128)(2,1)S(1)} %get-tuple-element.82), kind=kOutput, calls=%fused_computation.21 | convolution fusion | flops 8592031744 | bytes 16777216 | tf_op jit(solution)/shard_map/dot_general | solution.py:51
  329.2 3.3 copy-done.3
  332.5 15.9 %convert_reduce_fusion = (f32[1024]{0:T(1024)S(1)}, bf16[2048,1024]{1,0:T(8,128)(2,1)}) fusion(f32[2048,1024]{1,0:T(8,128)} %get-tuple-element.107, f32[2048,1024]{1,0:T(8,128)} %get-tuple-element.129, f32[1024]{0:T(1024)S(1)} %dynamic_slice.7, bf16[2048,2048]{1,0:T(8,128)(2,1)S(1)} %bitcast.114, bf16[2048,1024]{1,0:T(8,128)(2,1)S(1)} %bitcast.116), kind=kOutput, calls=%fused_computation.2 | convolution fusion | flops 8625585152 | bytes 33562624 | tf_op jit(solution)/shard_map/dot_general | solution.py:45
  348.4 44.2 %product_reduce.3 = f32[256,2048]{1,0:T(8,128)} custom-call(bf16[8,256,1024]{2,1,0:T(8,128)(2,1)} %bitcast.134, bf16[2048,1024]{1,0:T(8,128)(2,1)} %bitcast.121), custom_call_target="tpu_custom_call" | custom-call | tf_op jit(solution)/shard_map/product_reduce/pallas_call | solution.py:304
  392.6 12.7 %convolution_convert_fusion = bf16[2048,1024]{1,0:T(8,128)(2,1)S(1)} fusion(bf16[2048,2048]{1,0:T(8,128)(2,1)} %bitcast.109, bf16[2048,1024]{1,0:T(8,128)(2,1)} %get-tuple-element.102), kind=kOutput, calls=%fused_computation.20 | convolution fusion | flops 8592031744 | bytes 16777216 | tf_op jit(solution)/shard_map/dot_general | solution.py:51
  409.2 5.7 all-to-all-start
  417.6 4.5 convert_reduce_fusion.4
  422.1 55.5 %attend_back.1 = (bf16[8,256,2048]{2,1,0:T(8,128)(2,1)}, bf16[2048,768]{1,0:T(8,128)(2,1)}) custom-call(bf16[256,2048]{1,0:T(8,128)(2,1)} %get-tuple-element.104.branch_ref, bf16[2048,768]{1,0:T(8,128)(2,1)} %add_convert_fusion.1.head_ref, bf16[256,2048]{1,0:T(8,128)(2,1)} %bitcast.129, f32[2,8,2048]{2,1,0:T(8,128)} %get-tuple-element.71.total_ref, ...), custom_call_target="tpu_custom_call" | custom-call | tf_op jit(solution)/shard_map/attend_back/pallas_call | solution.py:623
  480.7 10.4 %convolution_convert_fusion.2 = bf16[2048,768]{1,0:T(8,128)(2,1)} fusion(bf16[2048,2048]{1,0:T(8,128)(2,1)} %bitcast.108, bf16[2048,768]{1,0:T(8,128)(2,1)S(1)} %copy-done.10), kind=kOutput, calls=%fused_computation.22 | convolution fusion | flops 6444023808 | bytes 14680064 | tf_op jit(solution)/shard_map/dot_general | solution.py:51
  491.1 3.9 copy.73
  495.3 46.4 %product_reduce.4 = f32[256,2048]{1,0:T(8,128)} custom-call(bf16[8,256,768]{2,1,0:T(8,128)(2,1)} %bitcast.125, bf16[2048,768]{1,0:T(8,128)(2,1)} %bitcast.124), custom_call_target="tpu_custom_call" | custom-call | tf_op jit(solution)/shard_map/product_reduce/pallas_call | solution.py:304
  544.5 3.4 fusion.18
  547.8 5.8 convolution_convert_fusion.3
  554.3 13.2 %collective-permute-done.3 = bf16[2,64,2048]{2,1,0:T(8,128)(2,1)S(1)} collective-permute-done((bf16[2,64,2048]{2,1,0:T(8,128)(2,1)S(1)}, bf16[2,64,2048]{2,1,0:T(8,128)(2,1)S(1)}, u32[]{:S(2)}, u32[]{:S(2)}) %collective-permute-start.3) | collective-permute-done | bytes 524320 | tf_op jit(solution)/shard_map/ppermute | solution.py:648
  569.0 5.2 all-to-all-start.1
  574.7 6.0 collective-permute-start.4
  581.3 7.8 %all-to-all-done.1 = bf16[8,64,1024]{2,1,0:T(8,128)(2,1)} async-done(((bf16[8,64,1024]{2,1,0:T(8,128)(2,1)}), bf16[8,64,1024]{2,1,0:T(8,128)(2,1)}, u32[]{:S(2)}, u32[]{:S(2)}) %all-to-all-start.1) | async-done | bytes 1048608 | tf_op jit(solution)/shard_map/all_to_all | solution.py:667
  592.0 52.3 %product_reduce.5 = f32[256,2048]{1,0:T(8,128)} custom-call(bf16[8,256,1024]{2,1,0:T(8,128)(2,1)} %bitcast.131, bf16[2048,1024]{1,0:T(8,128)(2,1)} %bitcast.117), custom_call_target="tpu_custom_call" | custom-call | tf_op jit(solution)/shard_map/product_reduce/pallas_call | solution.py:304
  644.3 5.8 all-to-all-start.2
  653.1 4.6 collective-permute-start.5
  662.2 51.3 %total_everywhere.1 = f32[192,128]{1,0:T(8,128)} custom-call(f32[192,128]{1,0:T(8,128)} %bitcast.151), custom_call_target="tpu_custom_call" | custom-call | tf_op jit(solution)/shard_map/total_everywhere/pallas_call | solution.py:340
  (171 shorter events, 62.2 us)
Async XLA Ops:
  7.2 67.3 %copy-start.20 = (f32[2048]{0:T(1024)S(1)}, f32[2048]{0:T(1024)}, u32[]{:S(2)}) copy-start(f32[2048]{0:T(1024)} %param.18) | copy-start | bytes 24580
  7.2 67.3 %copy-start.27 = (f32[2048]{0:T(1024)S(1)}, f32[2048]{0:T(1024)}, u32[]{:S(2)}) copy-start(f32[2048]{0:T(1024)} %param.19) | copy-start | bytes 24580
  7.2 69.0 %copy-start.32 = (f32[2048]{0:T(1024)S(1)}, f32[2048]{0:T(1024)}, u32[]{:S(2)}) copy-start(f32[2048]{0:T(1024)} %param.21) | copy-start | bytes 24580
  7.2 69.0 %copy-start.31 = (f32[2048]{0:T(1024)S(1)}, f32[2048]{0:T(1024)}, u32[]{:S(2)}) copy-start(f32[2048]{0:T(1024)} %param.22) | copy-start | bytes 24580
  7.2 59.3 %all-gather.5.cloned.1.call-start = ((), (), s32[]{:S(2)}) async-start(), calls=%async_computation.7 | async-start | bytes 1310720 | tf_op jit(solution)/shard_map/all_gather | solution.py:689
  8.0 127.0 %all-gather.7.cloned.1.call-start = ((), (), s32[]{:S(2)}) async-start(), calls=%async_computation.8 | async-start | bytes 3932160 | tf_op jit(solution)/shard_map/all_gather | solution.py:654
  66.6 176.0 %all-gather.9.cloned.1.call-start = ((), (), s32[]{:S(2)}) async-start(), calls=%async_computation.9 | async-start | bytes 5242880 | tf_op jit(solution)/shard_map/all_gather | solution.py:654
  67.3 259.0 %all-gather.11.cloned.1.call-start = ((), (), s32[]{:S(2)}) async-start(), calls=%async_computation.10 | async-start | bytes 5242880 | tf_op jit(solution)/shard_map/all_gather | solution.py:654
  68.1 52.3 %collective-permute-start = (s32[1,2052]{1,0:T(1,128)S(1)}, s32[1,2052]{1,0:T(1,128)S(1)}, u32[]{:S(2)}, u32[]{:S(2)}) collective-permute-start(s32[1,2052]{1,0:T(1,128)S(1)} %pad_add_fusion), channel_id=1, source_target_pairs={{0,0},{1,1},{2,8},{3,9},{4,16},{5,17},{6,24},{7,25},{8,4},{9,5},{1... | collective-permute-start | bytes 24632 | tf_op jit(solution)/shard_map/ppermute | solution.py:684
  71.1 338.1 %reduce-scatter.5.cloned.1.call-start = ((), (), s32[]{:S(2)}) async-start(), calls=%async_computation.11 | async-start | bytes 5242880 | tf_op jit(solution)/shard_map/reduce_scatter | solution.py:663
  72.6 47.8 %copy-start.15 = (bf16[256,2048]{1,0:T(8,128)(2,1)S(1)}, bf16[256,2048]{1,0:T(8,128)(2,1)}, u32[]{:S(2)}) copy-start(bf16[256,2048]{1,0:T(8,128)(2,1)} %all-gather.5.cloned.1.call-done) | copy-start | bytes 3145732
  120.5 13.3 %collective-permute-start.1 = (bf16[2,64,2048]{2,1,0:T(8,128)(2,1)S(1)}, bf16[2,64,2048]{2,1,0:T(8,128)(2,1)S(1)}, u32[]{:S(2)}, u32[]{:S(2)}) collective-permute-start(bf16[2,64,2048]{2,1,0:T(8,128)(2,1)S(1)} %bitcast.147), channel_id=1, source_target_pairs={{0,1},{1,0},{2,3},{3,2},{4,5},{5,4},{6,7},{7,6},{8,9},{9,8},{10,11... | collective-permute-start | bytes 1572872 | tf_op jit(solution)/shard_map/ppermute | solution.py:635
  123.3 119.2 %collective-permute-start.2 = (bf16[256,2048]{1,0:T(8,128)(2,1)}, bf16[256,2048]{1,0:T(8,128)(2,1)S(1)}, u32[]{:S(2)}, u32[]{:S(2)}) collective-permute-start(bf16[256,2048]{1,0:T(8,128)(2,1)} %param.33), channel_id=1, source_target_pairs={{0,0},{1,1},{2,8},{3,9},{4,16},{5,17},{6,24},{7,25},{8,4},{9,5},{1... | collective-permute-start | bytes 3145736 | tf_op jit(solution)/shard_map/ppermute | solution.py:684
  137.2 58.8 %copy-start.28 = (f32[2048]{0:T(1024)S(1)}, f32[2048]{0:T(1024)}, u32[]{:S(2)}) copy-start(f32[2048]{0:T(1024)} %param.24) | copy-start | bytes 24580
  148.9 49.6 %copy-start.19 = (f32[2048]{0:T(1024)S(1)}, f32[2048]{0:T(1024)}, u32[]{:S(2)}) copy-start(f32[2048]{0:T(1024)} %param.25) | copy-start | bytes 24580
  148.9 49.6 %copy-start.29 = (f32[2048]{0:T(1024)S(1)}, f32[2048]{0:T(1024)}, u32[]{:S(2)}) copy-start(f32[2048]{0:T(1024)} %param.26) | copy-start | bytes 24580
  198.1 219.4 %copy-start.4 = (f32[256,2048]{1,0:T(8,128)}, f32[256,2048]{1,0:T(8,128)S(1)}, u32[]{:S(2)}) copy-start(f32[256,2048]{1,0:T(8,128)S(1)} %get-tuple-element.109) | copy-start | bytes 6291460
  245.6 68.4 %copy-start.8 = (bf16[4,4,2,64,1024]{4,3,2,0,1:T(8,128)(2,1)}, bf16[4,4,2,64,1024]{4,3,2,0,1:T(8,128)(2,1)S(1)}, u32[]{:S(2)}) copy-start(bf16[4,4,2,64,1024]{4,3,2,0,1:T(8,128)(2,1)S(1)} %copy.65) | copy-start | bytes 12582916
  326.3 164.8 %reduce-scatter.7.cloned.1.call-start = ((), (), s32[]{:S(2)}) async-start(), calls=%async_computation.12 | async-start | bytes 5242880 | tf_op jit(solution)/shard_map/reduce_scatter | solution.py:663
  409.2 68.4 %all-to-all-start = ((bf16[8,64,1024]{2,1,0:T(8,128)(2,1)}), bf16[8,64,1024]{2,1,0:T(8,128)(2,1)}, u32[]{:S(2)}, u32[]{:S(2)}) async-start(bf16[8,64,1024]{2,1,0:T(8,128)(2,1)} %bitcast.145), calls=%async_computation.1 | async-start | bytes 2097152 | tf_op jit(solution)/shard_map/all_to_all | solution.py:667
  414.9 153.8 %reduce-scatter.9.cloned.1.call-start = ((), (), s32[]{:S(2)}) async-start(), calls=%async_computation.13 | async-start | bytes 3932160 | tf_op jit(solution)/shard_map/reduce_scatter | solution.py:663
  495.0 46.7 %copy-start.26 = (f32[256]{0:T(256)S(1)}, f32[256]{0:T(256)}, u32[]{:S(2)}) copy-start(f32[256]{0:T(256)} %copy-done.25) | copy-start | bytes 3076
  495.0 49.4 %copy-start.12 = (f32[256,2048]{1,0:T(8,128)S(1)}, f32[256,2048]{1,0:T(8,128)}, u32[]{:S(2)}) copy-start(f32[256,2048]{1,0:T(8,128)} %get-tuple-element.105) | copy-start | bytes 6291460
  495.0 155.1 %reduce-scatter.11.cloned.1.call-start = ((), (), s32[]{:S(2)}) async-start(), calls=%async_computation.14 | async-start | bytes 1310720 | tf_op jit(solution)/shard_map/reduce_scatter | solution.py:746
  553.8 13.7 %collective-permute-start.3 = (bf16[2,64,2048]{2,1,0:T(8,128)(2,1)S(1)}, bf16[2,64,2048]{2,1,0:T(8,128)(2,1)S(1)}, u32[]{:S(2)}, u32[]{:S(2)}) collective-permute-start(bf16[2,64,2048]{2,1,0:T(8,128)(2,1)S(1)} %select_bitcast_fusion), channel_id=1, source_target_pairs={{0,1},{1,0},{2,3},{3,2},{4,5},{5,4},{6,7},{7,6},{8,9},{9,8},{10,11... | collective-permute-start | bytes 1572872 | tf_op jit(solution)/shard_map/ppermute | solution.py:648
  569.0 20.1 %all-to-all-start.1 = ((bf16[8,64,1024]{2,1,0:T(8,128)(2,1)}), bf16[8,64,1024]{2,1,0:T(8,128)(2,1)}, u32[]{:S(2)}, u32[]{:S(2)}) async-start(bf16[8,64,1024]{2,1,0:T(8,128)(2,1)} %bitcast.144), calls=%async_computation.5 | async-start | bytes 2097152 | tf_op jit(solution)/shard_map/all_to_all | solution.py:667
  574.7 75.4 %collective-permute-start.4 = (bf16[256,2048]{1,0:T(8,128)(2,1)}, bf16[256,2048]{1,0:T(8,128)(2,1)}, u32[]{:S(2)}, u32[]{:S(2)}) collective-permute-start(bf16[256,2048]{1,0:T(8,128)(2,1)} %fusion.18), channel_id=1, source_target_pairs={{0,0},{1,1},{8,2},{9,3},{16,4},{17,5},{24,6},{25,7},{4,8},{5,9},{1... | collective-permute-start | bytes 3145736 | tf_op jit(solution)/shard_map/ppermute | solution.py:687
  592.0 58.2 %copy-start.5 = (f32[256,2048]{1,0:T(8,128)S(1)}, f32[256,2048]{1,0:T(8,128)}, u32[]{:S(2)}) copy-start(f32[256,2048]{1,0:T(8,128)} %copy-done.4) | copy-start | bytes 6291460
  592.0 58.2 %copy-start.30 = (f32[2048]{0:T(1024)S(1)}, f32[2048]{0:T(1024)}, u32[]{:S(2)}) copy-start(f32[2048]{0:T(1024)} %param.30) | copy-start | bytes 24580
  644.3 16.4 %all-to-all-start.2 = ((bf16[8,64,768]{2,1,0:T(8,128)(2,1)}), bf16[8,64,768]{2,1,0:T(8,128)(2,1)S(1)}, u32[]{:S(2)}, u32[]{:S(2)}) async-start(bf16[8,64,768]{2,1,0:T(8,128)(2,1)} %bitcast.146), calls=%async_computation.6 | async-start | bytes 1572864 | tf_op jit(solution)/shard_map/all_to_all | solution.py:667
  650.2 63.3 %copy-start.16 = (bf16[64,2048]{1,0:T(8,128)(2,1)S(1)}, bf16[64,2048]{1,0:T(8,128)(2,1)}, u32[]{:S(2)}) copy-start(bf16[64,2048]{1,0:T(8,128)(2,1)} %reduce-scatter.11.cloned.1.call-done) | copy-start | bytes 786436
  653.1 64.0 %collective-permute-start.5 = (bf16[256,2048]{1,0:T(8,128)(2,1)}, bf16[256,2048]{1,0:T(8,128)(2,1)S(1)}, u32[]{:S(2)}, u32[]{:S(2)}) collective-permute-start(bf16[256,2048]{1,0:T(8,128)(2,1)} %add_convert_fusion.2), channel_id=1, source_target_pairs={{0,0},{1,1},{8,2},{9,3},{16,4},{17,5},{24,6},{25,7},{4,8},{5,9},{1... | collective-permute-start | bytes 3145736 | tf_op jit(solution)/shard_map/ppermute | solution.py:687
  (20 other events, 374.1 us)
Sparse Core Ops, SparseCore 0:
  9.6 45.9 all-gather.4
  66.7 62.8 all-gather.6
  131.1 90.6 all-gather.8
  223.2 88.1 all-gather.10
  326.4 80.7 reduce-scatter.4
  409.4 80.6 reduce-scatter.6
  495.1 66.9 reduce-scatter.8
  568.8 58.2 reduce-scatter.10

commit v4 on v3

--- a/solution.py
+++ b/solution.py
@@ -17,6 +17,8 @@
 norm_epsilon = 1e-05
 masked_score = -1e+30
 log2_e = 1.4426950408889634
+root_half = 0.7071067811865476
+normal_peak = 0.3989422804014327
 
 def norm_terms(values):
     average = jnp.mean(values, axis=-1, keepdims=True)
@@ -28,9 +30,6 @@
 def norm_back(slope, gain, normal, inverse):
     scaled = slope * gain
     return inverse * (scaled - jnp.mean(scaled, axis=-1, keepdims=True) - normal * jnp.mean(scaled * normal, axis=-1, keepdims=True))
-
-def exact_gelu(values):
-    return jax.nn.gelu(values, approximate=False)
 
 def key_bounds(positions, lengths, prompt):
     segment = (positions - prompt) // CONT
@@ -128,81 +127,172 @@
 def remote(source, target, send, recv, number, device):
     return pltpu.make_async_remote_copy(src_ref=source, dst_ref=target, send_sem=send.at[number], recv_sem=recv.at[number], device_id=device, device_id_type=MESH)
 
-def gather_pieces(slots, send, recv, ids, on_piece):
-    across, up, partner, _ = ids
-    half = slots.shape[1] // 2
-    low, high = (pl.ds(0, half), pl.ds(half, half))
-
-    def copy(number, source, target, device):
-        return remote(slots.at[source], slots.at[target], send, recv, number, device)
-    x0 = copy(0, (0, low), (1, low), across)
-    y1 = copy(1, (0, high), (4, high), up)
-    x1 = copy(2, (0, high), (1, high), across)
-    y0 = copy(3, (0, low), (4, low), up)
-    own = copy(4, 0, 2, partner)
-    started = [x0, y1, own, x1, y0]
-    for one in started:
-        one.start()
-    on_piece(0)
-    own.wait_recv()
-    on_piece(2)
-
-    def forward(number, source, target, device):
-        one = copy(number, source, target, device)
-        one.start()
-        started.append(one)
-        return one
-    x0.wait_recv()
-    d0 = forward(5, (1, low), (5, low), up)
-    y1.wait_recv()
-    d1 = forward(6, (4, high), (5, high), across)
-    x1.wait_recv()
-    px = forward(7, 1, 3, partner)
-    on_piece(1)
-    y0.wait_recv()
-    py = forward(8, 4, 6, partner)
-    on_piece(4)
-    px.wait_recv()
-    on_piece(3)
-    py.wait_recv()
-    on_piece(6)
-    d0.wait_recv()
-    p0 = forward(9, (5, low), (7, low), partner)
-    d1.wait_recv()
-    p1 = forward(10, (5, high), (7, high), partner)
-    on_piece(5)
-    p0.wait_recv()
-    p1.wait_recv()
-    on_piece(7)
-    for one in started:
-        one.wait_send()
-
-def gather_kernel(parts, x_ref, out_ref, slots, load, send, recv, store):
+def plane_peers():
+    groups, _, subs = (lax.axis_size(n) for n in EVERY)
+    g, r, u = (lax.axis_index(n) for n in EVERY)
+    count = groups * subs
+    place = g * subs + u
+    return (place, [(t // subs, r, lax.rem(t, subs)) for t in (lax.rem(place + step, count) for step in range(1, count))])
+
+def owner_cargo(source, target, send, recv, local):
+    count = lax.axis_size('grp') * lax.axis_size('sub')
+    subs = lax.axis_size('sub')
+    rows, width = (target.shape[0], source.shape[1])
+    place, peers = plane_peers()
+
+    def block(t):
+        return source.at[pl.ds(pl.multiple_of(t * rows, rows), rows), :]
+    landing = target.at[:, pl.ds(pl.multiple_of(place * width, width), width)]
+    own = pltpu.make_async_copy(block(place), landing, local)
+    away = [remote(block(device[0] * subs + device[2]), landing, send, recv, number, device) for number, device in enumerate(peers)]
+
+    def start():
+        own.start()
+        for one in away:
+            one.start()
+
+    def finish():
+        own.wait()
+        for one in away:
+            one.wait_recv()
+        for one in away:
+            one.wait_send()
+    return (start, finish)
+
+def owner_scratch():
+    count = lax.axis_size('grp') * lax.axis_size('sub')
+    return [DMA((count - 1,)), DMA((count - 1,)), DMA]
+
+def position_of(turn):
+    groups = lax.axis_size('grp')
+    return lax.rem(turn, 2) * (groups // 2) + turn // 2
+
+def turn_of(position):
+    half = lax.axis_size('grp') // 2
+    return lax.rem(position, half) * 2 + position // half
+
+def home_devices():
+    g, r, u = (lax.axis_index(n) for n in EVERY)
+    groups = lax.axis_size('grp')
+    rep = lax.rem(turn_of(g) + groups - r, groups)
+    return ((r, rep, u), (position_of(lax.rem(g + r, groups)), g, u), (r == g) & (rep == r))
+
+def column_cargo(source, target, send, recv, local):
+    subs = lax.axis_size('sub')
+    rows, width = (source.shape[0], target.shape[1])
+    place, peers = plane_peers()
+
+    def block(t):
+        return source.at[:, pl.ds(pl.multiple_of(t * width, width), width)]
+    landing = target.at[pl.ds(pl.multiple_of(place * rows, rows), rows), :]
+    own = pltpu.make_async_copy(block(place), landing, local)
+    away = [remote(block(device[0] * subs + device[2]), landing, send, recv, number, device) for number, device in enumerate(peers)]
+
+    def start():
+        own.start()
+        for one in away:
+            one.start()
+
+    def finish():
+        own.wait()
+        for one in away:
+            one.wait_recv()
+        for one in away:
+            one.wait_send()
+    return (start, finish)
+
+def column_shape(weight):
+    count = lax.axis_size('grp') * lax.axis_size('sub')
+    return jax.ShapeDtypeStruct((weight.shape[0] * count, weight.shape[1] // count), weight.dtype)
+
+def row_loads(source, target, sem):
+    groups, reps = (lax.axis_size('grp'), lax.axis_size('rep'))
+    rows = source.shape[0] // (groups * reps)
+    return [pltpu.make_async_copy(source.at[pl.ds((r * groups + g) * rows, rows)], target.at[pl.ds((g * reps + r) * rows, rows)], sem.at[g, r]) for g in range(groups) for r in range(reps)]
+
+def row_loads_scratch(shape, dtype):
+    return [pltpu.VMEM(shape, dtype), DMA((lax.axis_size('grp'), lax.axis_size('rep')))]
+
+def home_cargo(source, target, send, recv, local):
+    goal, _, stays = home_devices()
+    kept = pltpu.make_async_copy(source, target, local)
+    moved = pltpu.make_async_remote_copy(src_ref=source, dst_ref=target, send_sem=send, recv_sem=recv, device_id=goal, device_id_type=MESH)
+
+    def start():
+
+        @pl.when(stays)
+        def _():
+            kept.start()
+
+        @pl.when(jnp.logical_not(stays))
+        def _():
+            moved.start()
+
+    def finish():
+
+        @pl.when(stays)
+        def _():
+            kept.wait()
+
+        @pl.when(jnp.logical_not(stays))
+        def _():
+            moved.wait_recv()
+            moved.wait_send()
+    return (start, finish)
+
+def greet_all(devices, homes):
+    barrier = pltpu.get_barrier_semaphore()
+    for device in devices:
+        pl.semaphore_signal(barrier, inc=1, device_id=device, device_id_type=MESH)
+    if not homes:
+        pl.semaphore_wait(barrier, len(devices))
+        return
+    _, origin, stays = home_devices()
+
+    @pl.when(jnp.logical_not(stays))
+    def _():
+        pl.semaphore_signal(barrier, inc=1, device_id=origin, device_id_type=MESH)
+    pl.semaphore_wait(barrier, len(devices) + 1 - stays.astype(jnp.int32))
+
+def gather_kernel(weights, x_ref, *refs):
+    sources, out_ref, landings = (refs[:weights], refs[weights], refs[weights + 1:2 * weights + 1])
+    slots, load, send, recv, store, *cargo = refs[2 * weights + 1:]
     ids = plane_ids()
-    first = pltpu.make_async_copy(x_ref, slots.at[0], load)
-    first.start()
-    greet(ids[:3])
-    first.wait()
-    stores = []
-    small = slots.shape[1] // parts
-
-    def on_piece(k):
-        piece = ids[3](k)
-        for part in range(parts):
-            one = pltpu.make_async_copy(slots.at[k, pl.ds(part * small, small)], out_ref.at[piece // 2, part, lax.rem(piece, 2)], store.at[k, part])
-            one.start()
-            stores.append(one)
-    gather_pieces(slots, send, recv, ids, on_piece)
-    for one in stores:
-        one.wait()
-
-def plane_gather(x, collective_id, parts=1):
+    step = pl.program_id(0)
+    cargos = [column_cargo(sources[i], landings[i], *cargo[3 * i:3 * i + 3]) for i in range(weights)]
+
+    @pl.when(step == 0)
+    def _():
+        first = pltpu.make_async_copy(x_ref, slots.at[0], load)
+        first.start()
+        greet(plane_peers()[1] if weights else ids[:3])
+        first.wait()
+    gather_step(step, slots, send, recv, ids)
+
+    def keep(number):
+        return pltpu.make_async_copy(slots.at[number], out_ref.at[ids[3](number)], store.at[number])
+    keep(gather_order(step)).start()
+    if weights:
+
+        @pl.when(step == 2)
+        def _():
+            for start, _ in cargos:
+                start()
+
+    @pl.when(step == 7)
+    def _():
+        for _, finish in cargos:
+            finish()
+        for number in range(8):
+            keep(number).wait()
+
+def plane_gather(x, weights, collective_id):
     rows, width = x.shape
-    groups, _, subs = (lax.axis_size(n) for n in EVERY)
     if not small_plane():
-        every = lax.all_gather(x, PLANE, axis=0).reshape(groups, subs, parts, rows // parts, width)
-        return every.transpose(0, 2, 1, 3, 4).reshape(-1, width)
-    return pl.pallas_call(functools.partial(gather_kernel, parts), out_shape=jax.ShapeDtypeStruct((groups, parts, subs, rows // parts, width), x.dtype), in_specs=[ANY], out_specs=ANY, scratch_shapes=[pltpu.VMEM((8, rows, width), x.dtype), DMA, DMA((11,)), DMA((11,)), DMA((8, parts))], compiler_params=pltpu.CompilerParams(collective_id=collective_id, has_side_effects=True, vmem_limit_bytes=40 * MIB), name='plane_gather')(x).reshape(-1, width)
+        return [lax.all_gather(x, PLANE, axis=0, tiled=True)] + [exchange(w, False, collective_id + 20 + i) for i, w in enumerate(weights)]
+    number = len(weights)
+    every, *columns = pl.pallas_call(functools.partial(gather_kernel, number), grid=(8,), out_shape=[jax.ShapeDtypeStruct((8, rows, width), x.dtype)] + [column_shape(w) for w in weights], in_specs=[ANY] * (1 + number), out_specs=[ANY] * (1 + number), scratch_shapes=[pltpu.VMEM((8, rows, width), x.dtype), DMA, DMA((11,)), DMA((11,)), DMA((8,))] + owner_scratch() * number, compiler_params=remote_params(collective_id, 40), name='plane_gather')(x, *weights)
+    return [every.reshape(8 * rows, width)] + columns
 
 def reduce_scratch(rows, width):
     wide, narrow = (jnp.float32, jnp.bfloat16)
@@ -211,7 +301,7 @@
 def reduce_order(step):
     return 7 - 2 * step + 7 * (step // 4)
 
-def reduce_step(step, piece, refs, ids, out):
+def reduce_step(step, piece, refs, ids, out, before=None):
     sums, give, take, leave, come, send, recv = refs
     across, up, partner, _ = ids
     half = sums.shape[1] // 2
@@ -238,6 +328,11 @@
     @pl.when(lax.rem(step, 2) == 1)
     def _():
         sums[pair] = piece
+    if before is not None:
+        before()
+
+    @pl.when(lax.rem(step, 2) == 1)
+    def _():
         to_partner(pair).wait_recv()
         sums[pair] += up_cast(take[pair])
     diagonal_across, diagonal_up = (part(4, 2, low, across), part(5, 2, high, up))
@@ -276,42 +371,85 @@
         for one in (diagonal_across, diagonal_up, across_low, up_high, across_high, up_low):
             one.wait_send()
 
-def product_reduce_kernel(slope_ref, weight_ref, out_ref, slopes, load, *refs):
+def product_reduce_kernel(owns, homes, slope_ref, weight_ref, *refs):
     ids = plane_ids()
     step = pl.program_id(0)
+    refs = list(refs)
+    parcels = [refs.pop(0) for _ in range(owns + homes)]
+    out_ref = refs.pop(0)
+    landings = [refs.pop(0) for _ in range(owns + homes)]
+    slopes, load, weight, weight_load, *refs = refs
+    tail = refs[7:]
+    rows_in = row_loads(weight_ref, weight, weight_load)
+    early, late = ([], [])
+    if owns:
+        late.append(owner_cargo(parcels[0], landings[0], *tail[:3]))
+    if homes:
+        early.append(home_cargo(parcels[-1], landings[-1], *tail[-3:]))
 
     def fetch(number):
         return pltpu.make_async_copy(slope_ref.at[ids[3](number)], slopes.at[number], load.at[number])
 
     @pl.when(step == 0)
     def _():
-        for early in range(8):
-            fetch(reduce_order(early)).start()
-        greet(ids[:3])
+        for one in rows_in:
+            one.start()
+        for number in range(8):
+            fetch(reduce_order(number)).start()
+        greet_all(plane_peers()[1] if owns else ids[:3], homes)
+        for start, _ in early:
+            start()
+        for one in rows_in:
+            one.wait()
     k = reduce_order(step)
     fetch(k).wait()
-    reduce_step(step, product_transposed(slopes[k], weight_ref[...]), refs, ids, out_ref)
+    reduce_step(step, product_transposed(slopes[k], weight[...]), refs[:7], ids, out_ref)
+    if owns:
+
+        @pl.when(step == 5)
+        def _():
+            for start, _ in late:
+                start()
+    if owns or homes:
+
+        @pl.when(step == 7)
+        def _():
+            for _, finish in late + early:
+                finish()
 
 def remote_params(collective_id, limit):
     return pltpu.CompilerParams(collective_id=collective_id, has_side_effects=True, vmem_limit_bytes=limit * MIB)
 
-def product_reduce(slopes, weight, collective_id):
+def owner_shape(parcel):
+    count = lax.axis_size('grp') * lax.axis_size('sub')
+    return jax.ShapeDtypeStruct((parcel.shape[0] // count, parcel.shape[1] * count), parcel.dtype)
+
+def product_reduce(slopes, weight, owned, homed, collective_id):
     count, rows, inner = slopes.shape
     width = weight.shape[0]
+    owns, homes = (owned is not None, homed is not None)
     if not small_plane():
-        part = product_transposed(slopes.reshape(-1, inner), weight)
-        return lax.psum_scatter(part.astype(jnp.bfloat16), PLANE, scatter_dimension=0, tiled=True).astype(jnp.float32)
-    return pl.pallas_call(product_reduce_kernel, grid=(8,), out_shape=jax.ShapeDtypeStruct((rows, width), jnp.float32), in_specs=[ANY, VMEM], out_specs=VMEM, scratch_shapes=[pltpu.VMEM((8, rows, inner), slopes.dtype), DMA((8,)), *reduce_scratch(rows, width)], compiler_params=remote_params(collective_id, 60), name='product_reduce')(slopes, weight)
-
-def total_kernel(x_ref, out_ref, *refs):
-    axes = ('grp', 'rep', 'sub')
-    here = {n: lax.axis_index(n) for n in axes}
+        part = product_transposed(slopes.reshape(-1, inner), rep_rows_last(weight))
+        whole = [lax.psum_scatter(part.astype(jnp.bfloat16), PLANE, scatter_dimension=0, tiled=True).astype(jnp.float32)]
+        return whole + ([exchange(owned, True, collective_id)] if owns else []) + ([from_plane(homed)] if homes else [])
+    cargo = ([owned] if owns else []) + ([homed] if homes else [])
+    shapes = ([owner_shape(owned)] if owns else []) + ([jax.ShapeDtypeStruct(homed.shape, homed.dtype)] if homes else [])
+    return pl.pallas_call(functools.partial(product_reduce_kernel, owns, homes), grid=(8,), out_shape=[jax.ShapeDtypeStruct((rows, width), jnp.float32)] + shapes, in_specs=[ANY, ANY] + [ANY] * len(cargo), out_specs=[VMEM] + [ANY] * len(cargo), scratch_shapes=[pltpu.VMEM((8, rows, inner), slopes.dtype), DMA((8,)), *row_loads_scratch(weight.shape, weight.dtype), *reduce_scratch(rows, width)] + (owner_scratch() if owns else []) + ([DMA, DMA, DMA] if homes else []), compiler_params=remote_params(collective_id, 60), name='product_reduce')(slopes, weight, *cargo)
+
+def closing_kernel(number, x_ref, homed_ref, *refs):
+    owned_refs, (out_ref, homed_out), owned_outs = (refs[:number], refs[number:number + 2], refs[number + 2:2 * number + 2])
+    refs = refs[2 * number + 2:]
+    here = {n: lax.axis_index(n) for n in EVERY}
     phases = ('grp', 'sub', 'rep')
+    home_start, home_finish = home_cargo(homed_ref, homed_out, *refs[:3])
+    owners = [owner_cargo(owned_refs[i], owned_outs[i], *refs[3 + 3 * i:6 + 3 * i]) for i in range(number)]
+    refs = refs[3 + 3 * number:]
 
     def other(name, step):
         size = lax.axis_size(name)
-        return tuple((lax.rem(here[n] + step, size) if n == name else here[n] for n in axes))
-    greet([other(n, s) for n in phases for s in range(1, lax.axis_size(n))])
+        return tuple((lax.rem(here[n] + step, size) if n == name else here[n] for n in EVERY))
+    greet_all(plane_peers()[1] + [other('rep', s) for s in range(1, lax.axis_size('rep'))], True)
+    home_start()
     out_ref[...] = x_ref[...]
     for j, name in enumerate(phases):
         slots, send, recv = refs[3 * j:3 * j + 3]
@@ -323,6 +461,9 @@
             one = pltpu.make_async_remote_copy(src_ref=out_ref, dst_ref=slots.at[me], send_sem=send.at[s], recv_sem=recv.at[s], device_id=other(name, s), device_id_type=MESH)
             one.start()
             copies.append(one)
+        if name == 'rep':
+            for start, _ in owners:
+                start()
         for one in copies:
             one.wait_recv()
         for one in copies:
@@ -331,13 +472,17 @@
         for s in range(1, size):
             value = value + slots[s]
         out_ref[...] = value
-
-def total_everywhere(x, collective_id):
+    for _, finish in owners:
+        finish()
+    home_finish()
+
+def closing(x, homed, owned, collective_id):
     scratch = []
     for name in ('grp', 'sub', 'rep'):
         n = lax.axis_size(name)
         scratch += [pltpu.VMEM((n,) + x.shape, x.dtype), DMA((n,)), DMA((n,))]
-    return pl.pallas_call(total_kernel, out_shape=jax.ShapeDtypeStruct(x.shape, x.dtype), in_specs=[VMEM], out_specs=VMEM, scratch_shapes=scratch, compiler_params=pltpu.CompilerParams(collective_id=collective_id, has_side_effects=True), name='total_everywhere')(x)
+    number = len(owned)
+    return pl.pallas_call(functools.partial(closing_kernel, number), out_shape=[jax.ShapeDtypeStruct(x.shape, x.dtype), jax.ShapeDtypeStruct(homed.shape, homed.dtype)] + [owner_shape(one) for one in owned], in_specs=[VMEM] + [ANY] * (1 + number), out_specs=[VMEM] + [ANY] * (1 + number), scratch_shapes=[DMA, DMA, DMA] + owner_scratch() * number + scratch, compiler_params=pltpu.CompilerParams(collective_id=collective_id, has_side_effects=True), name='closing')(x, homed, *owned)
 
 def exchange_kernel(to_tokens, x_ref, out_ref, send, recv, local):
     groups, reps, subs = (lax.axis_size(n) for n in EVERY)
@@ -378,28 +523,15 @@
     shape = (x.shape[0] // count, x.shape[1] * count) if to_tokens else (x.shape[0] * count, x.shape[1] // count)
     return pl.pallas_call(functools.partial(exchange_kernel, to_tokens), out_shape=jax.ShapeDtypeStruct(shape, x.dtype), in_specs=[ANY], out_specs=ANY, scratch_shapes=[DMA((count - 1,)), DMA((count - 1,)), DMA], compiler_params=pltpu.CompilerParams(collective_id=collective_id, has_side_effects=True), name='to_tokens' if to_tokens else 'to_heads')(x)
 
-def plane_of(group):
-    groups = lax.axis_size('grp')
-    return lax.rem(group, 2) * (groups // 2) + group // 2
-
-def group_of(plane):
-    groups = lax.axis_size('grp')
-    return lax.rem(plane, groups // 2) * 2 + plane // (groups // 2)
-
 def opening_kernel(x_ref, *refs):
-    count = lax.axis_size('grp') * lax.axis_size('sub')
-    weights = (len(refs) - 6) // 2
+    weights = (len(refs) - 8) // 2
     sources, (moved_ref, *landings) = (refs[:weights], refs[weights:2 * weights + 1])
-    move_send, move_recv, send, recv, local = refs[2 * weights + 1:]
-    subs = lax.axis_size('sub')
+    transit, move_send, move_recv, move_local, send, recv, local = refs[2 * weights + 1:]
+    groups, _, subs = (lax.axis_size(n) for n in EVERY)
     g, r, u = (lax.axis_index(n) for n in EVERY)
-    place = g * subs + u
-    peers = [lax.rem(place + step, count) for step in range(1, count)]
-
-    def device(t):
-        return (t // subs, r, lax.rem(t, subs))
-    target, source = ((r, plane_of(g), u), (group_of(r), g, u))
-    stays = (r == g) & (plane_of(g) == r)
+    place, peers = plane_peers()
+    relay = position_of(lax.rem(g + r, groups))
+    beyond = lax.rem(turn_of(g) + groups - r, groups)
 
     def block(number, t):
         width = landings[number].shape[1]
@@ -408,54 +540,74 @@
     def landing(number):
         rows = sources[number].shape[0]
         return landings[number].at[pl.ds(pl.multiple_of(place * rows, rows), rows), :]
+
+    def hop(number, source, target, device, stays):
+        kept = pltpu.make_async_copy(source, target, move_local.at[number])
+        moved = remote(source, target, move_send, move_recv, number, device)
+
+        def start():
+
+            @pl.when(stays)
+            def _():
+                kept.start()
+
+            @pl.when(jnp.logical_not(stays))
+            def _():
+                moved.start()
+
+        def arrive():
+
+            @pl.when(stays)
+            def _():
+                kept.wait()
+
+            @pl.when(jnp.logical_not(stays))
+            def _():
+                moved.wait_recv()
+
+        def leave():
+
+            @pl.when(jnp.logical_not(stays))
+            def _():
+                moved.wait_send()
+        return (start, arrive, leave)
+    first = hop(0, x_ref, transit, (relay, r, u), relay == g)
+    second = hop(1, transit, moved_ref, (g, beyond, u), beyond == r)
     owns = [pltpu.make_async_copy(block(number, place), landing(number), local.at[number]) for number in range(weights)]
     for one in owns:
         one.start()
-    kept = pltpu.make_async_copy(x_ref, moved_ref, local.at[weights])
-    moved = pltpu.make_async_remote_copy(src_ref=x_ref, dst_ref=moved_ref, send_sem=move_send, recv_sem=move_recv, device_id=target, device_id_type=MESH)
     barrier = pltpu.get_barrier_semaphore()
-    for t in peers:
-        pl.semaphore_signal(barrier, inc=1, device_id=device(t), device_id_type=MESH)
-
-    @pl.when(stays)
-    def _():
-        kept.start()
-
-    @pl.when(jnp.logical_not(stays))
-    def _():
-        pl.semaphore_signal(barrier, inc=1, device_id=source, device_id_type=MESH)
-    pl.semaphore_wait(barrier, count - stays.astype(jnp.int32))
-
-    @pl.when(jnp.logical_not(stays))
-    def _():
-        moved.start()
+    for device in peers:
+        pl.semaphore_signal(barrier, inc=1, device_id=device, device_id_type=MESH)
+
+    @pl.when(beyond != r)
+    def _():
+        pl.semaphore_signal(barrier, inc=1, device_id=(g, beyond, u), device_id_type=MESH)
+    pl.semaphore_wait(barrier, len(peers) + (beyond != r).astype(jnp.int32))
+    first[0]()
     copies = []
     for number in range(weights):
-        for step, t in enumerate(peers):
-            one = pltpu.make_async_remote_copy(src_ref=block(number, t), dst_ref=landing(number), send_sem=send.at[number, step], recv_sem=recv.at[number, step], device_id=device(t), device_id_type=MESH)
+        for step, device in enumerate(peers):
+            one = pltpu.make_async_remote_copy(src_ref=block(number, device[0] * subs + device[2]), dst_ref=landing(number), send_sem=send.at[number, step], recv_sem=recv.at[number, step], device_id=device, device_id_type=MESH)
             one.start()
             copies.append(one)
+    first[1]()
+    second[0]()
     for one in owns:
         one.wait()
     for one in copies:
         one.wait_recv()
     for one in copies:
         one.wait_send()
-
-    @pl.when(stays)
-    def _():
-        kept.wait()
-
-    @pl.when(jnp.logical_not(stays))
-    def _():
-        moved.wait_recv()
-        moved.wait_send()
+    first[2]()
+    second[1]()
+    second[2]()
 
 def opening(x, weights, collective_id):
     count = lax.axis_size('grp') * lax.axis_size('sub')
     number = len(weights)
     columns = [jax.ShapeDtypeStruct((w.shape[0] * count, w.shape[1] // count), w.dtype) for w in weights]
-    return pl.pallas_call(opening_kernel, out_shape=[jax.ShapeDtypeStruct(x.shape, x.dtype), *columns], in_specs=[VMEM] + [ANY] * number, out_specs=[VMEM] + [ANY] * number, scratch_shapes=[DMA, DMA, DMA((number, count - 1)), DMA((number, count - 1)), DMA((number + 1,))], compiler_params=pltpu.CompilerParams(collective_id=collective_id, has_side_effects=True), name='opening')(x, *weights)
+    return pl.pallas_call(opening_kernel, out_shape=[jax.ShapeDtypeStruct(x.shape, x.dtype), *columns], in_specs=[VMEM] + [ANY] * number, out_specs=[VMEM] + [ANY] * number, scratch_shapes=[pltpu.VMEM(x.shape, x.dtype), DMA((2,)), DMA((2,)), DMA((2,)), DMA((number, count - 1)), DMA((number, count - 1)), DMA((number,))], compiler_params=pltpu.CompilerParams(collective_id=collective_id, has_side_effects=True), name='opening')(x, *weights)
 
 def attend_kernel(heads, head_ref, place_ref, first_ref, last_ref, mixing_ref, attended_ref, total_ref, out_ref, *refs):
     ids = plane_ids()
@@ -560,9 +712,10 @@
         for one in (across_low, up_high, across_high, up_low, own, far_low, far_high, pass_across, pass_up, pass_low, pass_high):
             one.wait_send()
 
-def attend_back_kernel(heads, branch_ref, head_ref, mixing_ref, total_ref, place_ref, first_ref, last_ref, every_ref, out_ref, turned, key_sum, value_sum, slots, load, send, recv, store):
+def attend_back_kernel(heads, branch_ref, owned_ref, head_ref, mixing_ref, attended_ref, total_ref, place_ref, first_ref, last_ref, part_ref, out_ref, owned_out, turned, key_sum, value_sum, part_sum, slots, load, send, recv, *cargo):
     ids = plane_ids()
     step = pl.program_id(0)
+    start, finish = owner_cargo(owned_ref, owned_out, *cargo)
     rows = slots.shape[1]
     size = head_ref.shape[1] // (3 * heads)
     scale = size ** (-0.5)
@@ -576,16 +729,17 @@
             turned[h] = head_ref[:, (3 * h + 1) * size:(3 * h + 2) * size].T
         key_sum[...] = jnp.zeros_like(key_sum)
         value_sum[...] = jnp.zeros_like(value_sum)
-        greet(ids[:3])
+        part_sum[...] = jnp.zeros_like(part_sum)
+        greet(plane_peers()[1])
         first.wait()
     gather_step(step, slots, send, recv, ids)
     k = gather_order(step)
-    place_of = ids[3](k)
-
-    def keep(number):
-        return pltpu.make_async_copy(slots.at[number], every_ref.at[ids[3](number)], store.at[number])
-    keep(k).start()
-    here = pl.ds(pl.multiple_of(place_of * rows, rows), rows)
+
+    @pl.when(step == 4)
+    def _():
+        start()
+    here = pl.ds(pl.multiple_of(ids[3](k) * rows, rows), rows)
+    part_sum[...] += row_outer(attended_ref[here, :], slots[k])
     slopes = product_transposed(slots[k], mixing_ref[...]).astype(jnp.bfloat16)
     place = place_ref[:, here]
     allowed = (first_ref[...] <= place) & (place <= last_ref[...])
@@ -609,19 +763,232 @@
         for h in range(heads):
             out_ref[:, (3 * h + 1) * size:(3 * h + 2) * size] = (key_sum[h] * scale).astype(jnp.bfloat16)
             out_ref[:, (3 * h + 2) * size:(3 * h + 3) * size] = value_sum[h].astype(jnp.bfloat16)
-        for number in range(8):
-            keep(number).wait()
-
-def attend_back(branch_slope, packed, mixing, totals, places, key_last, heads, collective_id):
+        part_ref[...] = part_sum[...].astype(jnp.bfloat16)
+        finish()
+
+def attend_back(branch_slope, owned, packed, mixing, attended, totals, places, key_last, heads, collective_id):
     rows, columns = packed.shape
     token_rows, width = branch_slope.shape
     size = columns // (3 * heads)
     if not small_plane():
         every = lax.all_gather(branch_slope, PLANE, axis=0, tiled=True)
         slopes = product_transposed(every, mixing).astype(jnp.bfloat16)
-        return (every, attention_backward(packed, totals, slopes, places, key_last, heads))
-    every, slopes = pl.pallas_call(functools.partial(attend_back_kernel, heads), grid=(8,), out_shape=[jax.ShapeDtypeStruct((8, token_rows, width), jnp.bfloat16), jax.ShapeDtypeStruct((rows, columns), jnp.bfloat16)], in_specs=[ANY] + [VMEM] * 6, out_specs=[ANY, VMEM], scratch_shapes=[pltpu.VMEM((heads, size, rows), jnp.bfloat16), pltpu.VMEM((heads, rows, size), jnp.float32), pltpu.VMEM((heads, rows, size), jnp.float32), pltpu.VMEM((8, token_rows, width), jnp.bfloat16), DMA, DMA((11,)), DMA((11,)), DMA((8,))], compiler_params=remote_params(collective_id, 62), name='attend_back')(branch_slope, packed, mixing, totals, places[None, :], places[:, None], key_last[:, None])
-    return (every.reshape(rows, width), slopes)
+        part = row_outer(attended, every).astype(jnp.bfloat16)
+        slopes = attention_backward(packed, totals, slopes, places, key_last, heads)
+        return (part, slopes, exchange(owned, True, collective_id))
+    return pl.pallas_call(functools.partial(attend_back_kernel, heads), grid=(8,), out_shape=[jax.ShapeDtypeStruct(mixing.shape, jnp.bfloat16), jax.ShapeDtypeStruct((rows, columns), jnp.bfloat16), owner_shape(owned)], in_specs=[ANY] * 2 + [VMEM] * 7, out_specs=[VMEM, VMEM, ANY], scratch_shapes=[pltpu.VMEM((heads, size, rows), jnp.bfloat16), pltpu.VMEM((heads, rows, size), jnp.float32), pltpu.VMEM((heads, rows, size), jnp.float32), pltpu.VMEM(mixing.shape, jnp.float32), pltpu.VMEM((8, token_rows, width), jnp.bfloat16), DMA, DMA((11,)), DMA((11,)), *owner_scratch()], compiler_params=remote_params(collective_id, 62), name='attend_back')(branch_slope, owned, packed, mixing, attended, totals, places[None, :], places[:, None], key_last[:, None])
+
+def add_outer(total, left, right):
+    turned = left.T
+    for first in range(0, total.shape[1], 256):
+        here = pl.ds(first, 256)
+        total[:, here] += product(turned, right[:, first:first + 256])
+
+def rep_order(total, narrow, part_ref, sem):
+    groups, reps = (lax.axis_size('grp'), lax.axis_size('rep'))
+    rows = total.shape[0] // (groups * reps)
+    for g in range(groups):
+        for r in range(reps):
+            come, go = (pl.ds((g * reps + r) * rows, rows), pl.ds((r * groups + g) * rows, rows))
+            narrow[come, :] = total[come, :].astype(jnp.bfloat16)
+            pltpu.make_async_copy(narrow.at[come], part_ref.at[go], sem.at[g, r]).start()
+
+def rep_order_wait(narrow, part_ref, sem):
+    groups, reps = (lax.axis_size('grp'), lax.axis_size('rep'))
+    rows = narrow.shape[0] // (groups * reps)
+    for g in range(groups):
+        for r in range(reps):
+            come, go = (pl.ds((g * reps + r) * rows, rows), pl.ds((r * groups + g) * rows, rows))
+            pltpu.make_async_copy(narrow.at[come], part_ref.at[go], sem.at[g, r]).wait()
+
+def hidden_kernel(middle_ref, cotangent_ref, expand_ref, offset_ref, every_ref, active_ref, rise_ref, part_ref, slots, cotangents, actives, rises, total, load, send, recv, store, fetch_cotangent, active_store, rise_store, expand, expand_load, narrow, part_store):
+    ids = plane_ids()
+    step = pl.program_id(0)
+    turn = lax.rem(step, 2)
+
+    def fetch(number, side):
+        return pltpu.make_async_copy(cotangent_ref.at[ids[3](gather_order(number))], cotangents.at[side], fetch_cotangent.at[side])
+
+    @pl.when(step == 0)
+    def _():
+        first = pltpu.make_async_copy(middle_ref, slots.at[0], load)
+        first.start()
+        rows_in = row_loads(expand_ref, expand, expand_load)
+        for one in rows_in:
+            one.start()
+        fetch(0, 0).start()
+        total[...] = jnp.zeros_like(total)
+        greet(ids[:3])
+        first.wait()
+        for one in rows_in:
+            one.wait()
+    gather_step(step, slots, send, recv, ids)
+    k = gather_order(step)
+
+    def keep(number):
+        return pltpu.make_async_copy(slots.at[number], every_ref.at[ids[3](number)], store.at[number])
+
+    def put(number, side):
+        piece = ids[3](number)
+        return (pltpu.make_async_copy(actives.at[side], active_ref.at[piece], active_store.at[side]), pltpu.make_async_copy(rises.at[side], rise_ref.at[piece], rise_store.at[side]))
+    keep(k).start()
+
+    @pl.when(step >= 2)
+    def _():
+        for one in put(k, turn):
+            one.wait()
+    expanded = product(slots[k], expand[...]) + offset_ref[...]
+    below = 0.5 * (1.0 + lax.erf(expanded * root_half))
+    actives[turn] = (expanded * below).astype(jnp.bfloat16)
+    rises[turn] = below + expanded * (jnp.exp(-0.5 * expanded * expanded) * normal_peak)
+    for one in put(k, turn):
+        one.start()
+    fetch(step, turn).wait()
+
+    @pl.when(step < 7)
+    def _():
+        fetch(step + 1, 1 - turn).start()
+    add_outer(total, cotangents[turn], actives[turn])
+
+    @pl.when(step == 7)
+    def _():
+        rep_order(total, narrow, part_ref, part_store)
+        for late in range(2):
+            for one in put(k, late):
+                one.wait()
+        for number in range(8):
+            keep(number).wait()
+        rep_order_wait(narrow, part_ref, part_store)
+
+def hidden(middle, cotangent_all, expand_slice, offset, collective_id):
+    rows, width = middle.shape
+    count = lax.axis_size('grp') * lax.axis_size('sub')
+    inner = expand_slice.shape[1]
+    if not small_plane():
+        every = lax.all_gather(middle, PLANE, axis=0, tiled=True)
+        expanded = product(every, rep_rows_last(expand_slice)) + offset
+        below = 0.5 * (1.0 + lax.erf(expanded * root_half))
+        rise = below + expanded * (jnp.exp(-0.5 * expanded * expanded) * normal_peak)
+        active = (expanded * below).astype(jnp.bfloat16)
+        return (every, active, rise, rep_rows_first(row_outer(cotangent_all, active)))
+    every, active, rise, part = pl.pallas_call(hidden_kernel, grid=(8,), out_shape=[jax.ShapeDtypeStruct((8, rows, width), middle.dtype), jax.ShapeDtypeStruct((8, rows, inner), jnp.bfloat16), jax.ShapeDtypeStruct((8, rows, inner), jnp.float32), jax.ShapeDtypeStruct((width, inner), jnp.bfloat16)], in_specs=[ANY, ANY, ANY, VMEM], out_specs=[ANY] * 4, scratch_shapes=[pltpu.VMEM((8, rows, width), middle.dtype), pltpu.VMEM((2, rows, width), jnp.bfloat16), pltpu.VMEM((2, rows, inner), jnp.bfloat16), pltpu.VMEM((2, rows, inner), jnp.float32), pltpu.VMEM((width, inner), jnp.float32), DMA, DMA((11,)), DMA((11,)), DMA((8,)), DMA((2,)), DMA((2,)), DMA((2,)), *row_loads_scratch(expand_slice.shape, expand_slice.dtype), *row_loads_scratch(expand_slice.shape, jnp.bfloat16)], compiler_params=remote_params(collective_id, 60), name='hidden')(middle, cotangent_all.reshape(8, rows, width), expand_slice, offset[None, :])
+    return (every.reshape(count * rows, width), active.reshape(count * rows, inner), rise.reshape(count * rows, inner), part)
+
+def hidden_back_kernel(cotangent_ref, middle_ref, rise_ref, shrink_ref, expand_ref, slope_ref, out_ref, part_ref, cotangents, middles, rises, slopes, total, fetches, store, shrink, shrink_load, expand, expand_load, narrow, part_store, *refs):
+    ids = plane_ids()
+    step = pl.program_id(0)
+
+    def fetch(number, side):
+        piece = ids[3](reduce_order(number))
+        return [pltpu.make_async_copy(source.at[piece], target.at[side], fetches.at[kind, side]) for kind, (source, target) in enumerate(((cotangent_ref, cotangents), (rise_ref, rises), (middle_ref, middles)))]
+
+    def put(number, side):
+        return pltpu.make_async_copy(slopes.at[side], slope_ref.at[ids[3](reduce_order(number))], store.at[side])
+    turn = lax.rem(step, 2)
+
+    @pl.when(step == 0)
+    def _():
+        rows_in = row_loads(shrink_ref, shrink, shrink_load) + row_loads(expand_ref, expand, expand_load)
+        for one in rows_in:
+            one.start()
+        for one in fetch(0, 0):
+            one.start()
+        total[...] = jnp.zeros_like(total)
+        greet(ids[:3])
+        for one in rows_in:
+            one.wait()
+    for one in fetch(step, turn):
+        one.wait()
+
+    @pl.when(step < 7)
+    def _():
+        for one in fetch(step + 1, 1 - turn):
+            one.start()
+
+    @pl.when(step >= 2)
+    def _():
+        put(step, turn).wait()
+    slope = product(cotangents[turn], shrink[...]) * rises[turn]
+    slopes[turn] = slope.astype(jnp.bfloat16)
+    put(step, turn).start()
+
+    def before():
+        add_outer(total, middles[turn], slopes[turn])
+
+        @pl.when(step == 7)
+        def _():
+            rep_order(total, narrow, part_ref, part_store)
+    reduce_step(step, product_transposed(slopes[turn], expand[...]), refs, ids, out_ref, before)
+
+    @pl.when(step == 7)
+    def _():
+        put(6, 0).wait()
+        put(7, 1).wait()
+        rep_order_wait(narrow, part_ref, part_store)
+
+def hidden_back(cotangent_all, middle_all, rise, shrink_slice, expand_slice, token_rows, collective_id):
+    rows, width = cotangent_all.shape
+    inner = shrink_slice.shape[1]
+    if not small_plane():
+        slope = (product(cotangent_all, rep_rows_last(shrink_slice)) * rise).astype(jnp.bfloat16)
+        part = product_transposed(slope, rep_rows_last(expand_slice)).astype(jnp.bfloat16)
+        normed = lax.psum_scatter(part, PLANE, scatter_dimension=0, tiled=True).astype(jnp.float32)
+        return (slope, normed, rep_rows_first(row_outer(middle_all, slope)))
+    pieces = (8, token_rows, width)
+    slope, normed, part = pl.pallas_call(hidden_back_kernel, grid=(8,), out_shape=[jax.ShapeDtypeStruct((8, token_rows, inner), jnp.bfloat16), jax.ShapeDtypeStruct((token_rows, width), jnp.float32), jax.ShapeDtypeStruct((width, inner), jnp.bfloat16)], in_specs=[ANY] * 5, out_specs=[ANY, VMEM, ANY], scratch_shapes=[pltpu.VMEM((2, token_rows, width), jnp.bfloat16), pltpu.VMEM((2, token_rows, width), jnp.bfloat16), pltpu.VMEM((2, token_rows, inner), jnp.float32), pltpu.VMEM((2, token_rows, inner), jnp.bfloat16), pltpu.VMEM((width, inner), jnp.float32), DMA((3, 2)), DMA((2,)), *row_loads_scratch(shrink_slice.shape, shrink_slice.dtype), *row_loads_scratch(expand_slice.shape, expand_slice.dtype), *row_loads_scratch(expand_slice.shape, jnp.bfloat16), *reduce_scratch(token_rows, width)], compiler_params=remote_params(collective_id, 63), name='hidden_back')(cotangent_all.reshape(pieces), middle_all.reshape(pieces), rise.reshape(8, token_rows, inner), shrink_slice, expand_slice)
+    return (slope.reshape(rows, inner), normed, part)
+
+def plane_moves():
+    groups, reps, subs = (lax.axis_size(n) for n in EVERY)
+    moves = []
+    for g in range(groups):
+        for r in range(reps):
+            turn = (g + r) % groups
+            position = turn % 2 * (groups // 2) + turn // 2
+            for u in range(subs):
+                moves.append(tuple(((a * reps + b) * subs + u for a, b in ((g, r), (position, r), (position, g)))))
+    return moves
+
+def to_door(array):
+    return lax.ppermute(array, EVERY, [(home, door) for home, door, _ in plane_moves()])
+
+def to_keeper(array):
+    return lax.ppermute(array, EVERY, [(door, away) for _, door, away in plane_moves()])
+
+def to_plane_at_once(array):
+    return lax.ppermute(array, EVERY, [(home, away) for home, _, away in plane_moves()])
+
+def from_plane(array):
+    return lax.ppermute(array, EVERY, [(away, home) for home, _, away in plane_moves()])
+
+def plane_order(places):
+    groups = lax.axis_size('grp')
+    blocks = jnp.roll(places.reshape(groups, -1), lax.axis_index('rep'), axis=0)
+    return blocks.reshape(groups // 2, 2, -1).transpose(1, 0, 2).reshape(-1)
+
+def rep_rows(own):
+    return lax.all_gather(own, 'rep', axis=0, tiled=True)
+
+def rep_rows_last(every):
+    groups, reps, subs = (lax.axis_size(name) for name in EVERY)
+    columns = every.shape[1]
+    ordered = every.reshape(reps, groups, subs, -1, columns).transpose(1, 0, 2, 3, 4)
+    return ordered.reshape(-1, columns)
+
+def rep_rows_first(gradient):
+    groups, reps, subs = (lax.axis_size(name) for name in EVERY)
+    columns = gradient.shape[1]
+    ordered = gradient.astype(jnp.bfloat16).reshape(groups, reps, subs, -1, columns)
+    return ordered.transpose(1, 0, 2, 3, 4).reshape(-1, columns)
+
+def rep_sums(ordered):
+    return lax.psum_scatter(ordered, 'rep', scatter_dimension=0, tiled=True)
+
+def sub_turn(block):
+    groups, reps, subs = (lax.axis_size(name) for name in EVERY)
+    low = reps // subs
+    moves = [((g * reps + r) * subs + u, (g * reps + u * low + r % low) * subs + r // low) for g in range(groups) for r in range(reps) for u in range(subs)]
+    return lax.ppermute(block, EVERY, moves)
 
 def sub_rows(own):
     rows, width = own.shape
@@ -636,36 +1003,11 @@
     first, second = (jnp.where(me == 0, kept, come), jnp.where(me == 0, come, kept))
     return jnp.stack([first, second], axis=1).reshape(rows, width)
 
-def sub_owned(part, reps):
+def mixing_sums_of(part):
+    reps, subs = (lax.axis_size('rep'), lax.axis_size('sub'))
     rows, width = part.shape
-    subs = lax.axis_size('sub')
-    shares = part.reshape(reps // subs, subs, -1, width).transpose(1, 0, 2, 3)
-    if subs != 2:
-        every = lax.all_to_all(shares, 'sub', split_axis=0, concat_axis=0, tiled=True)
-        return every.reshape(rows, width)
-    me = lax.axis_index('sub')
-    kept = jnp.where(me == 0, shares[0], shares[1])
-    come = lax.ppermute(jnp.where(me == 0, shares[1], shares[0]), 'sub', [(0, 1), (1, 0)])
-    first, second = (jnp.where(me == 0, kept, come), jnp.where(me == 0, come, kept))
-    return jnp.concatenate([first, second], axis=0).reshape(rows, width)
-
-def rep_rows(own):
-    groups, reps, subs = (lax.axis_size(name) for name in EVERY)
-    every = lax.all_gather(own, 'rep', axis=0, tiled=True)
-    every = every.reshape(reps, groups, subs, -1, own.shape[1]).transpose(1, 0, 2, 3, 4)
-    return every.reshape(-1, own.shape[1])
-
-def rep_sums(gradient):
-    groups, reps, subs = (lax.axis_size(name) for name in EVERY)
-    columns = gradient.shape[1]
-    ordered = gradient.astype(jnp.bfloat16).reshape(groups, reps, subs, -1, columns)
-    ordered = ordered.transpose(1, 0, 2, 3, 4).reshape(-1, columns)
-    return lax.psum_scatter(ordered, 'rep', scatter_dimension=0, tiled=True)
-
-def owner_rows(summed, plane_count):
-    columns = summed.shape[1]
-    own = lax.all_to_all(summed.reshape(plane_count, -1, columns), PLANE, split_axis=0, concat_axis=0, tiled=True)
-    return own.transpose(1, 0, 2).reshape(-1, plane_count * columns).astype(jnp.float32)
+    ordered = part.reshape(reps // subs, subs, rows // reps, width).transpose(1, 0, 2, 3)
+    return lax.psum_scatter(ordered.reshape(rows, width), 'rep', scatter_dimension=0, tiled=True)
 
 def shards(layer_input, entry_gain, entry_shift, joint_weight, query_offset, value_offset, mixing_weight, attention_offset, middle_gain, middle_shift, expand_weight, expand_offset, shrink_weight, shrink_offset, placement, slot_lengths, cotangent):
     token_rows, width = layer_input.shape
@@ -677,91 +1019,72 @@
     local_heads = HEADS // plane_count
     head_columns = local_heads * head_size
     plane_rows = plane_count * token_rows
-    home = [g * reps * subs + r * subs + u for g in range(groups) for r in range(reps) for u in range(subs)]
-    away = [(r * reps + g % 2 * (groups // 2) + g // 2) * subs + u for g in range(groups) for r in range(reps) for u in range(subs)]
-
-    def to_plane(array):
-        return lax.ppermute(array, EVERY, list(zip(home, away)))
-
-    def from_plane(array):
-        return lax.ppermute(array, EVERY, list(zip(away, home)))
-    facts = to_plane(jnp.concatenate([placement, slot_lengths], axis=1))[0]
-    mixing_own = lax.all_gather(mixing_weight, 'rep', axis=0, tiled=True)
+    facts = to_plane_at_once(jnp.concatenate([placement, slot_lengths], axis=1))[0]
+    mixing_own = rep_rows(mixing_weight)
     moved_input, joint_own, expand_own, shrink_own = opening(layer_input, (joint_weight, expand_weight, shrink_weight), 12)
     joint_own, mixing_own = lax.optimization_barrier((joint_own, mixing_own))
     input_float = moved_input.astype(jnp.float32)
-    joint_slice = rep_rows(joint_own)
+    joint_every = rep_rows(joint_own)
     entry_normal, entry_inverse = norm_terms(input_float)
     entry_normed = (entry_normal * entry_gain + entry_shift).astype(jnp.bfloat16)
-    entry_all = plane_gather(entry_normed, 1)
+    entry_all, = plane_gather(entry_normed, (), 1)
     cotangent, facts, entry_all = lax.optimization_barrier((cotangent, facts, entry_all))
-    places, lengths = (facts[:placement.shape[1]], facts[placement.shape[1]:])
+    cotangent = to_door(cotangent)
+    places = plane_order(facts[:placement.shape[1]])
+    lengths = facts[placement.shape[1]:]
     prompt = places.shape[0] // 2
     key_last = key_bounds(places, lengths, prompt)
     expand_slice = rep_rows(expand_own)
     shrink_slice = rep_rows(shrink_own)
-    cotangent = to_plane(cotangent)
+    cotangent = to_keeper(cotangent)
     mixing_slice = sub_rows(mixing_own)
     offsets = jnp.stack([query_offset.reshape(HEADS, head_size), jnp.zeros((HEADS, head_size), jnp.float32), value_offset.reshape(HEADS, head_size)], axis=1).reshape(-1)
     offsets = lax.dynamic_slice_in_dim(offsets, plane_index * 3 * head_columns, 3 * head_columns)
-    heads_kept = (product(entry_all, joint_slice) + offsets).astype(jnp.bfloat16)
+    heads_kept = (product(entry_all, rep_rows_last(joint_every)) + offsets).astype(jnp.bfloat16)
     attended, log_totals, branch = attend(heads_kept, places, key_last, mixing_slice, local_heads, token_rows, 3)
     residual = input_float + (branch + attention_offset)
     middle_normal, middle_inverse = norm_terms(residual)
     middle_normed = (middle_normal * middle_gain + middle_shift).astype(jnp.bfloat16)
-    middle_all = plane_gather(middle_normed, 5)
-    cotangent, middle_all = lax.optimization_barrier((cotangent, middle_all))
-    cotangent_all = plane_gather(cotangent, 4)
+    cotangent, middle_normed = lax.optimization_barrier((cotangent, middle_normed))
+    cotangent_all, = plane_gather(cotangent, (), 4)
+    middle_normed, cotangent_all = lax.optimization_barrier((middle_normed, cotangent_all))
     hidden_local = hidden_width // plane_count
     offset_local = lax.dynamic_slice_in_dim(expand_offset, plane_index * hidden_local, hidden_local)
-    expanded = product(middle_all, expand_slice) + offset_local
-    activated_float, gelu_back = jax.vjp(exact_gelu, expanded)
-    activated = activated_float.astype(jnp.bfloat16)
-    shrink_part = row_outer(cotangent_all, activated).astype(jnp.bfloat16)
-    shrink_part, cotangent_all = lax.optimization_barrier((shrink_part, cotangent_all))
+    middle_all, activated, rise, shrink_part = hidden(middle_normed, cotangent_all, expand_slice, offset_local, 5)
     shrink_sums = rep_sums(shrink_part)
-    activated_slope = product(cotangent_all, shrink_slice)
-    expanded_slope = gelu_back(activated_slope)[0].astype(jnp.bfloat16)
-    normed_slope = product_reduce(expanded_slope.reshape(plane_count, token_rows, hidden_local), expand_slice, 6)
-    normed_slope, middle_all = lax.optimization_barrier((normed_slope, middle_all))
-    expand_part = row_outer(middle_all, expanded_slope).astype(jnp.bfloat16)
-    expand_part, normed_slope = lax.optimization_barrier((expand_part, normed_slope))
+    expanded_slope, normed_slope, expand_part = hidden_back(cotangent_all, middle_all, rise, shrink_slice, expand_slice, token_rows, 6)
     expand_sums = rep_sums(expand_part)
     cotangent_float = cotangent.astype(jnp.float32)
     residual_slope = cotangent_float + norm_back(normed_slope, middle_gain, middle_normal, middle_inverse)
     branch_slope = residual_slope.astype(jnp.bfloat16)
-    branch_all, joint_slope = attend_back(branch_slope, heads_kept, mixing_slice, log_totals, places, key_last, local_heads, 7)
-    shrink_gradient = owner_rows(shrink_sums, plane_count)
-    shrink_gradient, joint_slope = lax.optimization_barrier((shrink_gradient, joint_slope))
-    joint_part = row_outer(entry_all, joint_slope).astype(jnp.bfloat16)
-    joint_part, joint_slope, expand_sums, attended = lax.optimization_barrier((joint_part, joint_slope, expand_sums, attended))
+    mixing_part, joint_slope, shrink_rows = attend_back(branch_slope, shrink_sums, heads_kept, mixing_slice, attended, log_totals, places, key_last, local_heads, 7)
+    shrink_gradient = shrink_rows.astype(jnp.float32)
+    joint_part = rep_rows_first(row_outer(entry_all, joint_slope))
+    joint_part, joint_slope, expand_sums, mixing_part = lax.optimization_barrier((joint_part, joint_slope, expand_sums, mixing_part))
     joint_sums = rep_sums(joint_part)
-    entry_slope = product_reduce(joint_slope.reshape(plane_count, token_rows, 3 * head_columns), joint_slice, 9)
+    activated, joint_slope = lax.optimization_barrier((activated, joint_slope))
+    shrunk, = product_reduce(activated.reshape(plane_count, token_rows, hidden_local), shrink_slice, None, None, 8)
+    own_output = (residual + shrunk + shrink_offset).astype(jnp.bfloat16)
+    own_output, joint_slope = lax.optimization_barrier((own_output, joint_slope))
+    joint_sums, mixing_part = lax.optimization_barrier((joint_sums, mixing_part))
+    mixing_sums = mixing_sums_of(mixing_part)
+    entry_slope, layer_output = product_reduce(joint_slope.reshape(plane_count, token_rows, 3 * head_columns), joint_every, None, own_output, 9)
     own_gradient = (residual_slope + norm_back(entry_slope, entry_gain, entry_normal, entry_inverse)).astype(jnp.bfloat16)
-    own_gradient, attended, expand_sums = lax.optimization_barrier((own_gradient, attended, expand_sums))
-    input_gradient = from_plane(own_gradient)
-    expand_gradient = owner_rows(expand_sums, plane_count)
-    mixing_part = sub_owned(row_outer(attended, branch_all).astype(jnp.bfloat16), reps)
-    mixing_part, activated, joint_sums = lax.optimization_barrier((mixing_part, activated, joint_sums))
-    mixing_sums = lax.psum_scatter(mixing_part, 'rep', scatter_dimension=0, tiled=True)
-    shrunk = product_reduce(activated.reshape(plane_count, token_rows, hidden_local), shrink_slice, 8)
-    shrunk, mixing_sums, input_gradient, expand_gradient = lax.optimization_barrier((shrunk, mixing_sums, input_gradient, expand_gradient))
-    own_output = (residual + shrunk + shrink_offset).astype(jnp.bfloat16)
-    layer_output = from_plane(own_output)
-    mixing_gradient = mixing_sums.astype(jnp.float32)
     slope_sums = jnp.sum(joint_slope.astype(jnp.float32), axis=0).reshape(local_heads, 3, head_size)
 
     def placed(piece, whole_size):
         return lax.dynamic_update_slice_in_dim(jnp.zeros((whole_size,), jnp.float32), piece, plane_index * piece.shape[0], 0)
     small = [jnp.sum(entry_slope * entry_normal, axis=0), jnp.sum(entry_slope, axis=0), placed(slope_sums[:, 0].reshape(-1), width), placed(slope_sums[:, 2].reshape(-1), width), jnp.sum(branch_slope.astype(jnp.float32), axis=0), jnp.sum(normed_slope * middle_normal, axis=0), jnp.sum(normed_slope, axis=0), placed(jnp.sum(expanded_slope.astype(jnp.float32), axis=0), hidden_width), jnp.sum(cotangent_float, axis=0)]
     small_own = jnp.concatenate(small).reshape(-1, 128)
-    small_own, own_output = lax.optimization_barrier((small_own, own_output))
-    small_all = total_everywhere(small_own, 10).reshape(-1)
+    small_all, input_gradient, joint_rows, expand_rows = closing(small_own, own_gradient, (joint_sums, expand_sums), 10)
+    expand_gradient = expand_rows.astype(jnp.float32)
+    joint_gradient = joint_rows.astype(jnp.float32)
+    mixing_gradient = sub_turn(mixing_sums).astype(jnp.float32)
+    small_all = small_all.reshape(-1)
     small_sums, first = ([], 0)
     for piece in small:
         small_sums.append(small_all[first:first + piece.shape[0]])
         first += piece.shape[0]
-    joint_gradient = owner_rows(joint_sums, plane_count)
     return (layer_output, input_gradient, small_sums[0], small_sums[1], joint_gradient, small_sums[2], small_sums[3], mixing_gradient, small_sums[4], small_sums[5], small_sums[6], expand_gradient, small_sums[7], shrink_gradient, small_sums[8])
 
 def solution(mesh):

time: 736 us -> 683 us (0.928)
  matrix products: 95.1 us -> 21.1 us
  Pallas kernels: 475 us -> 506 us
  local copies, waits for them, and re-layouts: 42 us -> 22.5 us
  waiting for transfers between devices: 32.5 us -> 46.6 us
  starting transfers between devices: 35.5 us -> 24.6 us
    dot_general x3 -> x1, matrix products: 56.4 us -> 10.8 us  [product(): jnp.dot(left_matrix, right_matrix, preferred_element_type=jnp.float32)]
    pallas_call x7, Pallas kernels: 314 us -> 345 us  [the longest x2 99.5 us: product_reduce(): pl.pallas_call(functools.partial(product_reduce_kernel, owns, homes), gri...]
    dot_general x4 -> x1, matrix products: 38.7 us -> 10.3 us  [row_outer(): lax.dot_general(left_matrix, right_matrix, (((0,), (0,)), ((), ())), pref...]
    reduce_scatter x3, waiting for transfers between devices: 0.01 us -> 22.4 us  [rep_sums(): return lax.psum_scatter(ordered, 'rep', scatter_dimension=0, tiled=True)]
    all_to_all x3 -> x0, starting transfers between devices: 16.7 us -> none  [owner_rows(): lax.all_to_all(summed.reshape(plane_count, -1, columns), PLANE, split_axi...]
    reshape x7 -> x4, local copies, waits for them, and re-layouts: 17.1 us -> 4.48 us  [the longest x1 2.5 us: rep_rows_last(): every.reshape(reps, groups, subs, -1, columns).transpose(1, 0, 2, 3, 4)]
    all_gather x4, waiting for transfers between devices: 0.04 us -> 12.4 us  [rep_rows(): return lax.all_gather(own, 'rep', axis=0, tiled=True)]
    all_to_all x3 -> x0, waiting for transfers between devices: 10.7 us -> none  [owner_rows(): lax.all_to_all(summed.reshape(plane_count, -1, columns), PLANE, split_axi...]
  transfers between devices with their start and end apart: 17 -> 13, of which waited for: 4 -> 5; matrix products, arithmetic and copies ran while one was open for 21% -> 10% of each run, Pallas kernels for 65% -> 76%
where the time goes in v4:
time: 683 us; the launch traced here: 670 us
  Pallas kernels  506 us (74%)
  waiting for transfers between devices  46.6 us (7%)
  other arithmetic  34.2 us (5%)
  starting transfers between devices  24.6 us (4%)
  local copies, waits for them, and re-layouts  22.5 us (3%)
  matrix products  21.1 us (3%)
  between operations  15.1 us (2%)
    pallas_call x2, Pallas kernels, product_reduce(): pl.pallas_call(functools.partial(product_reduce_kernel, owns, homes), gri...  99.5 us
    pallas_call x2, Pallas kernels, plane_gather(): pl.pallas_call(functools.partial(gather_kernel, number), grid=(8,), out_s...  81.7 us
    pallas_call x1, Pallas kernels, attend_back(): pl.pallas_call(functools.partial(attend_back_kernel, heads), grid=(8,), o...  60.4 us
    pallas_call x1, Pallas kernels, closing(): pl.pallas_call(functools.partial(closing_kernel, number), out_shape=[jax....  60.1 us
    pallas_call x1, Pallas kernels, hidden_back(): pl.pallas_call(hidden_back_kernel, grid=(8,), out_shape=[jax.ShapeDtypeSt...  55.1 us
    pallas_call x1, Pallas kernels, opening(): pl.pallas_call(opening_kernel, out_shape=[jax.ShapeDtypeStruct(x.shape, x...  54.4 us
    pallas_call x1, Pallas kernels, hidden(): pl.pallas_call(hidden_kernel, grid=(8,), out_shape=[jax.ShapeDtypeStruct(...  48.2 us
    pallas_call x1, Pallas kernels, attend(): pl.pallas_call(functools.partial(attend_kernel, heads), grid=(8,), out_sh...  46.9 us
  transfers between devices with their start and end apart: 13, of which 5 were waited for; matrix products, arithmetic and copies ran while one was open for 10% of the time, Pallas kernels for 76%

profile of v4, /device:TPU:19, one launch (start us, length us, event | category | flops | bytes accessed | tf_op | source)
XLA Modules:
  0.0 670.4 jit_solution(3081678729241322469)
XLA Ops:
  8.0 54.4 %opening.1 = (bf16[256,2048]{1,0:T(8,128)(2,1)}, bf16[512,768]{1,0:T(8,128)(2,1)}, bf16[512,1024]{1,0:T(8,128)(2,1)}, bf16[512,1024]{1,0:T(8,128)(2,1)}) custom-call(bf16[256,2048]{1,0:T(8,128)(2,1)} %x_ref.1, bf16[64,6144]{1,0:T(8,128)(2,1)} %refs_0_.1, bf16[64,8192]{1,0:T(8,128)(2,1)} %refs_1_.1, bf16[64,8192]{1,0:T(8,128)(2,1)} %refs_2_.1), custom_call_target="tpu_custom_call" | custom-call | tf_op jit(solution)/shard_map/opening/pallas_call | solution.py:610
  63.3 13.4 %collective-permute-start = (s32[1,2052]{1,0:T(1,128)S(1)}, s32[1,2052]{1,0:T(1,128)S(1)}, u32[]{:S(2)}, u32[]{:S(2)}) collective-permute-start(s32[1,2052]{1,0:T(1,128)S(1)} %pad_add_fusion), channel_id=1, source_target_pairs={{0,0},{1,1},{2,16},{3,17},{4,8},{5,9},{6,24},{7,25},{8,18},{9,19},... | collective-permute-start | bytes 24632 | tf_op jit(solution)/shard_map/ppermute | solution.py:959
  78.1 38.7 %plane_gather.2 = bf16[8,256,2048]{2,1,0:T(8,128)(2,1)S(1)} custom-call(bf16[256,2048]{1,0:T(8,128)(2,1)S(1)} %fusion.7.x_ref), custom_call_target="tpu_custom_call" | custom-call | tf_op jit(solution)/shard_map/plane_gather/pallas_call | solution.py:294
  116.9 3.2 copy-done.1
  123.6 3.2 collective-permute-start.2
  128.6 10.2 %collective-permute-done.2 = bf16[256,2048]{1,0:T(8,128)(2,1)} collective-permute-done((bf16[256,2048]{1,0:T(8,128)(2,1)}, bf16[256,2048]{1,0:T(8,128)(2,1)}, u32[]{:S(2)}, u32[]{:S(2)}) %collective-permute-start.2) | collective-permute-done | bytes 1048608 | tf_op jit(solution)/shard_map/ppermute | solution.py:953
  138.8 5.0 collective-permute-start.3
  144.9 2.5 copy.58
  147.4 10.8 %add_convert_fusion.head_ref = bf16[2048,768]{1,0:T(8,128)(2,1)} fusion(f32[768]{0:T(1024)S(1)} %dynamic_slice.10, bf16[2048,2048]{1,0:T(8,128)(2,1)} %bitcast.64, bf16[2048,768]{1,0:T(8,128)(2,1)S(1)} %bitcast.72), kind=kOutput, calls=%fused_computation.2 | convolution fusion | flops 6445596672 | bytes 14683136 | tf_op jit(solution)/shard_map/dot_general | solution.py:44
  158.2 46.9 %attend.1 = (bf16[2048,256]{1,0:T(8,128)(2,1)}, f32[2,8,2048]{2,1,0:T(8,128)}, f32[256,2048]{1,0:T(8,128)}) custom-call(bf16[2048,768]{1,0:T(8,128)(2,1)} %add_convert_fusion.head_ref, s32[2048,1]{1,0:T(8,128)} %broadcast_in_dim_reshape.10.place_ref.first_ref, s32[1,2048]{1,0:T(1,128)} %copy-done.18, s32[1,2048]{1,0:T(1,128)} %compare_select_fusion.1.last_ref, ...), custom_call_target="tpu_custom_call" | custom-call | tf_op jit(solution)/shard_map/attend/pallas_call | solution.py:646
  205.2 2.0 fusion.20
  209.5 43.0 %plane_gather.3 = bf16[8,256,2048]{2,1,0:T(8,128)(2,1)S(1)} custom-call(bf16[256,2048]{1,0:T(8,128)(2,1)S(1)} %collective-permute-done.3.x_ref), custom_call_target="tpu_custom_call" | custom-call | tf_op jit(solution)/shard_map/plane_gather/pallas_call | solution.py:294
  252.5 3.2 copy-done
  255.8 48.2 %hidden.1 = (bf16[8,256,2048]{2,1,0:T(8,128)(2,1)}, bf16[8,256,1024]{2,1,0:T(8,128)(2,1)}, f32[8,256,1024]{2,1,0:T(8,128)}, bf16[2048,1024]{1,0:T(8,128)(2,1)}) custom-call(bf16[256,2048]{1,0:T(8,128)(2,1)} %add_convert_fusion.2.middle_ref, bf16[8,256,2048]{2,1,0:T(8,128)(2,1)} %copy-done, bf16[2048,1024]{1,0:T(8,128)(2,1)} %all-gather.9.cloned.1.call-done.expand_ref, ...), custom_call_target="tpu_custom_call" | custom-call | tf_op jit(solution)/shard_map/hidden/pallas_call | solution.py:874
  304.0 12.3 %all-gather.11.cloned.1.call-done.shrink_ref.weight_ref = bf16[2048,1024]{1,0:T(8,128)(2,1)} async-done(((bf16[512,1024]{1,0:T(8,128)(2,1)}), bf16[2048,1024]{1,0:T(8,128)(2,1)}) %all-gather.11.cloned.1.call-update) | async-done | bytes 4194320 | tf_op jit(solution)/shard_map/all_gather | solution.py:970
  316.3 55.1 %hidden_back.1 = (bf16[8,256,1024]{2,1,0:T(8,128)(2,1)}, f32[256,2048]{1,0:T(8,128)}, bf16[2048,1024]{1,0:T(8,128)(2,1)}) custom-call(bf16[8,256,2048]{2,1,0:T(8,128)(2,1)} %copy-done, bf16[8,256,2048]{2,1,0:T(8,128)(2,1)} %get-tuple-element.71.middle_ref, f32[8,256,1024]{2,1,0:T(8,128)} %get-tuple-element.72.rise_ref, ...), custom_call_target="tpu_custom_call" | custom-call | tf_op jit(solution)/shard_map/hidden_back/pallas_call | solution.py:938
  372.9 3.3 select_select_fusion.last_ref
  377.4 2.9 convert_reduce_fusion.4
  380.4 15.5 %reduce-scatter.5.cloned.1.call-done.owned_ref = bf16[512,1024]{1,0:T(8,128)(2,1)} async-done(((bf16[2048,1024]{1,0:T(8,128)(2,1)}), bf16[512,1024]{1,0:T(8,128)(2,1)}) %reduce-scatter.5.cloned.1.call-update) | async-done | bytes 1048592 | tf_op jit(solution)/shard_map/reduce_scatter | solution.py:985
  395.8 60.4 %attend_back.1 = (bf16[256,2048]{1,0:T(8,128)(2,1)}, bf16[2048,768]{1,0:T(8,128)(2,1)}, bf16[64,8192]{1,0:T(8,128)(2,1)}) custom-call(bf16[256,2048]{1,0:T(8,128)(2,1)} %get-tuple-element.108.branch_ref, bf16[512,1024]{1,0:T(8,128)(2,1)} %reduce-scatter.5.cloned.1.call-done.owned_ref, bf16[2048,768]{1,0:T(8,128)(2,1)} %add_convert_fusion.head_ref, ...), custom_call_target="tpu_custom_call" | custom-call | tf_op jit(solution)/shard_map/attend_back/pallas_call | solution.py:779
  456.2 10.3 %convolution_convert_fusion = bf16[2048,768]{1,0:T(8,128)(2,1)S(1)} fusion(bf16[2048,2048]{1,0:T(8,128)(2,1)} %bitcast.65, bf16[2048,768]{1,0:T(8,128)(2,1)} %get-tuple-element.84), kind=kOutput, calls=%fused_computation.3 | convolution fusion | flops 6444023808 | bytes 14680064 | tf_op jit(solution)/shard_map/dot_general | solution.py:50
  466.5 2.0 copy.68
  468.5 6.9 %reduce-scatter.7.cloned.1.call-done.refs_1_ = bf16[512,1024]{1,0:T(8,128)(2,1)} async-done(((bf16[2048,1024]{1,0:T(8,128)(2,1)}), bf16[512,1024]{1,0:T(8,128)(2,1)}) %reduce-scatter.7.cloned.1.call-update) | async-done | bytes 1048592 | tf_op jit(solution)/shard_map/reduce_scatter | solution.py:985
  475.5 2.9 convert_reduce_fusion
  478.9 46.1 %product_reduce.2 = f32[256,2048]{1,0:T(8,128)} custom-call(bf16[8,256,1024]{2,1,0:T(8,128)(2,1)} %get-tuple-element.70, bf16[2048,1024]{1,0:T(8,128)(2,1)} %all-gather.11.cloned.1.call-done.shrink_ref.weight_ref), custom_call_target="tpu_custom_call" | custom-call | tf_op jit(solution)/shard_map/product_reduce/pallas_call | solution.py:437
  525.0 3.1 add_convert_fusion.1.refs_0_
  528.6 53.4 %product_reduce.3 = (f32[256,2048]{1,0:T(8,128)}, bf16[256,2048]{1,0:T(8,128)(2,1)}) custom-call(bf16[8,256,768]{2,1,0:T(8,128)(2,1)} %bitcast.67, bf16[2048,768]{1,0:T(8,128)(2,1)} %all-gather.7.cloned.1.call-done.weight_ref, bf16[256,2048]{1,0:T(8,128)(2,1)} %add_convert_fusion.1.refs_0_), custom_call_target="tpu_custom_call" | custom-call | tf_op jit(solution)/shard_map/product_reduce/pallas_call | solution.py:437
  582.1 2.7 fusion.9
  585.9 2.8 convert_element_type.64
  589.3 3.4 fusion.13.homed_ref
  592.6 60.1 %closing.1 = (f32[192,128]{1,0:T(8,128)}, bf16[256,2048]{1,0:T(8,128)(2,1)}, bf16[64,6144]{1,0:T(8,128)(2,1)}, bf16[64,8192]{1,0:T(8,128)(2,1)}) custom-call(f32[192,128]{1,0:T(8,128)} %bitcast.77, bf16[256,2048]{1,0:T(8,128)(2,1)} %fusion.13.homed_ref, bf16[512,768]{1,0:T(8,128)(2,1)} %reduce-scatter.9.cloned.1.call-done.refs_0_, ...), custom_call_target="tpu_custom_call" | custom-call | tf_op jit(solution)/shard_map/closing/pallas_call | solution.py:485
  655.9 2.7 convert_element_type.63
  (150 shorter events, 24.9 us)
Async XLA Ops:
  7.2 55.3 %all-gather.5.cloned.1.call-start = ((), (), s32[]{:S(2)}) async-start(), calls=%async_computation.4 | async-start | bytes 1310720 | tf_op jit(solution)/shard_map/all_gather | solution.py:970
  7.9 55.4 %copy-start.29 = (s32[1,2048]{1,0:T(1,128)S(1)}, s32[1,2048]{1,0:T(1,128)}, u32[]{:S(2)}) copy-start(s32[1,2048]{1,0:T(1,128)} %param.31) | copy-start | bytes 24580
  7.9 55.4 %copy-start.30 = (s32[1,4]{1,0:T(1,128)S(1)}, s32[1,4]{1,0:T(1,128)}, u32[]{:S(2)}) copy-start(s32[1,4]{1,0:T(1,128)} %param.32) | copy-start | bytes 52
  7.9 137.0 %all-gather.7.cloned.1.call-start = ((), (), s32[]{:S(2)}) async-start(), calls=%async_computation.5 | async-start | bytes 3932160 | tf_op jit(solution)/shard_map/all_gather | solution.py:970
  62.4 14.4 %copy-start.7 = (bf16[256,2048]{1,0:T(8,128)(2,1)S(1)}, bf16[256,2048]{1,0:T(8,128)(2,1)}, u32[]{:S(2)}) copy-start(bf16[256,2048]{1,0:T(8,128)(2,1)} %get-tuple-element.57) | copy-start | bytes 3145732
  62.5 193.3 %all-gather.9.cloned.1.call-start = ((), (), s32[]{:S(2)}) async-start(), calls=%async_computation.6 | async-start | bytes 5242880 | tf_op jit(solution)/shard_map/all_gather | solution.py:970
  62.5 15.0 %copy-start.22 = (f32[2048]{0:T(1024)S(1)}, f32[2048]{0:T(1024)}, u32[]{:S(2)}) copy-start(f32[2048]{0:T(1024)} %param.18) | copy-start | bytes 24580
  62.5 15.0 %copy-start.23 = (f32[2048]{0:T(1024)S(1)}, f32[2048]{0:T(1024)}, u32[]{:S(2)}) copy-start(f32[2048]{0:T(1024)} %param.19) | copy-start | bytes 24580
  63.2 253.1 %all-gather.11.cloned.1.call-start = ((), (), s32[]{:S(2)}) async-start(), calls=%async_computation.7 | async-start | bytes 5242880 | tf_op jit(solution)/shard_map/all_gather | solution.py:970
  63.3 58.2 %collective-permute-start = (s32[1,2052]{1,0:T(1,128)S(1)}, s32[1,2052]{1,0:T(1,128)S(1)}, u32[]{:S(2)}, u32[]{:S(2)}) collective-permute-start(s32[1,2052]{1,0:T(1,128)S(1)} %pad_add_fusion), channel_id=1, source_target_pairs={{0,0},{1,1},{2,16},{3,17},{4,8},{5,9},{6,24},{7,25},{8,18},{9,19},... | collective-permute-start | bytes 24632 | tf_op jit(solution)/shard_map/ppermute | solution.py:959
  76.7 319.1 %reduce-scatter.5.cloned.1.call-start = ((), (), s32[]{:S(2)}) async-start(), calls=%async_computation.8 | async-start | bytes 5242880 | tf_op jit(solution)/shard_map/reduce_scatter | solution.py:985
  78.1 48.6 %copy-start.13 = (bf16[256,2048]{1,0:T(8,128)(2,1)S(1)}, bf16[256,2048]{1,0:T(8,128)(2,1)}, u32[]{:S(2)}) copy-start(bf16[256,2048]{1,0:T(8,128)(2,1)} %all-gather.5.cloned.1.call-done) | copy-start | bytes 3145732
  121.6 22.2 %copy-start.18 = (s32[1,2048]{1,0:T(1,128)}, s32[1,2048]{1,0:T(1,128)S(1)}, u32[]{:S(2)}) copy-start(s32[1,2048]{1,0:T(1,128)S(1)} %broadcast_in_dim_reshape.9.first_ref.place_ref) | copy-start | bytes 24580
  123.6 15.2 %collective-permute-start.2 = (bf16[256,2048]{1,0:T(8,128)(2,1)}, bf16[256,2048]{1,0:T(8,128)(2,1)}, u32[]{:S(2)}, u32[]{:S(2)}) collective-permute-start(bf16[256,2048]{1,0:T(8,128)(2,1)} %param.33), channel_id=1, source_target_pairs={{0,0},{1,1},{2,18},{3,19},{4,12},{5,13},{6,30},{7,31},{8,16},{9,17... | collective-permute-start | bytes 3145736 | tf_op jit(solution)/shard_map/ppermute | solution.py:953
  126.9 16.9 %collective-permute-start.1 = (bf16[2,64,2048]{2,1,0:T(8,128)(2,1)S(1)}, bf16[2,64,2048]{2,1,0:T(8,128)(2,1)S(1)}, u32[]{:S(2)}, u32[]{:S(2)}) collective-permute-start(bf16[2,64,2048]{2,1,0:T(8,128)(2,1)S(1)} %bitcast.76), channel_id=1, source_target_pairs={{0,1},{1,0},{2,3},{3,2},{4,5},{5,4},{6,7},{7,6},{8,9},{9,8},{10,11... | collective-permute-start | bytes 1572872 | tf_op jit(solution)/shard_map/ppermute | solution.py:1002
  138.8 70.8 %collective-permute-start.3 = (bf16[256,2048]{1,0:T(8,128)(2,1)}, bf16[256,2048]{1,0:T(8,128)(2,1)S(1)}, u32[]{:S(2)}, u32[]{:S(2)}) collective-permute-start(bf16[256,2048]{1,0:T(8,128)(2,1)} %collective-permute-done.2), channel_id=1, source_target_pairs={{0,0},{1,1},{18,16},{19,17},{12,8},{13,9},{30,24},{31,25},{16,18},... | collective-permute-start | bytes 3145736 | tf_op jit(solution)/shard_map/ppermute | solution.py:956
  158.2 46.9 %copy-start.24 = (f32[2048]{0:T(1024)S(1)}, f32[2048]{0:T(1024)}, u32[]{:S(2)}) copy-start(f32[2048]{0:T(1024)} %param.24) | copy-start | bytes 24580
  209.5 43.0 %copy-start.2 = (bf16[256,2048]{1,0:T(8,128)(2,1)}, bf16[256,2048]{1,0:T(8,128)(2,1)S(1)}, u32[]{:S(2)}) copy-start(bf16[256,2048]{1,0:T(8,128)(2,1)S(1)} %collective-permute-done.3.x_ref) | copy-start | bytes 3145732
  252.5 3.2 copy-start
  304.0 171.4 %reduce-scatter.7.cloned.1.call-start = ((), (), s32[]{:S(2)}) async-start(), calls=%async_computation.9 | async-start | bytes 5242880 | tf_op jit(solution)/shard_map/reduce_scatter | solution.py:985
  371.5 213.2 %reduce-scatter.9.cloned.1.call-start = ((), (), s32[]{:S(2)}) async-start(), calls=%async_computation.10 | async-start | bytes 3932160 | tf_op jit(solution)/shard_map/reduce_scatter | solution.py:985
  371.6 4.6 copy-start.5
  372.9 3.3 copy-start.11
  475.4 177.4 %reduce-scatter.11.cloned.1.call-start = ((), (), s32[]{:S(2)}) async-start(), calls=%async_computation.11 | async-start | bytes 1310720 | tf_op jit(solution)/shard_map/reduce_scatter | solution.py:1010
  478.9 46.1 %copy-start.6 = (f32[256,2048]{1,0:T(8,128)S(1)}, f32[256,2048]{1,0:T(8,128)}, u32[]{:S(2)}) copy-start(f32[256,2048]{1,0:T(8,128)} %copy-done.4) | copy-start | bytes 6291460
  478.9 46.1 %copy-start.26 = (f32[2048]{0:T(1024)S(1)}, f32[2048]{0:T(1024)}, u32[]{:S(2)}) copy-start(f32[2048]{0:T(1024)} %param.30) | copy-start | bytes 24580
  528.6 53.4 %copy-start.8 = (bf16[256,2048]{1,0:T(8,128)(2,1)S(1)}, bf16[256,2048]{1,0:T(8,128)(2,1)}, u32[]{:S(2)}) copy-start(bf16[256,2048]{1,0:T(8,128)(2,1)} %get-tuple-element.57) | copy-start | bytes 3145732
  585.8 3.4 copy-start.12
  589.2 3.4 copy-start.19
  652.8 5.9 copy-start.17
  652.8 7.7 %collective-permute-start.4 = (bf16[64,2048]{1,0:T(8,128)(2,1)}, bf16[64,2048]{1,0:T(8,128)(2,1)S(1)}, u32[]{:S(2)}, u32[]{:S(2)}) collective-permute-start(bf16[64,2048]{1,0:T(8,128)(2,1)} %reduce-scatter.11.cloned.1.call-done), channel_id=1, source_target_pairs={{0,0},{1,4},{2,2},{3,6},{4,1},{5,5},{6,3},{7,7},{8,8},{9,12},{10,1... | collective-permute-start | bytes 786440 | tf_op jit(solution)/shard_map/ppermute | solution.py:991
  655.9 4.0 copy-start.20
  (12 other events, 23.0 us)
Sparse Core Ops, SparseCore 0:
  9.6 38.8 all-gather.4
  62.6 72.7 all-gather.6
  137.0 97.4 all-gather.8
  235.9 80.4 all-gather.10
  318.5 77.3 reduce-scatter.4
  398.1 77.2 reduce-scatter.6
  477.7 62.7 reduce-scatter.8
  586.0 44.6 reduce-scatter.10

commit v5 on v4

--- a/solution.py
+++ b/solution.py
@@ -712,10 +712,10 @@
         for one in (across_low, up_high, across_high, up_low, own, far_low, far_high, pass_across, pass_up, pass_low, pass_high):
             one.wait_send()
 
-def attend_back_kernel(heads, branch_ref, owned_ref, head_ref, mixing_ref, attended_ref, total_ref, place_ref, first_ref, last_ref, part_ref, out_ref, owned_out, turned, key_sum, value_sum, part_sum, slots, load, send, recv, *cargo):
+def attend_back_kernel(heads, branch_ref, homed_ref, head_ref, mixing_ref, attended_ref, total_ref, place_ref, first_ref, last_ref, part_ref, out_ref, homed_out, turned, key_sum, value_sum, part_sum, slots, load, send, recv, *cargo):
     ids = plane_ids()
     step = pl.program_id(0)
-    start, finish = owner_cargo(owned_ref, owned_out, *cargo)
+    home_start, home_finish = home_cargo(homed_ref, homed_out, *cargo)
     rows = slots.shape[1]
     size = head_ref.shape[1] // (3 * heads)
     scale = size ** (-0.5)
@@ -730,14 +730,11 @@
         key_sum[...] = jnp.zeros_like(key_sum)
         value_sum[...] = jnp.zeros_like(value_sum)
         part_sum[...] = jnp.zeros_like(part_sum)
-        greet(plane_peers()[1])
+        greet_all(ids[:3], True)
+        home_start()
         first.wait()
     gather_step(step, slots, send, recv, ids)
     k = gather_order(step)
-
-    @pl.when(step == 4)
-    def _():
-        start()
     here = pl.ds(pl.multiple_of(ids[3](k) * rows, rows), rows)
     part_sum[...] += row_outer(attended_ref[here, :], slots[k])
     slopes = product_transposed(slots[k], mixing_ref[...]).astype(jnp.bfloat16)
@@ -764,9 +761,9 @@
             out_ref[:, (3 * h + 1) * size:(3 * h + 2) * size] = (key_sum[h] * scale).astype(jnp.bfloat16)
             out_ref[:, (3 * h + 2) * size:(3 * h + 3) * size] = value_sum[h].astype(jnp.bfloat16)
         part_ref[...] = part_sum[...].astype(jnp.bfloat16)
-        finish()
-
-def attend_back(branch_slope, owned, packed, mixing, attended, totals, places, key_last, heads, collective_id):
+        home_finish()
+
+def attend_back(branch_slope, homed, packed, mixing, attended, totals, places, key_last, heads, collective_id):
     rows, columns = packed.shape
     token_rows, width = branch_slope.shape
     size = columns // (3 * heads)
@@ -775,8 +772,8 @@
         slopes = product_transposed(every, mixing).astype(jnp.bfloat16)
         part = row_outer(attended, every).astype(jnp.bfloat16)
         slopes = attention_backward(packed, totals, slopes, places, key_last, heads)
-        return (part, slopes, exchange(owned, True, collective_id))
-    return pl.pallas_call(functools.partial(attend_back_kernel, heads), grid=(8,), out_shape=[jax.ShapeDtypeStruct(mixing.shape, jnp.bfloat16), jax.ShapeDtypeStruct((rows, columns), jnp.bfloat16), owner_shape(owned)], in_specs=[ANY] * 2 + [VMEM] * 7, out_specs=[VMEM, VMEM, ANY], scratch_shapes=[pltpu.VMEM((heads, size, rows), jnp.bfloat16), pltpu.VMEM((heads, rows, size), jnp.float32), pltpu.VMEM((heads, rows, size), jnp.float32), pltpu.VMEM(mixing.shape, jnp.float32), pltpu.VMEM((8, token_rows, width), jnp.bfloat16), DMA, DMA((11,)), DMA((11,)), *owner_scratch()], compiler_params=remote_params(collective_id, 62), name='attend_back')(branch_slope, owned, packed, mixing, attended, totals, places[None, :], places[:, None], key_last[:, None])
+        return (part, slopes, from_plane(homed))
+    return pl.pallas_call(functools.partial(attend_back_kernel, heads), grid=(8,), out_shape=[jax.ShapeDtypeStruct(mixing.shape, jnp.bfloat16), jax.ShapeDtypeStruct((rows, columns), jnp.bfloat16), jax.ShapeDtypeStruct(homed.shape, homed.dtype)], in_specs=[ANY] * 2 + [VMEM] * 7, out_specs=[VMEM, VMEM, ANY], scratch_shapes=[pltpu.VMEM((heads, size, rows), jnp.bfloat16), pltpu.VMEM((heads, rows, size), jnp.float32), pltpu.VMEM((heads, rows, size), jnp.float32), pltpu.VMEM(mixing.shape, jnp.float32), pltpu.VMEM((8, token_rows, width), jnp.bfloat16), DMA, DMA((11,)), DMA((11,)), DMA, DMA, DMA], compiler_params=remote_params(collective_id, 62), name='attend_back')(branch_slope, homed, packed, mixing, attended, totals, places[None, :], places[:, None], key_last[:, None])
 
 def add_outer(total, left, right):
     turned = left.T
@@ -1008,6 +1005,19 @@
     rows, width = part.shape
     ordered = part.reshape(reps // subs, subs, rows // reps, width).transpose(1, 0, 2, 3)
     return lax.psum_scatter(ordered.reshape(rows, width), 'rep', scatter_dimension=0, tiled=True)
+
+def sub_owned(part, reps):
+    rows, width = part.shape
+    subs = lax.axis_size('sub')
+    shares = part.reshape(reps // subs, subs, -1, width).transpose(1, 0, 2, 3)
+    if subs != 2:
+        every = lax.all_to_all(shares, 'sub', split_axis=0, concat_axis=0, tiled=True)
+        return every.reshape(rows, width)
+    me = lax.axis_index('sub')
+    kept = jnp.where(me == 0, shares[0], shares[1])
+    come = lax.ppermute(jnp.where(me == 0, shares[1], shares[0]), 'sub', [(0, 1), (1, 0)])
+    first, second = (jnp.where(me == 0, kept, come), jnp.where(me == 0, come, kept))
+    return jnp.concatenate([first, second], axis=0).reshape(rows, width)
 
 def shards(layer_input, entry_gain, entry_shift, joint_weight, query_offset, value_offset, mixing_weight, attention_offset, middle_gain, middle_shift, expand_weight, expand_offset, shrink_weight, shrink_offset, placement, slot_lengths, cotangent):
     token_rows, width = layer_input.shape
@@ -1054,21 +1064,22 @@
     shrink_sums = rep_sums(shrink_part)
     expanded_slope, normed_slope, expand_part = hidden_back(cotangent_all, middle_all, rise, shrink_slice, expand_slice, token_rows, 6)
     expand_sums = rep_sums(expand_part)
+    activated, normed_slope = lax.optimization_barrier((activated, normed_slope))
+    shrunk, = product_reduce(activated.reshape(plane_count, token_rows, hidden_local), shrink_slice, None, None, 8)
+    own_output = (residual + shrunk + shrink_offset).astype(jnp.bfloat16)
+    own_output, normed_slope = lax.optimization_barrier((own_output, normed_slope))
     cotangent_float = cotangent.astype(jnp.float32)
     residual_slope = cotangent_float + norm_back(normed_slope, middle_gain, middle_normal, middle_inverse)
     branch_slope = residual_slope.astype(jnp.bfloat16)
-    mixing_part, joint_slope, shrink_rows = attend_back(branch_slope, shrink_sums, heads_kept, mixing_slice, attended, log_totals, places, key_last, local_heads, 7)
-    shrink_gradient = shrink_rows.astype(jnp.float32)
+    mixing_part, joint_slope, layer_output = attend_back(branch_slope, own_output, heads_kept, mixing_slice, attended, log_totals, places, key_last, local_heads, 7)
+    shrink_sums, joint_slope = lax.optimization_barrier((shrink_sums, joint_slope))
     joint_part = rep_rows_first(row_outer(entry_all, joint_slope))
     joint_part, joint_slope, expand_sums, mixing_part = lax.optimization_barrier((joint_part, joint_slope, expand_sums, mixing_part))
     joint_sums = rep_sums(joint_part)
-    activated, joint_slope = lax.optimization_barrier((activated, joint_slope))
-    shrunk, = product_reduce(activated.reshape(plane_count, token_rows, hidden_local), shrink_slice, None, None, 8)
-    own_output = (residual + shrunk + shrink_offset).astype(jnp.bfloat16)
-    own_output, joint_slope = lax.optimization_barrier((own_output, joint_slope))
+    mixing_part = sub_owned(mixing_part, reps)
     joint_sums, mixing_part = lax.optimization_barrier((joint_sums, mixing_part))
-    mixing_sums = mixing_sums_of(mixing_part)
-    entry_slope, layer_output = product_reduce(joint_slope.reshape(plane_count, token_rows, 3 * head_columns), joint_every, None, own_output, 9)
+    mixing_sums = rep_sums(mixing_part)
+    entry_slope, expand_rows = product_reduce(joint_slope.reshape(plane_count, token_rows, 3 * head_columns), joint_every, expand_sums, None, 9)
     own_gradient = (residual_slope + norm_back(entry_slope, entry_gain, entry_normal, entry_inverse)).astype(jnp.bfloat16)
     slope_sums = jnp.sum(joint_slope.astype(jnp.float32), axis=0).reshape(local_heads, 3, head_size)
 
@@ -1076,10 +1087,11 @@
         return lax.dynamic_update_slice_in_dim(jnp.zeros((whole_size,), jnp.float32), piece, plane_index * piece.shape[0], 0)
     small = [jnp.sum(entry_slope * entry_normal, axis=0), jnp.sum(entry_slope, axis=0), placed(slope_sums[:, 0].reshape(-1), width), placed(slope_sums[:, 2].reshape(-1), width), jnp.sum(branch_slope.astype(jnp.float32), axis=0), jnp.sum(normed_slope * middle_normal, axis=0), jnp.sum(normed_slope, axis=0), placed(jnp.sum(expanded_slope.astype(jnp.float32), axis=0), hidden_width), jnp.sum(cotangent_float, axis=0)]
     small_own = jnp.concatenate(small).reshape(-1, 128)
-    small_all, input_gradient, joint_rows, expand_rows = closing(small_own, own_gradient, (joint_sums, expand_sums), 10)
+    small_all, input_gradient, joint_rows, shrink_rows = closing(small_own, own_gradient, (joint_sums, shrink_sums), 10)
+    shrink_gradient = shrink_rows.astype(jnp.float32)
     expand_gradient = expand_rows.astype(jnp.float32)
     joint_gradient = joint_rows.astype(jnp.float32)
-    mixing_gradient = sub_turn(mixing_sums).astype(jnp.float32)
+    mixing_gradient = mixing_sums.astype(jnp.float32)
     small_all = small_all.reshape(-1)
     small_sums, first = ([], 0)
     for piece in small:

time: 683 us -> 667 us (0.977); the launches traced: 670 us -> 663 us
  waiting for transfers between devices: 46.6 us -> 24.4 us
  Pallas kernels: 506 us -> 523 us
    reduce_scatter x3 -> x4, waiting for transfers between devices: 22.4 us -> 0.03 us  [rep_sums(): return lax.psum_scatter(ordered, 'rep', scatter_dimension=0, tiled=True)]
    pallas_call x1, Pallas kernels: 60.4 us -> 68.9 us  [attend_back(): pl.pallas_call(functools.partial(attend_back_kernel, heads), grid=(8,), o...]
  transfers between devices with their start and end apart: 13 -> 13, of which waited for: 5 -> 3; matrix products, arithmetic and copies ran while one was open for 10% -> 10% of each run, Pallas kernels for 76% -> 79%
where the time goes in v5:
time: 667 us; the launch traced here: 663 us
  Pallas kernels  523 us (78%)
  other arithmetic  33.7 us (5%)
  waiting for transfers between devices  24.4 us (4%)
  starting transfers between devices  23.2 us (3%)
  local copies, waits for them, and re-layouts  21.9 us (3%)
  matrix products  20.9 us (3%)
  between operations  15 us (2%)
    pallas_call x2, Pallas kernels, product_reduce(): pl.pallas_call(functools.partial(product_reduce_kernel, owns, homes), gri...  103 us
    pallas_call x2, Pallas kernels, plane_gather(): pl.pallas_call(functools.partial(gather_kernel, number), grid=(8,), out_s...  81.7 us
    pallas_call x1, Pallas kernels, attend_back(): pl.pallas_call(functools.partial(attend_back_kernel, heads), grid=(8,), o...  68.9 us
    pallas_call x1, Pallas kernels, closing(): pl.pallas_call(functools.partial(closing_kernel, number), out_shape=[jax....  64 us
    pallas_call x1, Pallas kernels, hidden_back(): pl.pallas_call(hidden_back_kernel, grid=(8,), out_shape=[jax.ShapeDtypeSt...  55.7 us
    pallas_call x1, Pallas kernels, opening(): pl.pallas_call(opening_kernel, out_shape=[jax.ShapeDtypeStruct(x.shape, x...  54.4 us
    pallas_call x1, Pallas kernels, hidden(): pl.pallas_call(hidden_kernel, grid=(8,), out_shape=[jax.ShapeDtypeStruct(...  48.2 us
    pallas_call x1, Pallas kernels, attend(): pl.pallas_call(functools.partial(attend_kernel, heads), grid=(8,), out_sh...  47 us
  transfers between devices with their start and end apart: 13, of which 3 were waited for; matrix products, arithmetic and copies ran while one was open for 10% of the time, Pallas kernels for 79%

profile of v5, /device:TPU:19, one launch (start us, length us, event | category | flops | bytes accessed | tf_op | source)
XLA Modules:
  0.0 662.5 jit_solution(9903092687734380516)
XLA Ops:
  8.0 54.4 %opening.1 = (bf16[256,2048]{1,0:T(8,128)(2,1)}, bf16[512,768]{1,0:T(8,128)(2,1)}, bf16[512,1024]{1,0:T(8,128)(2,1)}, bf16[512,1024]{1,0:T(8,128)(2,1)}) custom-call(bf16[256,2048]{1,0:T(8,128)(2,1)} %x_ref.1, bf16[64,6144]{1,0:T(8,128)(2,1)} %refs_0_.1, bf16[64,8192]{1,0:T(8,128)(2,1)} %refs_1_.1, bf16[64,8192]{1,0:T(8,128)(2,1)} %refs_2_.1), custom_call_target="tpu_custom_call" | custom-call | tf_op jit(solution)/shard_map/opening/pallas_call | solution.py:610
  63.3 13.4 %collective-permute-start = (s32[1,2052]{1,0:T(1,128)S(1)}, s32[1,2052]{1,0:T(1,128)S(1)}, u32[]{:S(2)}, u32[]{:S(2)}) collective-permute-start(s32[1,2052]{1,0:T(1,128)S(1)} %pad_add_fusion), channel_id=1, source_target_pairs={{0,0},{1,1},{2,16},{3,17},{4,8},{5,9},{6,24},{7,25},{8,18},{9,19},... | collective-permute-start | bytes 24632 | tf_op jit(solution)/shard_map/ppermute | solution.py:956
  78.1 38.7 %plane_gather.2 = bf16[8,256,2048]{2,1,0:T(8,128)(2,1)S(1)} custom-call(bf16[256,2048]{1,0:T(8,128)(2,1)S(1)} %fusion.7.x_ref), custom_call_target="tpu_custom_call" | custom-call | tf_op jit(solution)/shard_map/plane_gather/pallas_call | solution.py:294
  116.9 3.2 copy-done.1
  121.6 1.9 broadcast_in_dim_reshape.10.place_ref.first_ref
  123.6 3.2 collective-permute-start.1
  128.6 10.2 %collective-permute-done.1 = bf16[256,2048]{1,0:T(8,128)(2,1)} collective-permute-done((bf16[256,2048]{1,0:T(8,128)(2,1)}, bf16[256,2048]{1,0:T(8,128)(2,1)}, u32[]{:S(2)}, u32[]{:S(2)}) %collective-permute-start.1) | collective-permute-done | bytes 1048608 | tf_op jit(solution)/shard_map/ppermute | solution.py:950
  138.8 5.0 collective-permute-start.2
  144.9 2.5 copy.58
  147.4 10.5 %add_convert_fusion.head_ref = bf16[2048,768]{1,0:T(8,128)(2,1)} fusion(f32[768]{0:T(1024)S(1)} %dynamic_slice.10, bf16[2048,2048]{1,0:T(8,128)(2,1)} %bitcast.70, bf16[2048,768]{1,0:T(8,128)(2,1)S(1)} %bitcast.80), kind=kOutput, calls=%fused_computation.2 | convolution fusion | flops 6445596672 | bytes 14683136 | tf_op jit(solution)/shard_map/dot_general | solution.py:44
  157.9 47.0 %attend.1 = (bf16[2048,256]{1,0:T(8,128)(2,1)}, f32[2,8,2048]{2,1,0:T(8,128)}, f32[256,2048]{1,0:T(8,128)}) custom-call(bf16[2048,768]{1,0:T(8,128)(2,1)} %add_convert_fusion.head_ref, s32[2048,1]{1,0:T(8,128)} %broadcast_in_dim_reshape.10.place_ref.first_ref, s32[1,2048]{1,0:T(1,128)} %copy-done.20, s32[1,2048]{1,0:T(1,128)} %compare_select_fusion.1.last_ref, ...), custom_call_target="tpu_custom_call" | custom-call | tf_op jit(solution)/shard_map/attend/pallas_call | solution.py:646
  205.0 2.0 fusion.20
  209.5 43.0 %plane_gather.3 = bf16[8,256,2048]{2,1,0:T(8,128)(2,1)S(1)} custom-call(bf16[256,2048]{1,0:T(8,128)(2,1)S(1)} %collective-permute-done.2.x_ref), custom_call_target="tpu_custom_call" | custom-call | tf_op jit(solution)/shard_map/plane_gather/pallas_call | solution.py:294
  252.6 3.2 copy-done
  255.8 48.2 %hidden.1 = (bf16[8,256,2048]{2,1,0:T(8,128)(2,1)}, bf16[8,256,1024]{2,1,0:T(8,128)(2,1)}, f32[8,256,1024]{2,1,0:T(8,128)}, bf16[2048,1024]{1,0:T(8,128)(2,1)}) custom-call(bf16[256,2048]{1,0:T(8,128)(2,1)} %add_convert_fusion.2.middle_ref, bf16[8,256,2048]{2,1,0:T(8,128)(2,1)} %copy-done, bf16[2048,1024]{1,0:T(8,128)(2,1)} %all-gather.9.cloned.1.call-done.expand_ref, ...), custom_call_target="tpu_custom_call" | custom-call | tf_op jit(solution)/shard_map/hidden/pallas_call | solution.py:871
  304.0 12.3 %all-gather.11.cloned.1.call-done.shrink_ref.weight_ref = bf16[2048,1024]{1,0:T(8,128)(2,1)} async-done(((bf16[512,1024]{1,0:T(8,128)(2,1)}), bf16[2048,1024]{1,0:T(8,128)(2,1)}) %all-gather.11.cloned.1.call-update) | async-done | bytes 4194320 | tf_op jit(solution)/shard_map/all_gather | solution.py:967
  316.4 55.7 %hidden_back.1 = (bf16[8,256,1024]{2,1,0:T(8,128)(2,1)}, f32[256,2048]{1,0:T(8,128)}, bf16[2048,1024]{1,0:T(8,128)(2,1)}) custom-call(bf16[8,256,2048]{2,1,0:T(8,128)(2,1)} %copy-done, bf16[8,256,2048]{2,1,0:T(8,128)(2,1)} %get-tuple-element.73.middle_ref, f32[8,256,1024]{2,1,0:T(8,128)} %get-tuple-element.74.rise_ref, ...), custom_call_target="tpu_custom_call" | custom-call | tf_op jit(solution)/shard_map/hidden_back/pallas_call | solution.py:935
  373.3 1.9 select_select_fusion.last_ref
  375.2 45.1 %product_reduce.2 = f32[256,2048]{1,0:T(8,128)} custom-call(bf16[8,256,1024]{2,1,0:T(8,128)(2,1)} %get-tuple-element.72, bf16[2048,1024]{1,0:T(8,128)(2,1)} %all-gather.11.cloned.1.call-done.shrink_ref.weight_ref), custom_call_target="tpu_custom_call" | custom-call | tf_op jit(solution)/shard_map/product_reduce/pallas_call | solution.py:437
  420.3 3.1 add_convert_fusion.1.homed_ref
  424.7 2.9 convert_reduce_fusion.4
  427.6 68.9 %attend_back.1 = (bf16[256,2048]{1,0:T(8,128)(2,1)}, bf16[2048,768]{1,0:T(8,128)(2,1)}, bf16[256,2048]{1,0:T(8,128)(2,1)}) custom-call(bf16[256,2048]{1,0:T(8,128)(2,1)} %get-tuple-element.112.branch_ref, bf16[256,2048]{1,0:T(8,128)(2,1)} %add_convert_fusion.1.homed_ref, bf16[2048,768]{1,0:T(8,128)(2,1)} %add_convert_fusion.head_ref, ...), custom_call_target="tpu_custom_call" | custom-call | tf_op jit(solution)/shard_map/attend_back/pallas_call | solution.py:776
  496.6 10.4 %convolution_convert_fusion = bf16[2048,768]{1,0:T(8,128)(2,1)S(1)} fusion(bf16[2048,2048]{1,0:T(8,128)(2,1)} %bitcast.71, bf16[2048,768]{1,0:T(8,128)(2,1)} %get-tuple-element.89), kind=kOutput, calls=%fused_computation.3 | convolution fusion | flops 6444023808 | bytes 14680064 | tf_op jit(solution)/shard_map/dot_general | solution.py:50
  507.0 2.0 copy.68
  509.0 3.0 convert_reduce_fusion
  515.4 58.4 %product_reduce.3 = (f32[256,2048]{1,0:T(8,128)}, bf16[64,8192]{1,0:T(8,128)(2,1)}) custom-call(bf16[8,256,768]{2,1,0:T(8,128)(2,1)} %bitcast.73, bf16[2048,768]{1,0:T(8,128)(2,1)} %all-gather.7.cloned.1.call-done.weight_ref, bf16[512,1024]{1,0:T(8,128)(2,1)} %reduce-scatter.7.cloned.1.call-done.refs_0_), custom_call_target="tpu_custom_call" | custom-call | tf_op jit(solution)/shard_map/product_reduce/pallas_call | solution.py:437
  573.8 2.7 fusion.9
  577.7 2.8 convert_element_type.63
  580.6 1.8 fusion.13.homed_ref
  582.5 64.0 %closing.1 = (f32[192,128]{1,0:T(8,128)}, bf16[256,2048]{1,0:T(8,128)(2,1)}, bf16[64,6144]{1,0:T(8,128)(2,1)}, bf16[64,8192]{1,0:T(8,128)(2,1)}) custom-call(f32[192,128]{1,0:T(8,128)} %bitcast.85, bf16[256,2048]{1,0:T(8,128)(2,1)} %fusion.13.homed_ref, bf16[512,768]{1,0:T(8,128)(2,1)} %reduce-scatter.9.cloned.1.call-done.refs_0_, ...), custom_call_target="tpu_custom_call" | custom-call | tf_op jit(solution)/shard_map/closing/pallas_call | solution.py:485
  646.5 2.8 convert_element_type.64
  651.8 1.8 convert_element_type.62
  (157 shorter events, 21.6 us)
Async XLA Ops:
  7.2 55.3 %all-gather.5.cloned.1.call-start = ((), (), s32[]{:S(2)}) async-start(), calls=%async_computation.4 | async-start | bytes 1310720 | tf_op jit(solution)/shard_map/all_gather | solution.py:967
  7.9 55.4 %copy-start.31 = (s32[1,2048]{1,0:T(1,128)S(1)}, s32[1,2048]{1,0:T(1,128)}, u32[]{:S(2)}) copy-start(s32[1,2048]{1,0:T(1,128)} %param.31) | copy-start | bytes 24580
  7.9 55.4 %copy-start.32 = (s32[1,4]{1,0:T(1,128)S(1)}, s32[1,4]{1,0:T(1,128)}, u32[]{:S(2)}) copy-start(s32[1,4]{1,0:T(1,128)} %param.32) | copy-start | bytes 52
  7.9 137.0 %all-gather.7.cloned.1.call-start = ((), (), s32[]{:S(2)}) async-start(), calls=%async_computation.5 | async-start | bytes 3932160 | tf_op jit(solution)/shard_map/all_gather | solution.py:967
  62.4 14.4 %copy-start.6 = (bf16[256,2048]{1,0:T(8,128)(2,1)S(1)}, bf16[256,2048]{1,0:T(8,128)(2,1)}, u32[]{:S(2)}) copy-start(bf16[256,2048]{1,0:T(8,128)(2,1)} %get-tuple-element.59) | copy-start | bytes 3145732
  62.5 193.3 %all-gather.9.cloned.1.call-start = ((), (), s32[]{:S(2)}) async-start(), calls=%async_computation.6 | async-start | bytes 5242880 | tf_op jit(solution)/shard_map/all_gather | solution.py:967
  62.5 15.0 %copy-start.24 = (f32[2048]{0:T(1024)S(1)}, f32[2048]{0:T(1024)}, u32[]{:S(2)}) copy-start(f32[2048]{0:T(1024)} %param.18) | copy-start | bytes 24580
  62.5 15.0 %copy-start.25 = (f32[2048]{0:T(1024)S(1)}, f32[2048]{0:T(1024)}, u32[]{:S(2)}) copy-start(f32[2048]{0:T(1024)} %param.19) | copy-start | bytes 24580
  63.2 253.1 %all-gather.11.cloned.1.call-start = ((), (), s32[]{:S(2)}) async-start(), calls=%async_computation.7 | async-start | bytes 5242880 | tf_op jit(solution)/shard_map/all_gather | solution.py:967
  63.3 58.2 %collective-permute-start = (s32[1,2052]{1,0:T(1,128)S(1)}, s32[1,2052]{1,0:T(1,128)S(1)}, u32[]{:S(2)}, u32[]{:S(2)}) collective-permute-start(s32[1,2052]{1,0:T(1,128)S(1)} %pad_add_fusion), channel_id=1, source_target_pairs={{0,0},{1,1},{2,16},{3,17},{4,8},{5,9},{6,24},{7,25},{8,18},{9,19},... | collective-permute-start | bytes 24632 | tf_op jit(solution)/shard_map/ppermute | solution.py:956
  76.7 419.8 %reduce-scatter.5.cloned.1.call-start = ((), (), s32[]{:S(2)}) async-start(), calls=%async_computation.8 | async-start | bytes 5242880 | tf_op jit(solution)/shard_map/reduce_scatter | solution.py:982
  78.1 48.6 %copy-start.15 = (bf16[256,2048]{1,0:T(8,128)(2,1)S(1)}, bf16[256,2048]{1,0:T(8,128)(2,1)}, u32[]{:S(2)}) copy-start(bf16[256,2048]{1,0:T(8,128)(2,1)} %all-gather.5.cloned.1.call-done) | copy-start | bytes 3145732
  116.9 3.2 copy-start.1
  121.6 22.2 %copy-start.20 = (s32[1,2048]{1,0:T(1,128)}, s32[1,2048]{1,0:T(1,128)S(1)}, u32[]{:S(2)}) copy-start(s32[1,2048]{1,0:T(1,128)S(1)} %broadcast_in_dim_reshape.9.first_ref.place_ref) | copy-start | bytes 24580
  123.6 15.2 %collective-permute-start.1 = (bf16[256,2048]{1,0:T(8,128)(2,1)}, bf16[256,2048]{1,0:T(8,128)(2,1)}, u32[]{:S(2)}, u32[]{:S(2)}) collective-permute-start(bf16[256,2048]{1,0:T(8,128)(2,1)} %param.33), channel_id=1, source_target_pairs={{0,0},{1,1},{2,18},{3,19},{4,12},{5,13},{6,30},{7,31},{8,16},{9,17... | collective-permute-start | bytes 3145736 | tf_op jit(solution)/shard_map/ppermute | solution.py:950
  126.9 16.9 %collective-permute-start.3 = (bf16[2,64,2048]{2,1,0:T(8,128)(2,1)S(1)}, bf16[2,64,2048]{2,1,0:T(8,128)(2,1)S(1)}, u32[]{:S(2)}, u32[]{:S(2)}) collective-permute-start(bf16[2,64,2048]{2,1,0:T(8,128)(2,1)S(1)} %bitcast.84), channel_id=1, source_target_pairs={{0,1},{1,0},{2,3},{3,2},{4,5},{5,4},{6,7},{7,6},{8,9},{9,8},{10,11... | collective-permute-start | bytes 1572872 | tf_op jit(solution)/shard_map/ppermute | solution.py:999
  138.8 70.7 %collective-permute-start.2 = (bf16[256,2048]{1,0:T(8,128)(2,1)}, bf16[256,2048]{1,0:T(8,128)(2,1)S(1)}, u32[]{:S(2)}, u32[]{:S(2)}) collective-permute-start(bf16[256,2048]{1,0:T(8,128)(2,1)} %collective-permute-done.1), channel_id=1, source_target_pairs={{0,0},{1,1},{18,16},{19,17},{12,8},{13,9},{30,24},{31,25},{16,18},... | collective-permute-start | bytes 3145736 | tf_op jit(solution)/shard_map/ppermute | solution.py:953
  157.9 47.0 %copy-start.26 = (f32[2048]{0:T(1024)S(1)}, f32[2048]{0:T(1024)}, u32[]{:S(2)}) copy-start(f32[2048]{0:T(1024)} %param.24) | copy-start | bytes 24580
  209.5 43.0 %copy-start.2 = (bf16[256,2048]{1,0:T(8,128)(2,1)}, bf16[256,2048]{1,0:T(8,128)(2,1)S(1)}, u32[]{:S(2)}) copy-start(bf16[256,2048]{1,0:T(8,128)(2,1)S(1)} %collective-permute-done.2.x_ref) | copy-start | bytes 3145732
  252.5 3.2 copy-start
  304.0 205.0 %reduce-scatter.7.cloned.1.call-start = ((), (), s32[]{:S(2)}) async-start(), calls=%async_computation.9 | async-start | bytes 5242880 | tf_op jit(solution)/shard_map/reduce_scatter | solution.py:982
  372.1 205.6 %reduce-scatter.9.cloned.1.call-start = ((), (), s32[]{:S(2)}) async-start(), calls=%async_computation.10 | async-start | bytes 3932160 | tf_op jit(solution)/shard_map/reduce_scatter | solution.py:982
  375.2 45.1 %copy-start.5 = (f32[256,2048]{1,0:T(8,128)S(1)}, f32[256,2048]{1,0:T(8,128)}, u32[]{:S(2)}) copy-start(f32[256,2048]{1,0:T(8,128)} %copy-done.4) | copy-start | bytes 6291460
  375.2 45.1 %copy-start.28 = (f32[2048]{0:T(1024)S(1)}, f32[2048]{0:T(1024)}, u32[]{:S(2)}) copy-start(f32[2048]{0:T(1024)} %param.30) | copy-start | bytes 24580
  420.3 3.1 copy-start.12
  509.0 142.8 %reduce-scatter.11.cloned.1.call-start = ((), (), s32[]{:S(2)}) async-start(), calls=%async_computation.11 | async-start | bytes 1310720 | tf_op jit(solution)/shard_map/reduce_scatter | solution.py:982
  509.0 3.3 copy-start.17
  513.5 63.0 %collective-permute-start.4 = (bf16[2,64,2048]{2,1,0:T(8,128)(2,1)S(1)}, bf16[2,64,2048]{2,1,0:T(8,128)(2,1)S(1)}, u32[]{:S(2)}, u32[]{:S(2)}) collective-permute-start(bf16[2,64,2048]{2,1,0:T(8,128)(2,1)S(1)} %select_bitcast_fusion), channel_id=1, source_target_pairs={{0,1},{1,0},{2,3},{3,2},{4,5},{5,4},{6,7},{7,6},{8,9},{9,8},{10,11... | collective-permute-start | bytes 1572872 | tf_op jit(solution)/shard_map/ppermute | solution.py:1018
  515.4 58.4 %copy-start.7 = (bf16[256,2048]{1,0:T(8,128)(2,1)S(1)}, bf16[256,2048]{1,0:T(8,128)(2,1)}, u32[]{:S(2)}) copy-start(bf16[256,2048]{1,0:T(8,128)(2,1)} %get-tuple-element.59) | copy-start | bytes 3145732
  646.5 4.0 copy-start.22
  649.3 4.3 copy-start.16
  650.5 4.0 copy-start.18
  (14 other events, 25.1 us)
Sparse Core Ops, SparseCore 0:
  9.6 38.8 all-gather.4
  62.6 72.7 all-gather.6
  137.0 97.4 all-gather.8
  235.9 80.4 all-gather.10
  318.5 77.3 reduce-scatter.4
  398.1 95.7 reduce-scatter.6
  509.1 62.9 reduce-scatter.8
  577.8 48.4 reduce-scatter.10

commit v6 on v5

--- a/solution.py
+++ b/solution.py
@@ -712,7 +712,7 @@
         for one in (across_low, up_high, across_high, up_low, own, far_low, far_high, pass_across, pass_up, pass_low, pass_high):
             one.wait_send()
 
-def attend_back_kernel(heads, branch_ref, homed_ref, head_ref, mixing_ref, attended_ref, total_ref, place_ref, first_ref, last_ref, part_ref, out_ref, homed_out, turned, key_sum, value_sum, part_sum, slots, load, send, recv, *cargo):
+def attend_back_kernel(heads, branch_ref, homed_ref, head_ref, mixing_ref, attended_ref, total_ref, place_ref, first_ref, last_ref, part_ref, out_ref, homed_out, sums_ref, turned, key_sum, value_sum, part_sum, slots, load, send, recv, *cargo):
     ids = plane_ids()
     step = pl.program_id(0)
     home_start, home_finish = home_cargo(homed_ref, homed_out, *cargo)
@@ -730,6 +730,7 @@
         key_sum[...] = jnp.zeros_like(key_sum)
         value_sum[...] = jnp.zeros_like(value_sum)
         part_sum[...] = jnp.zeros_like(part_sum)
+        sums_ref[...] = jnp.zeros_like(sums_ref)
         greet_all(ids[:3], True)
         home_start()
         first.wait()
@@ -753,13 +754,17 @@
         value_sum[h] += product(soft.astype(jnp.bfloat16), slope)
         key_sum[h] += product(score_slope, queries)
         query_slope = product(turned[h], score_slope)
-        out_ref[here, 3 * h * size:(3 * h + 1) * size] = (query_slope.T * scale).astype(jnp.bfloat16)
+        query_slope = (query_slope.T * scale).astype(jnp.bfloat16)
+        out_ref[here, 3 * h * size:(3 * h + 1) * size] = query_slope
+        sums_ref[:, 3 * h * size:(3 * h + 1) * size] += jnp.sum(query_slope.astype(jnp.float32), axis=0, keepdims=True)
 
     @pl.when(step == 7)
     def _():
         for h in range(heads):
             out_ref[:, (3 * h + 1) * size:(3 * h + 2) * size] = (key_sum[h] * scale).astype(jnp.bfloat16)
-            out_ref[:, (3 * h + 2) * size:(3 * h + 3) * size] = value_sum[h].astype(jnp.bfloat16)
+            value_slope = value_sum[h].astype(jnp.bfloat16)
+            out_ref[:, (3 * h + 2) * size:(3 * h + 3) * size] = value_slope
+            sums_ref[:, (3 * h + 2) * size:(3 * h + 3) * size] = jnp.sum(value_slope.astype(jnp.float32), axis=0, keepdims=True)
         part_ref[...] = part_sum[...].astype(jnp.bfloat16)
         home_finish()
 
@@ -772,8 +777,8 @@
         slopes = product_transposed(every, mixing).astype(jnp.bfloat16)
         part = row_outer(attended, every).astype(jnp.bfloat16)
         slopes = attention_backward(packed, totals, slopes, places, key_last, heads)
-        return (part, slopes, from_plane(homed))
-    return pl.pallas_call(functools.partial(attend_back_kernel, heads), grid=(8,), out_shape=[jax.ShapeDtypeStruct(mixing.shape, jnp.bfloat16), jax.ShapeDtypeStruct((rows, columns), jnp.bfloat16), jax.ShapeDtypeStruct(homed.shape, homed.dtype)], in_specs=[ANY] * 2 + [VMEM] * 7, out_specs=[VMEM, VMEM, ANY], scratch_shapes=[pltpu.VMEM((heads, size, rows), jnp.bfloat16), pltpu.VMEM((heads, rows, size), jnp.float32), pltpu.VMEM((heads, rows, size), jnp.float32), pltpu.VMEM(mixing.shape, jnp.float32), pltpu.VMEM((8, token_rows, width), jnp.bfloat16), DMA, DMA((11,)), DMA((11,)), DMA, DMA, DMA], compiler_params=remote_params(collective_id, 62), name='attend_back')(branch_slope, homed, packed, mixing, attended, totals, places[None, :], places[:, None], key_last[:, None])
+        return (part, slopes, from_plane(homed), jnp.sum(slopes.astype(jnp.float32), axis=0, keepdims=True))
+    return pl.pallas_call(functools.partial(attend_back_kernel, heads), grid=(8,), out_shape=[jax.ShapeDtypeStruct(mixing.shape, jnp.bfloat16), jax.ShapeDtypeStruct((rows, columns), jnp.bfloat16), jax.ShapeDtypeStruct(homed.shape, homed.dtype), jax.ShapeDtypeStruct((1, columns), jnp.float32)], in_specs=[ANY] * 2 + [VMEM] * 7, out_specs=[VMEM, VMEM, ANY, VMEM], scratch_shapes=[pltpu.VMEM((heads, size, rows), jnp.bfloat16), pltpu.VMEM((heads, rows, size), jnp.float32), pltpu.VMEM((heads, rows, size), jnp.float32), pltpu.VMEM(mixing.shape, jnp.float32), pltpu.VMEM((8, token_rows, width), jnp.bfloat16), DMA, DMA((11,)), DMA((11,)), DMA, DMA, DMA], compiler_params=remote_params(collective_id, 62), name='attend_back')(branch_slope, homed, packed, mixing, attended, totals, places[None, :], places[:, None], key_last[:, None])
 
 def add_outer(total, left, right):
     turned = left.T
@@ -871,7 +876,7 @@
     every, active, rise, part = pl.pallas_call(hidden_kernel, grid=(8,), out_shape=[jax.ShapeDtypeStruct((8, rows, width), middle.dtype), jax.ShapeDtypeStruct((8, rows, inner), jnp.bfloat16), jax.ShapeDtypeStruct((8, rows, inner), jnp.float32), jax.ShapeDtypeStruct((width, inner), jnp.bfloat16)], in_specs=[ANY, ANY, ANY, VMEM], out_specs=[ANY] * 4, scratch_shapes=[pltpu.VMEM((8, rows, width), middle.dtype), pltpu.VMEM((2, rows, width), jnp.bfloat16), pltpu.VMEM((2, rows, inner), jnp.bfloat16), pltpu.VMEM((2, rows, inner), jnp.float32), pltpu.VMEM((width, inner), jnp.float32), DMA, DMA((11,)), DMA((11,)), DMA((8,)), DMA((2,)), DMA((2,)), DMA((2,)), *row_loads_scratch(expand_slice.shape, expand_slice.dtype), *row_loads_scratch(expand_slice.shape, jnp.bfloat16)], compiler_params=remote_params(collective_id, 60), name='hidden')(middle, cotangent_all.reshape(8, rows, width), expand_slice, offset[None, :])
     return (every.reshape(count * rows, width), active.reshape(count * rows, inner), rise.reshape(count * rows, inner), part)
 
-def hidden_back_kernel(cotangent_ref, middle_ref, rise_ref, shrink_ref, expand_ref, slope_ref, out_ref, part_ref, cotangents, middles, rises, slopes, total, fetches, store, shrink, shrink_load, expand, expand_load, narrow, part_store, *refs):
+def hidden_back_kernel(cotangent_ref, middle_ref, rise_ref, shrink_ref, expand_ref, slope_ref, out_ref, part_ref, sums_ref, cotangents, middles, rises, slopes, total, fetches, store, shrink, shrink_load, expand, expand_load, narrow, part_store, *refs):
     ids = plane_ids()
     step = pl.program_id(0)
 
@@ -891,6 +896,7 @@
         for one in fetch(0, 0):
             one.start()
         total[...] = jnp.zeros_like(total)
+        sums_ref[...] = jnp.zeros_like(sums_ref)
         greet(ids[:3])
         for one in rows_in:
             one.wait()
@@ -911,6 +917,7 @@
 
     def before():
         add_outer(total, middles[turn], slopes[turn])
+        sums_ref[...] += jnp.sum(slopes[turn].astype(jnp.float32), axis=0, keepdims=True)
 
         @pl.when(step == 7)
         def _():
@@ -930,10 +937,11 @@
         slope = (product(cotangent_all, rep_rows_last(shrink_slice)) * rise).astype(jnp.bfloat16)
         part = product_transposed(slope, rep_rows_last(expand_slice)).astype(jnp.bfloat16)
         normed = lax.psum_scatter(part, PLANE, scatter_dimension=0, tiled=True).astype(jnp.float32)
-        return (slope, normed, rep_rows_first(row_outer(middle_all, slope)))
+        sums = jnp.sum(slope.astype(jnp.float32), axis=0)
+        return (slope, normed, rep_rows_first(row_outer(middle_all, slope)), sums)
     pieces = (8, token_rows, width)
-    slope, normed, part = pl.pallas_call(hidden_back_kernel, grid=(8,), out_shape=[jax.ShapeDtypeStruct((8, token_rows, inner), jnp.bfloat16), jax.ShapeDtypeStruct((token_rows, width), jnp.float32), jax.ShapeDtypeStruct((width, inner), jnp.bfloat16)], in_specs=[ANY] * 5, out_specs=[ANY, VMEM, ANY], scratch_shapes=[pltpu.VMEM((2, token_rows, width), jnp.bfloat16), pltpu.VMEM((2, token_rows, width), jnp.bfloat16), pltpu.VMEM((2, token_rows, inner), jnp.float32), pltpu.VMEM((2, token_rows, inner), jnp.bfloat16), pltpu.VMEM((width, inner), jnp.float32), DMA((3, 2)), DMA((2,)), *row_loads_scratch(shrink_slice.shape, shrink_slice.dtype), *row_loads_scratch(expand_slice.shape, expand_slice.dtype), *row_loads_scratch(expand_slice.shape, jnp.bfloat16), *reduce_scratch(token_rows, width)], compiler_params=remote_params(collective_id, 63), name='hidden_back')(cotangent_all.reshape(pieces), middle_all.reshape(pieces), rise.reshape(8, token_rows, inner), shrink_slice, expand_slice)
-    return (slope.reshape(rows, inner), normed, part)
+    slope, normed, part, sums = pl.pallas_call(hidden_back_kernel, grid=(8,), out_shape=[jax.ShapeDtypeStruct((8, token_rows, inner), jnp.bfloat16), jax.ShapeDtypeStruct((token_rows, width), jnp.float32), jax.ShapeDtypeStruct((width, inner), jnp.bfloat16), jax.ShapeDtypeStruct((1, inner), jnp.float32)], in_specs=[ANY] * 5, out_specs=[ANY, VMEM, ANY, VMEM], scratch_shapes=[pltpu.VMEM((2, token_rows, width), jnp.bfloat16), pltpu.VMEM((2, token_rows, width), jnp.bfloat16), pltpu.VMEM((2, token_rows, inner), jnp.float32), pltpu.VMEM((2, token_rows, inner), jnp.bfloat16), pltpu.VMEM((width, inner), jnp.float32), DMA((3, 2)), DMA((2,)), *row_loads_scratch(shrink_slice.shape, shrink_slice.dtype), *row_loads_scratch(expand_slice.shape, expand_slice.dtype), *row_loads_scratch(expand_slice.shape, jnp.bfloat16), *reduce_scratch(token_rows, width)], compiler_params=remote_params(collective_id, 63), name='hidden_back')(cotangent_all.reshape(pieces), middle_all.reshape(pieces), rise.reshape(8, token_rows, inner), shrink_slice, expand_slice)
+    return (slope.reshape(rows, inner), normed, part, sums[0])
 
 def plane_moves():
     groups, reps, subs = (lax.axis_size(n) for n in EVERY)
@@ -1031,13 +1039,13 @@
     plane_rows = plane_count * token_rows
     facts = to_plane_at_once(jnp.concatenate([placement, slot_lengths], axis=1))[0]
     mixing_own = rep_rows(mixing_weight)
-    moved_input, joint_own, expand_own, shrink_own = opening(layer_input, (joint_weight, expand_weight, shrink_weight), 12)
+    moved_input, joint_own, expand_own = opening(layer_input, (joint_weight, expand_weight), 12)
     joint_own, mixing_own = lax.optimization_barrier((joint_own, mixing_own))
     input_float = moved_input.astype(jnp.float32)
     joint_every = rep_rows(joint_own)
     entry_normal, entry_inverse = norm_terms(input_float)
     entry_normed = (entry_normal * entry_gain + entry_shift).astype(jnp.bfloat16)
-    entry_all, = plane_gather(entry_normed, (), 1)
+    entry_all, shrink_own = plane_gather(entry_normed, (shrink_weight,), 1)
     cotangent, facts, entry_all = lax.optimization_barrier((cotangent, facts, entry_all))
     cotangent = to_door(cotangent)
     places = plane_order(facts[:placement.shape[1]])
@@ -1062,7 +1070,7 @@
     offset_local = lax.dynamic_slice_in_dim(expand_offset, plane_index * hidden_local, hidden_local)
     middle_all, activated, rise, shrink_part = hidden(middle_normed, cotangent_all, expand_slice, offset_local, 5)
     shrink_sums = rep_sums(shrink_part)
-    expanded_slope, normed_slope, expand_part = hidden_back(cotangent_all, middle_all, rise, shrink_slice, expand_slice, token_rows, 6)
+    expanded_slope, normed_slope, expand_part, expanded_sums = hidden_back(cotangent_all, middle_all, rise, shrink_slice, expand_slice, token_rows, 6)
     expand_sums = rep_sums(expand_part)
     activated, normed_slope = lax.optimization_barrier((activated, normed_slope))
     shrunk, = product_reduce(activated.reshape(plane_count, token_rows, hidden_local), shrink_slice, None, None, 8)
@@ -1071,7 +1079,7 @@
     cotangent_float = cotangent.astype(jnp.float32)
     residual_slope = cotangent_float + norm_back(normed_slope, middle_gain, middle_normal, middle_inverse)
     branch_slope = residual_slope.astype(jnp.bfloat16)
-    mixing_part, joint_slope, layer_output = attend_back(branch_slope, own_output, heads_kept, mixing_slice, attended, log_totals, places, key_last, local_heads, 7)
+    mixing_part, joint_slope, layer_output, slope_sums = attend_back(branch_slope, own_output, heads_kept, mixing_slice, attended, log_totals, places, key_last, local_heads, 7)
     shrink_sums, joint_slope = lax.optimization_barrier((shrink_sums, joint_slope))
     joint_part = rep_rows_first(row_outer(entry_all, joint_slope))
     joint_part, joint_slope, expand_sums, mixing_part = lax.optimization_barrier((joint_part, joint_slope, expand_sums, mixing_part))
@@ -1081,11 +1089,11 @@
     mixing_sums = rep_sums(mixing_part)
     entry_slope, expand_rows = product_reduce(joint_slope.reshape(plane_count, token_rows, 3 * head_columns), joint_every, expand_sums, None, 9)
     own_gradient = (residual_slope + norm_back(entry_slope, entry_gain, entry_normal, entry_inverse)).astype(jnp.bfloat16)
-    slope_sums = jnp.sum(joint_slope.astype(jnp.float32), axis=0).reshape(local_heads, 3, head_size)
+    slope_sums = slope_sums.reshape(local_heads, 3, head_size)
 
     def placed(piece, whole_size):
         return lax.dynamic_update_slice_in_dim(jnp.zeros((whole_size,), jnp.float32), piece, plane_index * piece.shape[0], 0)
-    small = [jnp.sum(entry_slope * entry_normal, axis=0), jnp.sum(entry_slope, axis=0), placed(slope_sums[:, 0].reshape(-1), width), placed(slope_sums[:, 2].reshape(-1), width), jnp.sum(branch_slope.astype(jnp.float32), axis=0), jnp.sum(normed_slope * middle_normal, axis=0), jnp.sum(normed_slope, axis=0), placed(jnp.sum(expanded_slope.astype(jnp.float32), axis=0), hidden_width), jnp.sum(cotangent_float, axis=0)]
+    small = [jnp.sum(entry_slope * entry_normal, axis=0), jnp.sum(entry_slope, axis=0), placed(slope_sums[:, 0].reshape(-1), width), placed(slope_sums[:, 2].reshape(-1), width), jnp.sum(branch_slope.astype(jnp.float32), axis=0), jnp.sum(normed_slope * middle_normal, axis=0), jnp.sum(normed_slope, axis=0), placed(expanded_sums, hidden_width), jnp.sum(cotangent_float, axis=0)]
     small_own = jnp.concatenate(small).reshape(-1, 128)
     small_all, input_gradient, joint_rows, shrink_rows = closing(small_own, own_gradient, (joint_sums, shrink_sums), 10)
     shrink_gradient = shrink_rows.astype(jnp.float32)

time: 667 us -> 661 us (level)
    all_gather x4, waiting for transfers between devices: 12.4 us -> 1.15 us  [rep_rows(): return lax.all_gather(own, 'rep', axis=0, tiled=True)]
    ppermute x1, waiting for transfers between devices: 0.4 us -> 10 us  [to_keeper(): lax.ppermute(array, EVERY, [(door, away) for _, door, away in plane_moves...]
  transfers between devices with their start and end apart: 13 -> 13, of which waited for: 3 -> 3; matrix products, arithmetic and copies ran while one was open for 10% -> 9% of each run, Pallas kernels for 79% -> 81%
where the time goes in v6:
time: 661 us; the launch traced here: 656 us
  Pallas kernels  529 us (80%)
  other arithmetic  30 us (5%)
  waiting for transfers between devices  23.3 us (4%)
  local copies, waits for them, and re-layouts  20.9 us (3%)
  matrix products  20.9 us (3%)
  starting transfers between devices  17.8 us (3%)
  between operations  15 us (2%)
    pallas_call x2, Pallas kernels, product_reduce(): pl.pallas_call(functools.partial(product_reduce_kernel, owns, homes), gri...  104 us
    pallas_call x2, Pallas kernels, plane_gather(): pl.pallas_call(functools.partial(gather_kernel, number), grid=(8,), out_s...  87.5 us
    pallas_call x1, Pallas kernels, attend_back(): pl.pallas_call(functools.partial(attend_back_kernel, heads), grid=(8,), o...  68.9 us
    pallas_call x1, Pallas kernels, closing(): pl.pallas_call(functools.partial(closing_kernel, number), out_shape=[jax....  64.8 us
    pallas_call x1, Pallas kernels, hidden_back(): pl.pallas_call(hidden_back_kernel, grid=(8,), out_shape=[jax.ShapeDtypeSt...  55.4 us
    pallas_call x1, Pallas kernels, opening(): pl.pallas_call(opening_kernel, out_shape=[jax.ShapeDtypeStruct(x.shape, x...  50.5 us
    pallas_call x1, Pallas kernels, hidden(): pl.pallas_call(hidden_kernel, grid=(8,), out_shape=[jax.ShapeDtypeStruct(...  48.7 us
    pallas_call x1, Pallas kernels, attend(): pl.pallas_call(functools.partial(attend_kernel, heads), grid=(8,), out_sh...  48.6 us
  transfers between devices with their start and end apart: 13, of which 3 were waited for; matrix products, arithmetic and copies ran while one was open for 9% of the time, Pallas kernels for 81%

profile of v6, /device:TPU:19, one launch (start us, length us, event | category | flops | bytes accessed | tf_op | source)
XLA Modules:
  0.0 656.4 jit_solution(5733836496563465036)
XLA Ops:
  8.0 50.5 %opening.1 = (bf16[256,2048]{1,0:T(8,128)(2,1)}, bf16[512,768]{1,0:T(8,128)(2,1)}, bf16[512,1024]{1,0:T(8,128)(2,1)}) custom-call(bf16[256,2048]{1,0:T(8,128)(2,1)} %x_ref.1, bf16[64,6144]{1,0:T(8,128)(2,1)} %refs_0_.2, bf16[64,8192]{1,0:T(8,128)(2,1)} %refs_1_.1), custom_call_target="tpu_custom_call" | custom-call | tf_op jit(solution)/shard_map/opening/pallas_call | solution.py:610
  59.4 11.2 %collective-permute-start = (s32[1,2052]{1,0:T(1,128)S(1)}, s32[1,2052]{1,0:T(1,128)S(1)}, u32[]{:S(2)}, u32[]{:S(2)}) collective-permute-start(s32[1,2052]{1,0:T(1,128)S(1)} %pad_add_fusion), channel_id=1, source_target_pairs={{0,0},{1,1},{2,16},{3,17},{4,8},{5,9},{6,24},{7,25},{8,18},{9,19},... | collective-permute-start | bytes 24632 | tf_op jit(solution)/shard_map/ppermute | solution.py:964
  71.9 49.3 %plane_gather.2 = (bf16[8,256,2048]{2,1,0:T(8,128)(2,1)S(1)}, bf16[512,1024]{1,0:T(8,128)(2,1)}) custom-call(bf16[256,2048]{1,0:T(8,128)(2,1)S(1)} %fusion.7.x_ref, bf16[64,8192]{1,0:T(8,128)(2,1)S(1)} %copy-done.3), custom_call_target="tpu_custom_call" | custom-call | tf_op jit(solution)/shard_map/plane_gather/pallas_call | solution.py:294
  121.3 3.2 copy-done.4
  126.3 1.9 broadcast_in_dim_reshape.10.place_ref.first_ref
  128.2 1.9 collective-permute-start.1
  131.6 10.6 %collective-permute-done.1 = bf16[256,2048]{1,0:T(8,128)(2,1)} collective-permute-done((bf16[256,2048]{1,0:T(8,128)(2,1)}, bf16[256,2048]{1,0:T(8,128)(2,1)}, u32[]{:S(2)}, u32[]{:S(2)}) %collective-permute-start.1) | collective-permute-done | bytes 1048608 | tf_op jit(solution)/shard_map/ppermute | solution.py:958
  142.2 3.4 collective-permute-start.2
  146.8 2.2 copy.58
  149.0 10.4 %add_convert_fusion.head_ref = bf16[2048,768]{1,0:T(8,128)(2,1)} fusion(f32[768]{0:T(1024)S(1)} %dynamic_slice.10, bf16[2048,2048]{1,0:T(8,128)(2,1)} %bitcast.71, bf16[2048,768]{1,0:T(8,128)(2,1)S(1)} %bitcast.81), kind=kOutput, calls=%fused_computation | convolution fusion | flops 6445596672 | bytes 14683136 | tf_op jit(solution)/shard_map/dot_general | solution.py:44
  159.4 48.6 %attend.1 = (bf16[2048,256]{1,0:T(8,128)(2,1)}, f32[2,8,2048]{2,1,0:T(8,128)}, f32[256,2048]{1,0:T(8,128)}) custom-call(bf16[2048,768]{1,0:T(8,128)(2,1)} %add_convert_fusion.head_ref, s32[2048,1]{1,0:T(8,128)} %broadcast_in_dim_reshape.10.place_ref.first_ref, s32[1,2048]{1,0:T(1,128)} %copy-done.18, s32[1,2048]{1,0:T(1,128)} %compare_select_fusion.1.last_ref, ...), custom_call_target="tpu_custom_call" | custom-call | tf_op jit(solution)/shard_map/attend/pallas_call | solution.py:646
  208.0 2.0 fusion.20
  210.7 1.4 add_convert_fusion.2.middle_ref
  212.2 10.0 %collective-permute-done.2.x_ref = bf16[256,2048]{1,0:T(8,128)(2,1)S(1)} collective-permute-done((bf16[256,2048]{1,0:T(8,128)(2,1)}, bf16[256,2048]{1,0:T(8,128)(2,1)S(1)}, u32[]{:S(2)}, u32[]{:S(2)}) %collective-permute-start.2) | collective-permute-done | bytes 1048608 | tf_op jit(solution)/shard_map/ppermute | solution.py:961
  222.2 38.2 %plane_gather.3 = bf16[8,256,2048]{2,1,0:T(8,128)(2,1)S(1)} custom-call(bf16[256,2048]{1,0:T(8,128)(2,1)S(1)} %collective-permute-done.2.x_ref), custom_call_target="tpu_custom_call" | custom-call | tf_op jit(solution)/shard_map/plane_gather/pallas_call | solution.py:294
  260.4 3.2 copy-done
  263.6 48.7 %hidden.1 = (bf16[8,256,2048]{2,1,0:T(8,128)(2,1)}, bf16[8,256,1024]{2,1,0:T(8,128)(2,1)}, f32[8,256,1024]{2,1,0:T(8,128)}, bf16[2048,1024]{1,0:T(8,128)(2,1)}) custom-call(bf16[256,2048]{1,0:T(8,128)(2,1)} %add_convert_fusion.2.middle_ref, bf16[8,256,2048]{2,1,0:T(8,128)(2,1)} %copy-done, bf16[2048,1024]{1,0:T(8,128)(2,1)} %all-gather.9.cloned.1.call-done.expand_ref, ...), custom_call_target="tpu_custom_call" | custom-call | tf_op jit(solution)/shard_map/hidden/pallas_call | solution.py:876
  313.6 55.4 %hidden_back.1 = (bf16[8,256,1024]{2,1,0:T(8,128)(2,1)}, f32[256,2048]{1,0:T(8,128)}, bf16[2048,1024]{1,0:T(8,128)(2,1)}, f32[1,1024]{1,0:T(1,128)}) custom-call(bf16[8,256,2048]{2,1,0:T(8,128)(2,1)} %copy-done, bf16[8,256,2048]{2,1,0:T(8,128)(2,1)} %get-tuple-element.76.middle_ref, f32[8,256,1024]{2,1,0:T(8,128)} %get-tuple-element.77.rise_ref, ...), custom_call_target="tpu_custom_call" | custom-call | tf_op jit(solution)/shard_map/hidden_back/pallas_call | solution.py:943
  370.2 1.9 select_select_fusion.last_ref
  372.1 45.5 %product_reduce.2 = f32[256,2048]{1,0:T(8,128)} custom-call(bf16[8,256,1024]{2,1,0:T(8,128)(2,1)} %get-tuple-element.75, bf16[2048,1024]{1,0:T(8,128)(2,1)} %all-gather.11.cloned.1.call-done.shrink_ref.weight_ref), custom_call_target="tpu_custom_call" | custom-call | tf_op jit(solution)/shard_map/product_reduce/pallas_call | solution.py:437
  417.6 3.1 add_convert_fusion.1.homed_ref
  421.9 2.9 convert_reduce_fusion.2
  424.9 68.9 %attend_back.1 = (bf16[256,2048]{1,0:T(8,128)(2,1)}, bf16[2048,768]{1,0:T(8,128)(2,1)}, bf16[256,2048]{1,0:T(8,128)(2,1)}, f32[1,768]{1,0:T(1,128)}) custom-call(bf16[256,2048]{1,0:T(8,128)(2,1)} %get-tuple-element.116.branch_ref, bf16[256,2048]{1,0:T(8,128)(2,1)} %add_convert_fusion.1.homed_ref, bf16[2048,768]{1,0:T(8,128)(2,1)} %add_convert_fusion.head_ref, ...), custom_call_target="tpu_custom_call" | custom-call | tf_op jit(solution)/shard_map/attend_back/pallas_call | solution.py:781
  493.8 10.4 %convolution_convert_fusion = bf16[2048,768]{1,0:T(8,128)(2,1)S(1)} fusion(bf16[2048,2048]{1,0:T(8,128)(2,1)} %bitcast.72, bf16[2048,768]{1,0:T(8,128)(2,1)} %get-tuple-element.92), kind=kOutput, calls=%fused_computation.1 | convolution fusion | flops 6444023808 | bytes 14680064 | tf_op jit(solution)/shard_map/dot_general | solution.py:50
  504.3 1.9 copy.68
  508.3 58.7 %product_reduce.3 = (f32[256,2048]{1,0:T(8,128)}, bf16[64,8192]{1,0:T(8,128)(2,1)}) custom-call(bf16[8,256,768]{2,1,0:T(8,128)(2,1)} %bitcast.80, bf16[2048,768]{1,0:T(8,128)(2,1)} %all-gather.7.cloned.1.call-done.weight_ref, bf16[512,1024]{1,0:T(8,128)(2,1)} %reduce-scatter.7.cloned.1.call-done.refs_0_), custom_call_target="tpu_custom_call" | custom-call | tf_op jit(solution)/shard_map/product_reduce/pallas_call | solution.py:437
  567.0 2.6 fusion.9
  570.8 2.8 convert_element_type.54
  573.7 1.8 fusion.13.homed_ref
  575.5 64.8 %closing.1 = (f32[192,128]{1,0:T(8,128)}, bf16[256,2048]{1,0:T(8,128)(2,1)}, bf16[64,6144]{1,0:T(8,128)(2,1)}, bf16[64,8192]{1,0:T(8,128)(2,1)}) custom-call(f32[192,128]{1,0:T(8,128)} %bitcast.86, bf16[256,2048]{1,0:T(8,128)(2,1)} %fusion.13.homed_ref, bf16[512,768]{1,0:T(8,128)(2,1)} %reduce-scatter.9.cloned.1.call-done.refs_0_, ...), custom_call_target="tpu_custom_call" | custom-call | tf_op jit(solution)/shard_map/closing/pallas_call | solution.py:485
  640.4 2.8 convert_element_type.55
  645.6 1.8 convert_element_type.53
  (156 shorter events, 19.2 us)
Async XLA Ops:
  7.2 51.4 %all-gather.5.cloned.1.call-start = ((), (), s32[]{:S(2)}) async-start(), calls=%async_computation.4 | async-start | bytes 1310720 | tf_op jit(solution)/shard_map/all_gather | solution.py:975
  7.9 51.5 %copy-start.29 = (s32[1,2048]{1,0:T(1,128)S(1)}, s32[1,2048]{1,0:T(1,128)}, u32[]{:S(2)}) copy-start(s32[1,2048]{1,0:T(1,128)} %param.31) | copy-start | bytes 24580
  7.9 51.5 %copy-start.32 = (s32[1,4]{1,0:T(1,128)S(1)}, s32[1,4]{1,0:T(1,128)}, u32[]{:S(2)}) copy-start(s32[1,4]{1,0:T(1,128)} %param.32) | copy-start | bytes 52
  7.9 138.8 %all-gather.7.cloned.1.call-start = ((), (), s32[]{:S(2)}) async-start(), calls=%async_computation.5 | async-start | bytes 3932160 | tf_op jit(solution)/shard_map/all_gather | solution.py:975
  58.5 12.2 %copy-start.7 = (bf16[256,2048]{1,0:T(8,128)(2,1)S(1)}, bf16[256,2048]{1,0:T(8,128)(2,1)}, u32[]{:S(2)}) copy-start(bf16[256,2048]{1,0:T(8,128)(2,1)} %get-tuple-element.61) | copy-start | bytes 3145732
  58.5 12.8 %copy-start.22 = (f32[2048]{0:T(1024)S(1)}, f32[2048]{0:T(1024)}, u32[]{:S(2)}) copy-start(f32[2048]{0:T(1024)} %param.18) | copy-start | bytes 24580
  58.6 12.8 %copy-start.23 = (f32[2048]{0:T(1024)S(1)}, f32[2048]{0:T(1024)}, u32[]{:S(2)}) copy-start(f32[2048]{0:T(1024)} %param.19) | copy-start | bytes 24580
  58.6 205.0 %all-gather.9.cloned.1.call-start = ((), (), s32[]{:S(2)}) async-start(), calls=%async_computation.6 | async-start | bytes 5242880 | tf_op jit(solution)/shard_map/all_gather | solution.py:975
  59.4 254.2 %all-gather.11.cloned.1.call-start = ((), (), s32[]{:S(2)}) async-start(), calls=%async_computation.7 | async-start | bytes 5242880 | tf_op jit(solution)/shard_map/all_gather | solution.py:975
  59.4 66.7 %collective-permute-start = (s32[1,2052]{1,0:T(1,128)S(1)}, s32[1,2052]{1,0:T(1,128)S(1)}, u32[]{:S(2)}, u32[]{:S(2)}) collective-permute-start(s32[1,2052]{1,0:T(1,128)S(1)} %pad_add_fusion), channel_id=1, source_target_pairs={{0,0},{1,1},{2,16},{3,17},{4,8},{5,9},{6,24},{7,25},{8,18},{9,19},... | collective-permute-start | bytes 24632 | tf_op jit(solution)/shard_map/ppermute | solution.py:964
  71.9 52.7 %copy-start.27 = (f32[2048]{0:T(1024)S(1)}, f32[2048]{0:T(1024)}, u32[]{:S(2)}) copy-start(f32[2048]{0:T(1024)} %param.22) | copy-start | bytes 24580
  71.9 52.7 %copy-start.28 = (f32[2048]{0:T(1024)S(1)}, f32[2048]{0:T(1024)}, u32[]{:S(2)}) copy-start(f32[2048]{0:T(1024)} %param.21) | copy-start | bytes 24580
  71.9 58.2 %copy-start.13 = (bf16[256,2048]{1,0:T(8,128)(2,1)S(1)}, bf16[256,2048]{1,0:T(8,128)(2,1)}, u32[]{:S(2)}) copy-start(bf16[256,2048]{1,0:T(8,128)(2,1)} %all-gather.5.cloned.1.call-done) | copy-start | bytes 3145732
  121.3 3.2 copy-start.4
  124.5 369.3 %reduce-scatter.5.cloned.1.call-start = ((), (), s32[]{:S(2)}) async-start(), calls=%async_computation.8 | async-start | bytes 5242880 | tf_op jit(solution)/shard_map/reduce_scatter | solution.py:990
  126.3 19.4 %copy-start.18 = (s32[1,2048]{1,0:T(1,128)}, s32[1,2048]{1,0:T(1,128)S(1)}, u32[]{:S(2)}) copy-start(s32[1,2048]{1,0:T(1,128)S(1)} %broadcast_in_dim_reshape.9.first_ref.place_ref) | copy-start | bytes 24580
  128.2 14.0 %collective-permute-start.1 = (bf16[256,2048]{1,0:T(8,128)(2,1)}, bf16[256,2048]{1,0:T(8,128)(2,1)}, u32[]{:S(2)}, u32[]{:S(2)}) collective-permute-start(bf16[256,2048]{1,0:T(8,128)(2,1)} %param.33), channel_id=1, source_target_pairs={{0,0},{1,1},{2,18},{3,19},{4,12},{5,13},{6,30},{7,31},{8,16},{9,17... | collective-permute-start | bytes 3145736 | tf_op jit(solution)/shard_map/ppermute | solution.py:958
  130.2 15.3 %collective-permute-start.3 = (bf16[2,64,2048]{2,1,0:T(8,128)(2,1)S(1)}, bf16[2,64,2048]{2,1,0:T(8,128)(2,1)S(1)}, u32[]{:S(2)}, u32[]{:S(2)}) collective-permute-start(bf16[2,64,2048]{2,1,0:T(8,128)(2,1)S(1)} %bitcast.85), channel_id=1, source_target_pairs={{0,1},{1,0},{2,3},{3,2},{4,5},{5,4},{6,7},{7,6},{8,9},{9,8},{10,11... | collective-permute-start | bytes 1572872 | tf_op jit(solution)/shard_map/ppermute | solution.py:1007
  142.2 80.0 %collective-permute-start.2 = (bf16[256,2048]{1,0:T(8,128)(2,1)}, bf16[256,2048]{1,0:T(8,128)(2,1)S(1)}, u32[]{:S(2)}, u32[]{:S(2)}) collective-permute-start(bf16[256,2048]{1,0:T(8,128)(2,1)} %collective-permute-done.1), channel_id=1, source_target_pairs={{0,0},{1,1},{18,16},{19,17},{12,8},{13,9},{30,24},{31,25},{16,18},... | collective-permute-start | bytes 3145736 | tf_op jit(solution)/shard_map/ppermute | solution.py:961
  159.4 48.6 %copy-start.24 = (f32[2048]{0:T(1024)S(1)}, f32[2048]{0:T(1024)}, u32[]{:S(2)}) copy-start(f32[2048]{0:T(1024)} %param.24) | copy-start | bytes 24580
  222.2 38.2 %copy-start.1 = (bf16[256,2048]{1,0:T(8,128)(2,1)}, bf16[256,2048]{1,0:T(8,128)(2,1)S(1)}, u32[]{:S(2)}) copy-start(bf16[256,2048]{1,0:T(8,128)(2,1)S(1)} %collective-permute-done.2.x_ref) | copy-start | bytes 3145732
  260.4 3.2 copy-start
  312.4 193.8 %reduce-scatter.7.cloned.1.call-start = ((), (), s32[]{:S(2)}) async-start(), calls=%async_computation.9 | async-start | bytes 5242880 | tf_op jit(solution)/shard_map/reduce_scatter | solution.py:990
  369.0 201.8 %reduce-scatter.9.cloned.1.call-start = ((), (), s32[]{:S(2)}) async-start(), calls=%async_computation.10 | async-start | bytes 3932160 | tf_op jit(solution)/shard_map/reduce_scatter | solution.py:990
  372.1 45.5 %copy-start.6 = (f32[256,2048]{1,0:T(8,128)S(1)}, f32[256,2048]{1,0:T(8,128)}, u32[]{:S(2)}) copy-start(f32[256,2048]{1,0:T(8,128)} %copy-done.5) | copy-start | bytes 6291460
  372.1 45.5 %copy-start.26 = (f32[2048]{0:T(1024)S(1)}, f32[2048]{0:T(1024)}, u32[]{:S(2)}) copy-start(f32[2048]{0:T(1024)} %param.30) | copy-start | bytes 24580
  506.2 139.4 %reduce-scatter.11.cloned.1.call-start = ((), (), s32[]{:S(2)}) async-start(), calls=%async_computation.11 | async-start | bytes 1310720 | tf_op jit(solution)/shard_map/reduce_scatter | solution.py:990
  508.0 61.6 %collective-permute-start.4 = (bf16[2,64,2048]{2,1,0:T(8,128)(2,1)S(1)}, bf16[2,64,2048]{2,1,0:T(8,128)(2,1)S(1)}, u32[]{:S(2)}, u32[]{:S(2)}) collective-permute-start(bf16[2,64,2048]{2,1,0:T(8,128)(2,1)S(1)} %select_bitcast_fusion), channel_id=1, source_target_pairs={{0,1},{1,0},{2,3},{3,2},{4,5},{5,4},{6,7},{7,6},{8,9},{9,8},{10,11... | collective-permute-start | bytes 1572872 | tf_op jit(solution)/shard_map/ppermute | solution.py:1026
  508.3 58.7 %copy-start.8 = (bf16[256,2048]{1,0:T(8,128)(2,1)S(1)}, bf16[256,2048]{1,0:T(8,128)(2,1)}, u32[]{:S(2)}) copy-start(bf16[256,2048]{1,0:T(8,128)(2,1)} %get-tuple-element.61) | copy-start | bytes 3145732
  640.4 4.0 copy-start.20
  643.1 4.3 copy-start.14
  644.4 4.0 copy-start.16
  (14 other events, 24.5 us)
Sparse Core Ops, SparseCore 0:
  9.6 39.9 all-gather.4
  58.7 70.8 all-gather.6
  131.2 99.7 all-gather.8
  232.4 81.0 all-gather.10
  315.7 77.3 reduce-scatter.4
  395.3 95.1 reduce-scatter.6
  506.4 62.8 reduce-scatter.8
  572.1 47.8 reduce-scatter.10

commit v7 on v6

--- a/solution.py
+++ b/solution.py
@@ -461,7 +461,7 @@
             one = pltpu.make_async_remote_copy(src_ref=out_ref, dst_ref=slots.at[me], send_sem=send.at[s], recv_sem=recv.at[s], device_id=other(name, s), device_id_type=MESH)
             one.start()
             copies.append(one)
-        if name == 'rep':
+        if j == 0:
             for start, _ in owners:
                 start()
         for one in copies:

time: 661 us -> 653 us (0.988)
  Pallas kernels: 529 us -> 517 us
    pallas_call x1, Pallas kernels: 64.8 us -> 53.6 us  [closing(): pl.pallas_call(functools.partial(closing_kernel, number), out_shape=[jax....]
  transfers between devices with their start and end apart: 13 -> 13, of which waited for: 3 -> 3; matrix products, arithmetic and copies ran while one was open for 9% -> 9% of each run, Pallas kernels for 81% -> 80%
where the time goes in v7:
time: 653 us; the launch traced here: 645 us
  Pallas kernels  517 us (79%)
  other arithmetic  30 us (5%)
  waiting for transfers between devices  23.3 us (4%)
  local copies, waits for them, and re-layouts  20.9 us (3%)
  matrix products  20.9 us (3%)
  starting transfers between devices  17.8 us (3%)
  between operations  15 us (2%)
    pallas_call x2, Pallas kernels, product_reduce(): pl.pallas_call(functools.partial(product_reduce_kernel, owns, homes), gri...  104 us
    pallas_call x2, Pallas kernels, plane_gather(): pl.pallas_call(functools.partial(gather_kernel, number), grid=(8,), out_s...  87.5 us
    pallas_call x1, Pallas kernels, attend_back(): pl.pallas_call(functools.partial(attend_back_kernel, heads), grid=(8,), o...  68.9 us
    pallas_call x1, Pallas kernels, hidden_back(): pl.pallas_call(hidden_back_kernel, grid=(8,), out_shape=[jax.ShapeDtypeSt...  55.4 us
    pallas_call x1, Pallas kernels, closing(): pl.pallas_call(functools.partial(closing_kernel, number), out_shape=[jax....  53.6 us
    pallas_call x1, Pallas kernels, opening(): pl.pallas_call(opening_kernel, out_shape=[jax.ShapeDtypeStruct(x.shape, x...  50.5 us
    pallas_call x1, Pallas kernels, hidden(): pl.pallas_call(hidden_kernel, grid=(8,), out_shape=[jax.ShapeDtypeStruct(...  48.7 us
    pallas_call x1, Pallas kernels, attend(): pl.pallas_call(functools.partial(attend_kernel, heads), grid=(8,), out_sh...  48.6 us
  transfers between devices with their start and end apart: 13, of which 3 were waited for; matrix products, arithmetic and copies ran while one was open for 9% of the time, Pallas kernels for 80%

profile of v7, /device:TPU:19, one launch (start us, length us, event | category | flops | bytes accessed | tf_op | source)
XLA Modules:
  0.0 645.2 jit_solution(2743809392592522400)
XLA Ops:
  8.0 50.5 %opening.1 = (bf16[256,2048]{1,0:T(8,128)(2,1)}, bf16[512,768]{1,0:T(8,128)(2,1)}, bf16[512,1024]{1,0:T(8,128)(2,1)}) custom-call(bf16[256,2048]{1,0:T(8,128)(2,1)} %x_ref.1, bf16[64,6144]{1,0:T(8,128)(2,1)} %refs_0_.2, bf16[64,8192]{1,0:T(8,128)(2,1)} %refs_1_.1), custom_call_target="tpu_custom_call" | custom-call | tf_op jit(solution)/shard_map/opening/pallas_call | solution.py:610
  59.4 11.2 %collective-permute-start = (s32[1,2052]{1,0:T(1,128)S(1)}, s32[1,2052]{1,0:T(1,128)S(1)}, u32[]{:S(2)}, u32[]{:S(2)}) collective-permute-start(s32[1,2052]{1,0:T(1,128)S(1)} %pad_add_fusion), channel_id=1, source_target_pairs={{0,0},{1,1},{2,16},{3,17},{4,8},{5,9},{6,24},{7,25},{8,18},{9,19},... | collective-permute-start | bytes 24632 | tf_op jit(solution)/shard_map/ppermute | solution.py:964
  71.9 49.3 %plane_gather.2 = (bf16[8,256,2048]{2,1,0:T(8,128)(2,1)S(1)}, bf16[512,1024]{1,0:T(8,128)(2,1)}) custom-call(bf16[256,2048]{1,0:T(8,128)(2,1)S(1)} %fusion.7.x_ref, bf16[64,8192]{1,0:T(8,128)(2,1)S(1)} %copy-done.3), custom_call_target="tpu_custom_call" | custom-call | tf_op jit(solution)/shard_map/plane_gather/pallas_call | solution.py:294
  121.3 3.2 copy-done.4
  126.3 1.9 broadcast_in_dim_reshape.10.place_ref.first_ref
  128.2 1.9 collective-permute-start.1
  131.6 10.6 %collective-permute-done.1 = bf16[256,2048]{1,0:T(8,128)(2,1)} collective-permute-done((bf16[256,2048]{1,0:T(8,128)(2,1)}, bf16[256,2048]{1,0:T(8,128)(2,1)}, u32[]{:S(2)}, u32[]{:S(2)}) %collective-permute-start.1) | collective-permute-done | bytes 1048608 | tf_op jit(solution)/shard_map/ppermute | solution.py:958
  142.2 3.4 collective-permute-start.2
  146.8 2.2 copy.58
  149.0 10.4 %add_convert_fusion.head_ref = bf16[2048,768]{1,0:T(8,128)(2,1)} fusion(f32[768]{0:T(1024)S(1)} %dynamic_slice.10, bf16[2048,2048]{1,0:T(8,128)(2,1)} %bitcast.71, bf16[2048,768]{1,0:T(8,128)(2,1)S(1)} %bitcast.81), kind=kOutput, calls=%fused_computation | convolution fusion | flops 6445596672 | bytes 14683136 | tf_op jit(solution)/shard_map/dot_general | solution.py:44
  159.4 48.6 %attend.1 = (bf16[2048,256]{1,0:T(8,128)(2,1)}, f32[2,8,2048]{2,1,0:T(8,128)}, f32[256,2048]{1,0:T(8,128)}) custom-call(bf16[2048,768]{1,0:T(8,128)(2,1)} %add_convert_fusion.head_ref, s32[2048,1]{1,0:T(8,128)} %broadcast_in_dim_reshape.10.place_ref.first_ref, s32[1,2048]{1,0:T(1,128)} %copy-done.18, s32[1,2048]{1,0:T(1,128)} %compare_select_fusion.1.last_ref, ...), custom_call_target="tpu_custom_call" | custom-call | tf_op jit(solution)/shard_map/attend/pallas_call | solution.py:646
  208.0 2.0 fusion.20
  210.7 1.4 add_convert_fusion.2.middle_ref
  212.2 10.0 %collective-permute-done.2.x_ref = bf16[256,2048]{1,0:T(8,128)(2,1)S(1)} collective-permute-done((bf16[256,2048]{1,0:T(8,128)(2,1)}, bf16[256,2048]{1,0:T(8,128)(2,1)S(1)}, u32[]{:S(2)}, u32[]{:S(2)}) %collective-permute-start.2) | collective-permute-done | bytes 1048608 | tf_op jit(solution)/shard_map/ppermute | solution.py:961
  222.2 38.2 %plane_gather.3 = bf16[8,256,2048]{2,1,0:T(8,128)(2,1)S(1)} custom-call(bf16[256,2048]{1,0:T(8,128)(2,1)S(1)} %collective-permute-done.2.x_ref), custom_call_target="tpu_custom_call" | custom-call | tf_op jit(solution)/shard_map/plane_gather/pallas_call | solution.py:294
  260.4 3.2 copy-done
  263.6 48.7 %hidden.1 = (bf16[8,256,2048]{2,1,0:T(8,128)(2,1)}, bf16[8,256,1024]{2,1,0:T(8,128)(2,1)}, f32[8,256,1024]{2,1,0:T(8,128)}, bf16[2048,1024]{1,0:T(8,128)(2,1)}) custom-call(bf16[256,2048]{1,0:T(8,128)(2,1)} %add_convert_fusion.2.middle_ref, bf16[8,256,2048]{2,1,0:T(8,128)(2,1)} %copy-done, bf16[2048,1024]{1,0:T(8,128)(2,1)} %all-gather.9.cloned.1.call-done.expand_ref, ...), custom_call_target="tpu_custom_call" | custom-call | tf_op jit(solution)/shard_map/hidden/pallas_call | solution.py:876
  313.6 55.4 %hidden_back.1 = (bf16[8,256,1024]{2,1,0:T(8,128)(2,1)}, f32[256,2048]{1,0:T(8,128)}, bf16[2048,1024]{1,0:T(8,128)(2,1)}, f32[1,1024]{1,0:T(1,128)}) custom-call(bf16[8,256,2048]{2,1,0:T(8,128)(2,1)} %copy-done, bf16[8,256,2048]{2,1,0:T(8,128)(2,1)} %get-tuple-element.76.middle_ref, f32[8,256,1024]{2,1,0:T(8,128)} %get-tuple-element.77.rise_ref, ...), custom_call_target="tpu_custom_call" | custom-call | tf_op jit(solution)/shard_map/hidden_back/pallas_call | solution.py:943
  370.2 1.9 select_select_fusion.last_ref
  372.1 45.5 %product_reduce.2 = f32[256,2048]{1,0:T(8,128)} custom-call(bf16[8,256,1024]{2,1,0:T(8,128)(2,1)} %get-tuple-element.75, bf16[2048,1024]{1,0:T(8,128)(2,1)} %all-gather.11.cloned.1.call-done.shrink_ref.weight_ref), custom_call_target="tpu_custom_call" | custom-call | tf_op jit(solution)/shard_map/product_reduce/pallas_call | solution.py:437
  417.6 3.1 add_convert_fusion.1.homed_ref
  421.9 2.9 convert_reduce_fusion.2
  424.9 68.9 %attend_back.1 = (bf16[256,2048]{1,0:T(8,128)(2,1)}, bf16[2048,768]{1,0:T(8,128)(2,1)}, bf16[256,2048]{1,0:T(8,128)(2,1)}, f32[1,768]{1,0:T(1,128)}) custom-call(bf16[256,2048]{1,0:T(8,128)(2,1)} %get-tuple-element.116.branch_ref, bf16[256,2048]{1,0:T(8,128)(2,1)} %add_convert_fusion.1.homed_ref, bf16[2048,768]{1,0:T(8,128)(2,1)} %add_convert_fusion.head_ref, ...), custom_call_target="tpu_custom_call" | custom-call | tf_op jit(solution)/shard_map/attend_back/pallas_call | solution.py:781
  493.8 10.4 %convolution_convert_fusion = bf16[2048,768]{1,0:T(8,128)(2,1)S(1)} fusion(bf16[2048,2048]{1,0:T(8,128)(2,1)} %bitcast.72, bf16[2048,768]{1,0:T(8,128)(2,1)} %get-tuple-element.92), kind=kOutput, calls=%fused_computation.1 | convolution fusion | flops 6444023808 | bytes 14680064 | tf_op jit(solution)/shard_map/dot_general | solution.py:50
  504.3 1.9 copy.68
  508.3 58.7 %product_reduce.3 = (f32[256,2048]{1,0:T(8,128)}, bf16[64,8192]{1,0:T(8,128)(2,1)}) custom-call(bf16[8,256,768]{2,1,0:T(8,128)(2,1)} %bitcast.80, bf16[2048,768]{1,0:T(8,128)(2,1)} %all-gather.7.cloned.1.call-done.weight_ref, bf16[512,1024]{1,0:T(8,128)(2,1)} %reduce-scatter.7.cloned.1.call-done.refs_0_), custom_call_target="tpu_custom_call" | custom-call | tf_op jit(solution)/shard_map/product_reduce/pallas_call | solution.py:437
  567.0 2.6 fusion.9
  570.8 2.8 convert_element_type.54
  573.7 1.8 fusion.13.homed_ref
  575.5 53.6 %closing.1 = (f32[192,128]{1,0:T(8,128)}, bf16[256,2048]{1,0:T(8,128)(2,1)}, bf16[64,6144]{1,0:T(8,128)(2,1)}, bf16[64,8192]{1,0:T(8,128)(2,1)}) custom-call(f32[192,128]{1,0:T(8,128)} %bitcast.86, bf16[256,2048]{1,0:T(8,128)(2,1)} %fusion.13.homed_ref, bf16[512,768]{1,0:T(8,128)(2,1)} %reduce-scatter.9.cloned.1.call-done.refs_0_, ...), custom_call_target="tpu_custom_call" | custom-call | tf_op jit(solution)/shard_map/closing/pallas_call | solution.py:485
  629.2 2.8 convert_element_type.55
  634.4 1.8 convert_element_type.53
  (156 shorter events, 19.2 us)
Async XLA Ops:
  7.2 51.4 %all-gather.5.cloned.1.call-start = ((), (), s32[]{:S(2)}) async-start(), calls=%async_computation.4 | async-start | bytes 1310720 | tf_op jit(solution)/shard_map/all_gather | solution.py:975
  7.9 51.5 %copy-start.29 = (s32[1,2048]{1,0:T(1,128)S(1)}, s32[1,2048]{1,0:T(1,128)}, u32[]{:S(2)}) copy-start(s32[1,2048]{1,0:T(1,128)} %param.31) | copy-start | bytes 24580
  7.9 51.5 %copy-start.32 = (s32[1,4]{1,0:T(1,128)S(1)}, s32[1,4]{1,0:T(1,128)}, u32[]{:S(2)}) copy-start(s32[1,4]{1,0:T(1,128)} %param.32) | copy-start | bytes 52
  7.9 138.8 %all-gather.7.cloned.1.call-start = ((), (), s32[]{:S(2)}) async-start(), calls=%async_computation.5 | async-start | bytes 3932160 | tf_op jit(solution)/shard_map/all_gather | solution.py:975
  58.5 12.2 %copy-start.7 = (bf16[256,2048]{1,0:T(8,128)(2,1)S(1)}, bf16[256,2048]{1,0:T(8,128)(2,1)}, u32[]{:S(2)}) copy-start(bf16[256,2048]{1,0:T(8,128)(2,1)} %get-tuple-element.61) | copy-start | bytes 3145732
  58.5 12.8 %copy-start.22 = (f32[2048]{0:T(1024)S(1)}, f32[2048]{0:T(1024)}, u32[]{:S(2)}) copy-start(f32[2048]{0:T(1024)} %param.18) | copy-start | bytes 24580
  58.6 12.8 %copy-start.23 = (f32[2048]{0:T(1024)S(1)}, f32[2048]{0:T(1024)}, u32[]{:S(2)}) copy-start(f32[2048]{0:T(1024)} %param.19) | copy-start | bytes 24580
  58.6 205.0 %all-gather.9.cloned.1.call-start = ((), (), s32[]{:S(2)}) async-start(), calls=%async_computation.6 | async-start | bytes 5242880 | tf_op jit(solution)/shard_map/all_gather | solution.py:975
  59.4 254.2 %all-gather.11.cloned.1.call-start = ((), (), s32[]{:S(2)}) async-start(), calls=%async_computation.7 | async-start | bytes 5242880 | tf_op jit(solution)/shard_map/all_gather | solution.py:975
  59.4 66.7 %collective-permute-start = (s32[1,2052]{1,0:T(1,128)S(1)}, s32[1,2052]{1,0:T(1,128)S(1)}, u32[]{:S(2)}, u32[]{:S(2)}) collective-permute-start(s32[1,2052]{1,0:T(1,128)S(1)} %pad_add_fusion), channel_id=1, source_target_pairs={{0,0},{1,1},{2,16},{3,17},{4,8},{5,9},{6,24},{7,25},{8,18},{9,19},... | collective-permute-start | bytes 24632 | tf_op jit(solution)/shard_map/ppermute | solution.py:964
  71.9 52.7 %copy-start.27 = (f32[2048]{0:T(1024)S(1)}, f32[2048]{0:T(1024)}, u32[]{:S(2)}) copy-start(f32[2048]{0:T(1024)} %param.22) | copy-start | bytes 24580
  71.9 52.7 %copy-start.28 = (f32[2048]{0:T(1024)S(1)}, f32[2048]{0:T(1024)}, u32[]{:S(2)}) copy-start(f32[2048]{0:T(1024)} %param.21) | copy-start | bytes 24580
  71.9 58.2 %copy-start.13 = (bf16[256,2048]{1,0:T(8,128)(2,1)S(1)}, bf16[256,2048]{1,0:T(8,128)(2,1)}, u32[]{:S(2)}) copy-start(bf16[256,2048]{1,0:T(8,128)(2,1)} %all-gather.5.cloned.1.call-done) | copy-start | bytes 3145732
  121.3 3.2 copy-start.4
  124.5 369.3 %reduce-scatter.5.cloned.1.call-start = ((), (), s32[]{:S(2)}) async-start(), calls=%async_computation.8 | async-start | bytes 5242880 | tf_op jit(solution)/shard_map/reduce_scatter | solution.py:990
  126.3 19.4 %copy-start.18 = (s32[1,2048]{1,0:T(1,128)}, s32[1,2048]{1,0:T(1,128)S(1)}, u32[]{:S(2)}) copy-start(s32[1,2048]{1,0:T(1,128)S(1)} %broadcast_in_dim_reshape.9.first_ref.place_ref) | copy-start | bytes 24580
  128.2 14.0 %collective-permute-start.1 = (bf16[256,2048]{1,0:T(8,128)(2,1)}, bf16[256,2048]{1,0:T(8,128)(2,1)}, u32[]{:S(2)}, u32[]{:S(2)}) collective-permute-start(bf16[256,2048]{1,0:T(8,128)(2,1)} %param.33), channel_id=1, source_target_pairs={{0,0},{1,1},{2,18},{3,19},{4,12},{5,13},{6,30},{7,31},{8,16},{9,17... | collective-permute-start | bytes 3145736 | tf_op jit(solution)/shard_map/ppermute | solution.py:958
  130.2 15.3 %collective-permute-start.3 = (bf16[2,64,2048]{2,1,0:T(8,128)(2,1)S(1)}, bf16[2,64,2048]{2,1,0:T(8,128)(2,1)S(1)}, u32[]{:S(2)}, u32[]{:S(2)}) collective-permute-start(bf16[2,64,2048]{2,1,0:T(8,128)(2,1)S(1)} %bitcast.85), channel_id=1, source_target_pairs={{0,1},{1,0},{2,3},{3,2},{4,5},{5,4},{6,7},{7,6},{8,9},{9,8},{10,11... | collective-permute-start | bytes 1572872 | tf_op jit(solution)/shard_map/ppermute | solution.py:1007
  142.2 80.0 %collective-permute-start.2 = (bf16[256,2048]{1,0:T(8,128)(2,1)}, bf16[256,2048]{1,0:T(8,128)(2,1)S(1)}, u32[]{:S(2)}, u32[]{:S(2)}) collective-permute-start(bf16[256,2048]{1,0:T(8,128)(2,1)} %collective-permute-done.1), channel_id=1, source_target_pairs={{0,0},{1,1},{18,16},{19,17},{12,8},{13,9},{30,24},{31,25},{16,18},... | collective-permute-start | bytes 3145736 | tf_op jit(solution)/shard_map/ppermute | solution.py:961
  159.4 48.6 %copy-start.24 = (f32[2048]{0:T(1024)S(1)}, f32[2048]{0:T(1024)}, u32[]{:S(2)}) copy-start(f32[2048]{0:T(1024)} %param.24) | copy-start | bytes 24580
  222.2 38.2 %copy-start.1 = (bf16[256,2048]{1,0:T(8,128)(2,1)}, bf16[256,2048]{1,0:T(8,128)(2,1)S(1)}, u32[]{:S(2)}) copy-start(bf16[256,2048]{1,0:T(8,128)(2,1)S(1)} %collective-permute-done.2.x_ref) | copy-start | bytes 3145732
  260.4 3.2 copy-start
  312.4 193.8 %reduce-scatter.7.cloned.1.call-start = ((), (), s32[]{:S(2)}) async-start(), calls=%async_computation.9 | async-start | bytes 5242880 | tf_op jit(solution)/shard_map/reduce_scatter | solution.py:990
  369.0 201.8 %reduce-scatter.9.cloned.1.call-start = ((), (), s32[]{:S(2)}) async-start(), calls=%async_computation.10 | async-start | bytes 3932160 | tf_op jit(solution)/shard_map/reduce_scatter | solution.py:990
  372.1 45.5 %copy-start.6 = (f32[256,2048]{1,0:T(8,128)S(1)}, f32[256,2048]{1,0:T(8,128)}, u32[]{:S(2)}) copy-start(f32[256,2048]{1,0:T(8,128)} %copy-done.5) | copy-start | bytes 6291460
  372.1 45.5 %copy-start.26 = (f32[2048]{0:T(1024)S(1)}, f32[2048]{0:T(1024)}, u32[]{:S(2)}) copy-start(f32[2048]{0:T(1024)} %param.30) | copy-start | bytes 24580
  506.2 128.2 %reduce-scatter.11.cloned.1.call-start = ((), (), s32[]{:S(2)}) async-start(), calls=%async_computation.11 | async-start | bytes 1310720 | tf_op jit(solution)/shard_map/reduce_scatter | solution.py:990
  508.0 61.6 %collective-permute-start.4 = (bf16[2,64,2048]{2,1,0:T(8,128)(2,1)S(1)}, bf16[2,64,2048]{2,1,0:T(8,128)(2,1)S(1)}, u32[]{:S(2)}, u32[]{:S(2)}) collective-permute-start(bf16[2,64,2048]{2,1,0:T(8,128)(2,1)S(1)} %select_bitcast_fusion), channel_id=1, source_target_pairs={{0,1},{1,0},{2,3},{3,2},{4,5},{5,4},{6,7},{7,6},{8,9},{9,8},{10,11... | collective-permute-start | bytes 1572872 | tf_op jit(solution)/shard_map/ppermute | solution.py:1026
  508.3 58.7 %copy-start.8 = (bf16[256,2048]{1,0:T(8,128)(2,1)S(1)}, bf16[256,2048]{1,0:T(8,128)(2,1)}, u32[]{:S(2)}) copy-start(bf16[256,2048]{1,0:T(8,128)(2,1)} %get-tuple-element.61) | copy-start | bytes 3145732
  629.2 4.0 copy-start.20
  631.9 4.3 copy-start.14
  633.2 4.0 copy-start.16
  (14 other events, 24.5 us)
Sparse Core Ops, SparseCore 0:
  9.6 39.9 all-gather.4
  58.7 70.8 all-gather.6
  131.2 99.7 all-gather.8
  232.4 81.0 all-gather.10
  315.7 77.3 reduce-scatter.4
  395.3 95.1 reduce-scatter.6
  506.4 62.8 reduce-scatter.8
  572.1 46.7 reduce-scatter.10

commit v8 on v7

--- a/solution.py
+++ b/solution.py
@@ -440,7 +440,7 @@
     owned_refs, (out_ref, homed_out), owned_outs = (refs[:number], refs[number:number + 2], refs[number + 2:2 * number + 2])
     refs = refs[2 * number + 2:]
     here = {n: lax.axis_index(n) for n in EVERY}
-    phases = ('grp', 'sub', 'rep')
+    phases = ('rep', 'grp', 'sub')
     home_start, home_finish = home_cargo(homed_ref, homed_out, *refs[:3])
     owners = [owner_cargo(owned_refs[i], owned_outs[i], *refs[3 + 3 * i:6 + 3 * i]) for i in range(number)]
     refs = refs[3 + 3 * number:]
@@ -449,7 +449,6 @@
         size = lax.axis_size(name)
         return tuple((lax.rem(here[n] + step, size) if n == name else here[n] for n in EVERY))
     greet_all(plane_peers()[1] + [other('rep', s) for s in range(1, lax.axis_size('rep'))], True)
-    home_start()
     out_ref[...] = x_ref[...]
     for j, name in enumerate(phases):
         slots, send, recv = refs[3 * j:3 * j + 3]
@@ -462,6 +461,7 @@
             one.start()
             copies.append(one)
         if j == 0:
+            home_start()
             for start, _ in owners:
                 start()
         for one in copies:
@@ -478,7 +478,7 @@
 
 def closing(x, homed, owned, collective_id):
     scratch = []
-    for name in ('grp', 'sub', 'rep'):
+    for name in ('rep', 'grp', 'sub'):
         n = lax.axis_size(name)
         scratch += [pltpu.VMEM((n,) + x.shape, x.dtype), DMA((n,)), DMA((n,))]
     number = len(owned)

time: 653 us -> 653 us (level)
  no operation moved by 1% of the time
where the time goes in v8:
time: 653 us; the launch traced here: 647 us
  Pallas kernels  519 us (79%)
  other arithmetic  30 us (5%)
  waiting for transfers between devices  23.3 us (4%)
  local copies, waits for them, and re-layouts  20.9 us (3%)
  matrix products  20.9 us (3%)
  starting transfers between devices  17.8 us (3%)
  between operations  15 us (2%)
    pallas_call x2, Pallas kernels, product_reduce(): pl.pallas_call(functools.partial(product_reduce_kernel, owns, homes), gri...  104 us
    pallas_call x2, Pallas kernels, plane_gather(): pl.pallas_call(functools.partial(gather_kernel, number), grid=(8,), out_s...  87.5 us
    pallas_call x1, Pallas kernels, attend_back(): pl.pallas_call(functools.partial(attend_back_kernel, heads), grid=(8,), o...  68.9 us
    pallas_call x1, Pallas kernels, hidden_back(): pl.pallas_call(hidden_back_kernel, grid=(8,), out_shape=[jax.ShapeDtypeSt...  55.4 us
    pallas_call x1, Pallas kernels, closing(): pl.pallas_call(functools.partial(closing_kernel, number), out_shape=[jax....  55.2 us
    pallas_call x1, Pallas kernels, opening(): pl.pallas_call(opening_kernel, out_shape=[jax.ShapeDtypeStruct(x.shape, x...  50.5 us
    pallas_call x1, Pallas kernels, hidden(): pl.pallas_call(hidden_kernel, grid=(8,), out_shape=[jax.ShapeDtypeStruct(...  48.7 us
    pallas_call x1, Pallas kernels, attend(): pl.pallas_call(functools.partial(attend_kernel, heads), grid=(8,), out_sh...  48.6 us
  transfers between devices with their start and end apart: 13, of which 3 were waited for; matrix products, arithmetic and copies ran while one was open for 9% of the time, Pallas kernels for 80%

profile of v8, /device:TPU:19, one launch (start us, length us, event | category | flops | bytes accessed | tf_op | source)
XLA Modules:
  0.0 646.8 jit_solution(10686944703928392816)
XLA Ops:
  8.0 50.5 %opening.1 = (bf16[256,2048]{1,0:T(8,128)(2,1)}, bf16[512,768]{1,0:T(8,128)(2,1)}, bf16[512,1024]{1,0:T(8,128)(2,1)}) custom-call(bf16[256,2048]{1,0:T(8,128)(2,1)} %x_ref.1, bf16[64,6144]{1,0:T(8,128)(2,1)} %refs_0_.2, bf16[64,8192]{1,0:T(8,128)(2,1)} %refs_1_.1), custom_call_target="tpu_custom_call" | custom-call | tf_op jit(solution)/shard_map/opening/pallas_call | solution.py:610
  59.4 11.2 %collective-permute-start = (s32[1,2052]{1,0:T(1,128)S(1)}, s32[1,2052]{1,0:T(1,128)S(1)}, u32[]{:S(2)}, u32[]{:S(2)}) collective-permute-start(s32[1,2052]{1,0:T(1,128)S(1)} %pad_add_fusion), channel_id=1, source_target_pairs={{0,0},{1,1},{2,16},{3,17},{4,8},{5,9},{6,24},{7,25},{8,18},{9,19},... | collective-permute-start | bytes 24632 | tf_op jit(solution)/shard_map/ppermute | solution.py:964
  71.9 49.3 %plane_gather.2 = (bf16[8,256,2048]{2,1,0:T(8,128)(2,1)S(1)}, bf16[512,1024]{1,0:T(8,128)(2,1)}) custom-call(bf16[256,2048]{1,0:T(8,128)(2,1)S(1)} %fusion.7.x_ref, bf16[64,8192]{1,0:T(8,128)(2,1)S(1)} %copy-done.3), custom_call_target="tpu_custom_call" | custom-call | tf_op jit(solution)/shard_map/plane_gather/pallas_call | solution.py:294
  121.3 3.2 copy-done.4
  126.3 1.9 broadcast_in_dim_reshape.10.place_ref.first_ref
  128.2 1.9 collective-permute-start.1
  131.6 10.6 %collective-permute-done.1 = bf16[256,2048]{1,0:T(8,128)(2,1)} collective-permute-done((bf16[256,2048]{1,0:T(8,128)(2,1)}, bf16[256,2048]{1,0:T(8,128)(2,1)}, u32[]{:S(2)}, u32[]{:S(2)}) %collective-permute-start.1) | collective-permute-done | bytes 1048608 | tf_op jit(solution)/shard_map/ppermute | solution.py:958
  142.2 3.4 collective-permute-start.2
  146.8 2.2 copy.58
  149.0 10.4 %add_convert_fusion.head_ref = bf16[2048,768]{1,0:T(8,128)(2,1)} fusion(f32[768]{0:T(1024)S(1)} %dynamic_slice.10, bf16[2048,2048]{1,0:T(8,128)(2,1)} %bitcast.71, bf16[2048,768]{1,0:T(8,128)(2,1)S(1)} %bitcast.81), kind=kOutput, calls=%fused_computation | convolution fusion | flops 6445596672 | bytes 14683136 | tf_op jit(solution)/shard_map/dot_general | solution.py:44
  159.4 48.6 %attend.1 = (bf16[2048,256]{1,0:T(8,128)(2,1)}, f32[2,8,2048]{2,1,0:T(8,128)}, f32[256,2048]{1,0:T(8,128)}) custom-call(bf16[2048,768]{1,0:T(8,128)(2,1)} %add_convert_fusion.head_ref, s32[2048,1]{1,0:T(8,128)} %broadcast_in_dim_reshape.10.place_ref.first_ref, s32[1,2048]{1,0:T(1,128)} %copy-done.18, s32[1,2048]{1,0:T(1,128)} %compare_select_fusion.1.last_ref, ...), custom_call_target="tpu_custom_call" | custom-call | tf_op jit(solution)/shard_map/attend/pallas_call | solution.py:646
  208.0 2.0 fusion.20
  210.7 1.4 add_convert_fusion.2.middle_ref
  212.2 10.0 %collective-permute-done.2.x_ref = bf16[256,2048]{1,0:T(8,128)(2,1)S(1)} collective-permute-done((bf16[256,2048]{1,0:T(8,128)(2,1)}, bf16[256,2048]{1,0:T(8,128)(2,1)S(1)}, u32[]{:S(2)}, u32[]{:S(2)}) %collective-permute-start.2) | collective-permute-done | bytes 1048608 | tf_op jit(solution)/shard_map/ppermute | solution.py:961
  222.2 38.2 %plane_gather.3 = bf16[8,256,2048]{2,1,0:T(8,128)(2,1)S(1)} custom-call(bf16[256,2048]{1,0:T(8,128)(2,1)S(1)} %collective-permute-done.2.x_ref), custom_call_target="tpu_custom_call" | custom-call | tf_op jit(solution)/shard_map/plane_gather/pallas_call | solution.py:294
  260.4 3.2 copy-done
  263.6 48.7 %hidden.1 = (bf16[8,256,2048]{2,1,0:T(8,128)(2,1)}, bf16[8,256,1024]{2,1,0:T(8,128)(2,1)}, f32[8,256,1024]{2,1,0:T(8,128)}, bf16[2048,1024]{1,0:T(8,128)(2,1)}) custom-call(bf16[256,2048]{1,0:T(8,128)(2,1)} %add_convert_fusion.2.middle_ref, bf16[8,256,2048]{2,1,0:T(8,128)(2,1)} %copy-done, bf16[2048,1024]{1,0:T(8,128)(2,1)} %all-gather.9.cloned.1.call-done.expand_ref, ...), custom_call_target="tpu_custom_call" | custom-call | tf_op jit(solution)/shard_map/hidden/pallas_call | solution.py:876
  313.6 55.4 %hidden_back.1 = (bf16[8,256,1024]{2,1,0:T(8,128)(2,1)}, f32[256,2048]{1,0:T(8,128)}, bf16[2048,1024]{1,0:T(8,128)(2,1)}, f32[1,1024]{1,0:T(1,128)}) custom-call(bf16[8,256,2048]{2,1,0:T(8,128)(2,1)} %copy-done, bf16[8,256,2048]{2,1,0:T(8,128)(2,1)} %get-tuple-element.76.middle_ref, f32[8,256,1024]{2,1,0:T(8,128)} %get-tuple-element.77.rise_ref, ...), custom_call_target="tpu_custom_call" | custom-call | tf_op jit(solution)/shard_map/hidden_back/pallas_call | solution.py:943
  370.2 1.9 select_select_fusion.last_ref
  372.1 45.5 %product_reduce.2 = f32[256,2048]{1,0:T(8,128)} custom-call(bf16[8,256,1024]{2,1,0:T(8,128)(2,1)} %get-tuple-element.75, bf16[2048,1024]{1,0:T(8,128)(2,1)} %all-gather.11.cloned.1.call-done.shrink_ref.weight_ref), custom_call_target="tpu_custom_call" | custom-call | tf_op jit(solution)/shard_map/product_reduce/pallas_call | solution.py:437
  417.6 3.1 add_convert_fusion.1.homed_ref
  421.9 2.9 convert_reduce_fusion.2
  424.9 68.9 %attend_back.1 = (bf16[256,2048]{1,0:T(8,128)(2,1)}, bf16[2048,768]{1,0:T(8,128)(2,1)}, bf16[256,2048]{1,0:T(8,128)(2,1)}, f32[1,768]{1,0:T(1,128)}) custom-call(bf16[256,2048]{1,0:T(8,128)(2,1)} %get-tuple-element.116.branch_ref, bf16[256,2048]{1,0:T(8,128)(2,1)} %add_convert_fusion.1.homed_ref, bf16[2048,768]{1,0:T(8,128)(2,1)} %add_convert_fusion.head_ref, ...), custom_call_target="tpu_custom_call" | custom-call | tf_op jit(solution)/shard_map/attend_back/pallas_call | solution.py:781
  493.8 10.4 %convolution_convert_fusion = bf16[2048,768]{1,0:T(8,128)(2,1)S(1)} fusion(bf16[2048,2048]{1,0:T(8,128)(2,1)} %bitcast.72, bf16[2048,768]{1,0:T(8,128)(2,1)} %get-tuple-element.92), kind=kOutput, calls=%fused_computation.1 | convolution fusion | flops 6444023808 | bytes 14680064 | tf_op jit(solution)/shard_map/dot_general | solution.py:50
  504.3 1.9 copy.68
  508.3 58.7 %product_reduce.3 = (f32[256,2048]{1,0:T(8,128)}, bf16[64,8192]{1,0:T(8,128)(2,1)}) custom-call(bf16[8,256,768]{2,1,0:T(8,128)(2,1)} %bitcast.80, bf16[2048,768]{1,0:T(8,128)(2,1)} %all-gather.7.cloned.1.call-done.weight_ref, bf16[512,1024]{1,0:T(8,128)(2,1)} %reduce-scatter.7.cloned.1.call-done.refs_0_), custom_call_target="tpu_custom_call" | custom-call | tf_op jit(solution)/shard_map/product_reduce/pallas_call | solution.py:437
  567.0 2.6 fusion.9
  570.8 2.8 convert_element_type.54
  573.7 1.8 fusion.13.homed_ref
  575.5 55.2 %closing.1 = (f32[192,128]{1,0:T(8,128)}, bf16[256,2048]{1,0:T(8,128)(2,1)}, bf16[64,6144]{1,0:T(8,128)(2,1)}, bf16[64,8192]{1,0:T(8,128)(2,1)}) custom-call(f32[192,128]{1,0:T(8,128)} %bitcast.86, bf16[256,2048]{1,0:T(8,128)(2,1)} %fusion.13.homed_ref, bf16[512,768]{1,0:T(8,128)(2,1)} %reduce-scatter.9.cloned.1.call-done.refs_0_, ...), custom_call_target="tpu_custom_call" | custom-call | tf_op jit(solution)/shard_map/closing/pallas_call | solution.py:485
  630.8 2.8 convert_element_type.55
  636.1 1.8 convert_element_type.53
  (156 shorter events, 19.2 us)
Async XLA Ops:
  7.2 51.4 %all-gather.5.cloned.1.call-start = ((), (), s32[]{:S(2)}) async-start(), calls=%async_computation.4 | async-start | bytes 1310720 | tf_op jit(solution)/shard_map/all_gather | solution.py:975
  7.9 51.5 %copy-start.29 = (s32[1,2048]{1,0:T(1,128)S(1)}, s32[1,2048]{1,0:T(1,128)}, u32[]{:S(2)}) copy-start(s32[1,2048]{1,0:T(1,128)} %param.31) | copy-start | bytes 24580
  7.9 51.5 %copy-start.32 = (s32[1,4]{1,0:T(1,128)S(1)}, s32[1,4]{1,0:T(1,128)}, u32[]{:S(2)}) copy-start(s32[1,4]{1,0:T(1,128)} %param.32) | copy-start | bytes 52
  7.9 138.8 %all-gather.7.cloned.1.call-start = ((), (), s32[]{:S(2)}) async-start(), calls=%async_computation.5 | async-start | bytes 3932160 | tf_op jit(solution)/shard_map/all_gather | solution.py:975
  58.5 12.2 %copy-start.7 = (bf16[256,2048]{1,0:T(8,128)(2,1)S(1)}, bf16[256,2048]{1,0:T(8,128)(2,1)}, u32[]{:S(2)}) copy-start(bf16[256,2048]{1,0:T(8,128)(2,1)} %get-tuple-element.61) | copy-start | bytes 3145732
  58.5 12.8 %copy-start.22 = (f32[2048]{0:T(1024)S(1)}, f32[2048]{0:T(1024)}, u32[]{:S(2)}) copy-start(f32[2048]{0:T(1024)} %param.18) | copy-start | bytes 24580
  58.6 12.8 %copy-start.23 = (f32[2048]{0:T(1024)S(1)}, f32[2048]{0:T(1024)}, u32[]{:S(2)}) copy-start(f32[2048]{0:T(1024)} %param.19) | copy-start | bytes 24580
  58.6 205.0 %all-gather.9.cloned.1.call-start = ((), (), s32[]{:S(2)}) async-start(), calls=%async_computation.6 | async-start | bytes 5242880 | tf_op jit(solution)/shard_map/all_gather | solution.py:975
  59.4 254.2 %all-gather.11.cloned.1.call-start = ((), (), s32[]{:S(2)}) async-start(), calls=%async_computation.7 | async-start | bytes 5242880 | tf_op jit(solution)/shard_map/all_gather | solution.py:975
  59.4 66.7 %collective-permute-start = (s32[1,2052]{1,0:T(1,128)S(1)}, s32[1,2052]{1,0:T(1,128)S(1)}, u32[]{:S(2)}, u32[]{:S(2)}) collective-permute-start(s32[1,2052]{1,0:T(1,128)S(1)} %pad_add_fusion), channel_id=1, source_target_pairs={{0,0},{1,1},{2,16},{3,17},{4,8},{5,9},{6,24},{7,25},{8,18},{9,19},... | collective-permute-start | bytes 24632 | tf_op jit(solution)/shard_map/ppermute | solution.py:964
  71.9 52.7 %copy-start.27 = (f32[2048]{0:T(1024)S(1)}, f32[2048]{0:T(1024)}, u32[]{:S(2)}) copy-start(f32[2048]{0:T(1024)} %param.22) | copy-start | bytes 24580
  71.9 52.7 %copy-start.28 = (f32[2048]{0:T(1024)S(1)}, f32[2048]{0:T(1024)}, u32[]{:S(2)}) copy-start(f32[2048]{0:T(1024)} %param.21) | copy-start | bytes 24580
  71.9 58.2 %copy-start.13 = (bf16[256,2048]{1,0:T(8,128)(2,1)S(1)}, bf16[256,2048]{1,0:T(8,128)(2,1)}, u32[]{:S(2)}) copy-start(bf16[256,2048]{1,0:T(8,128)(2,1)} %all-gather.5.cloned.1.call-done) | copy-start | bytes 3145732
  121.3 3.2 copy-start.4
  124.5 369.3 %reduce-scatter.5.cloned.1.call-start = ((), (), s32[]{:S(2)}) async-start(), calls=%async_computation.8 | async-start | bytes 5242880 | tf_op jit(solution)/shard_map/reduce_scatter | solution.py:990
  126.3 19.4 %copy-start.18 = (s32[1,2048]{1,0:T(1,128)}, s32[1,2048]{1,0:T(1,128)S(1)}, u32[]{:S(2)}) copy-start(s32[1,2048]{1,0:T(1,128)S(1)} %broadcast_in_dim_reshape.9.first_ref.place_ref) | copy-start | bytes 24580
  128.2 14.0 %collective-permute-start.1 = (bf16[256,2048]{1,0:T(8,128)(2,1)}, bf16[256,2048]{1,0:T(8,128)(2,1)}, u32[]{:S(2)}, u32[]{:S(2)}) collective-permute-start(bf16[256,2048]{1,0:T(8,128)(2,1)} %param.33), channel_id=1, source_target_pairs={{0,0},{1,1},{2,18},{3,19},{4,12},{5,13},{6,30},{7,31},{8,16},{9,17... | collective-permute-start | bytes 3145736 | tf_op jit(solution)/shard_map/ppermute | solution.py:958
  130.2 15.3 %collective-permute-start.3 = (bf16[2,64,2048]{2,1,0:T(8,128)(2,1)S(1)}, bf16[2,64,2048]{2,1,0:T(8,128)(2,1)S(1)}, u32[]{:S(2)}, u32[]{:S(2)}) collective-permute-start(bf16[2,64,2048]{2,1,0:T(8,128)(2,1)S(1)} %bitcast.85), channel_id=1, source_target_pairs={{0,1},{1,0},{2,3},{3,2},{4,5},{5,4},{6,7},{7,6},{8,9},{9,8},{10,11... | collective-permute-start | bytes 1572872 | tf_op jit(solution)/shard_map/ppermute | solution.py:1007
  142.2 80.0 %collective-permute-start.2 = (bf16[256,2048]{1,0:T(8,128)(2,1)}, bf16[256,2048]{1,0:T(8,128)(2,1)S(1)}, u32[]{:S(2)}, u32[]{:S(2)}) collective-permute-start(bf16[256,2048]{1,0:T(8,128)(2,1)} %collective-permute-done.1), channel_id=1, source_target_pairs={{0,0},{1,1},{18,16},{19,17},{12,8},{13,9},{30,24},{31,25},{16,18},... | collective-permute-start | bytes 3145736 | tf_op jit(solution)/shard_map/ppermute | solution.py:961
  159.4 48.6 %copy-start.24 = (f32[2048]{0:T(1024)S(1)}, f32[2048]{0:T(1024)}, u32[]{:S(2)}) copy-start(f32[2048]{0:T(1024)} %param.24) | copy-start | bytes 24580
  222.2 38.2 %copy-start.1 = (bf16[256,2048]{1,0:T(8,128)(2,1)}, bf16[256,2048]{1,0:T(8,128)(2,1)S(1)}, u32[]{:S(2)}) copy-start(bf16[256,2048]{1,0:T(8,128)(2,1)S(1)} %collective-permute-done.2.x_ref) | copy-start | bytes 3145732
  260.4 3.2 copy-start
  312.4 193.8 %reduce-scatter.7.cloned.1.call-start = ((), (), s32[]{:S(2)}) async-start(), calls=%async_computation.9 | async-start | bytes 5242880 | tf_op jit(solution)/shard_map/reduce_scatter | solution.py:990
  369.0 201.8 %reduce-scatter.9.cloned.1.call-start = ((), (), s32[]{:S(2)}) async-start(), calls=%async_computation.10 | async-start | bytes 3932160 | tf_op jit(solution)/shard_map/reduce_scatter | solution.py:990
  372.1 45.5 %copy-start.6 = (f32[256,2048]{1,0:T(8,128)S(1)}, f32[256,2048]{1,0:T(8,128)}, u32[]{:S(2)}) copy-start(f32[256,2048]{1,0:T(8,128)} %copy-done.5) | copy-start | bytes 6291460
  372.1 45.5 %copy-start.26 = (f32[2048]{0:T(1024)S(1)}, f32[2048]{0:T(1024)}, u32[]{:S(2)}) copy-start(f32[2048]{0:T(1024)} %param.30) | copy-start | bytes 24580
  506.2 129.8 %reduce-scatter.11.cloned.1.call-start = ((), (), s32[]{:S(2)}) async-start(), calls=%async_computation.11 | async-start | bytes 1310720 | tf_op jit(solution)/shard_map/reduce_scatter | solution.py:990
  508.0 61.6 %collective-permute-start.4 = (bf16[2,64,2048]{2,1,0:T(8,128)(2,1)S(1)}, bf16[2,64,2048]{2,1,0:T(8,128)(2,1)S(1)}, u32[]{:S(2)}, u32[]{:S(2)}) collective-permute-start(bf16[2,64,2048]{2,1,0:T(8,128)(2,1)S(1)} %select_bitcast_fusion), channel_id=1, source_target_pairs={{0,1},{1,0},{2,3},{3,2},{4,5},{5,4},{6,7},{7,6},{8,9},{9,8},{10,11... | collective-permute-start | bytes 1572872 | tf_op jit(solution)/shard_map/ppermute | solution.py:1026
  508.3 58.7 %copy-start.8 = (bf16[256,2048]{1,0:T(8,128)(2,1)S(1)}, bf16[256,2048]{1,0:T(8,128)(2,1)}, u32[]{:S(2)}) copy-start(bf16[256,2048]{1,0:T(8,128)(2,1)} %get-tuple-element.61) | copy-start | bytes 3145732
  630.8 4.0 copy-start.20
  633.6 4.3 copy-start.14
  634.8 4.0 copy-start.16
  (14 other events, 24.5 us)
Sparse Core Ops, SparseCore 0:
  9.6 39.9 all-gather.4
  58.7 70.8 all-gather.6
  131.2 99.7 all-gather.8
  232.4 81.0 all-gather.10
  315.7 77.3 reduce-scatter.4
  395.3 95.1 reduce-scatter.6
  506.4 62.8 reduce-scatter.8
  572.1 47.1 reduce-scatter.10
